TPU v7x, 256 devices: a 8x8x2 block of a 8x8x16 slice. The times are simulated.
256 devices in a mesh: groups: 2 (over z), seq: 128 (over y, x, core).
Axes of the slice: x: 8, y: 8, z: 2, core: 2. Of those that a mesh axis runs over, the one named last changes fastest.
The devices are a block of a 8x8x16 slice.
Arguments:
- queries: bfloat16 [256, 8192], P(('groups', 'seq')), parts along dimension 0, may hold values from -320 to 320, as said below
- span_keys: bfloat16 [256, 1024], P(('groups', 'seq')), parts along dimension 0, may hold values from -6 to 6
- span_values: bfloat16 [256, 1024], P(('groups', 'seq')), parts along dimension 0, may hold values from -6 to 6
- cache_keys: bfloat16 [65536, 1024], P(('groups', 'seq')), parts along dimension 0, may hold values from -6 to 6
- cache_values: bfloat16 [65536, 1024], P(('groups', 'seq')), parts along dimension 0, may hold values from -6 to 6
- page_table: int32 [4096], P(('groups', 'seq')), parts along dimension 0, may hold values from 0 to 2047, each once
- page_counts: int32 [256], P(('groups', 'seq')), parts along dimension 0, may hold values from 1 to 16, 1024 in all
- span_start: int32 [2], P('groups'), parts along dimension 0, may hold values from 16384 to 32767
Outputs:
- attended: bfloat16 [256, 8192], P(('groups', 'seq')), parts along dimension 0
There are 2 independent parts, one for each index of `groups`. A program takes and returns all parts, laid end to end along the dimension named above; each array names one. Nothing has to cross between parts.
Inputs may be any that keep to these rules, and one draw needn't show every extreme that they name: `queries`: queries of every row; in some draws rows differ in scale by a large factor. `page_table`: A permutation of the 2048 logical pages. `page_counts`: counts of the shards sum to 1024; slots at or beyond a shard's count hold no page; some shard holds 16.
All inputs are finite; a program needn't handle non-finite values.
Results may differ from a plain program's by a relative error of at most 0.02.
The roundings to bfloat16 on the way count: a program that leaves them out, or rounds other values in their place, can miss the bound.
Values may be sent and summed in bfloat16 or wider, within the bound.
A program may use at most 64 MiB of HBM per device.

v0:
```python
import jax
import jax.numpy as jnp
from jax import lax
from jax.sharding import PartitionSpec as P

H = 64
KVH = 8
PAGE = 16


rope_base = 1000000.0
masked_low = -1e30


def side_by_side(arrays, axis, dim, along):
    widths = [a.shape[along] for a in arrays]
    both = jnp.concatenate(arrays, axis=along)
    filled = lax.all_gather(both, axis, axis=dim, tiled=True)
    return tuple(jnp.split(filled, [sum(widths[:k]) for k in range(1, len(widths))], axis=along))


def sent_together(arrays, axis, split_dim, concat_dim, along):
    both = jnp.concatenate(arrays, axis=along)
    filled, at, done = (
        lax.all_to_all(both, axis, split_axis=split_dim, concat_axis=concat_dim, tiled=True),
        0,
        [],
    )
    for a in arrays:
        done.append(lax.slice_in_dim(filled, at, at + a.shape[along], axis=along))
        at += a.shape[along]
    return tuple(done)


def rotate(values, positions, heads):
    count_rows = values.shape[0]
    width = values.shape[1] // heads
    half_width = width // 2
    frequency = rope_base ** (-(jnp.arange(half_width, dtype=jnp.float32) * 2.0 / width))
    angles = positions.astype(jnp.float32)[:, None] * frequency[None, :]
    cosine = jnp.cos(angles)[:, None, :]
    sine_part = jnp.sin(angles)[:, None, :]
    headed = values.astype(jnp.float32).reshape(count_rows, heads, width)
    first_half = headed[..., :half_width]
    second_half = headed[..., half_width:]
    turned = jnp.concatenate(
        [
            first_half * cosine - second_half * sine_part,
            second_half * cosine + first_half * sine_part,
        ],
        axis=-1,
    )
    return turned.reshape(count_rows, heads * width)


def merge_states(states):
    shard_max, numer, denom = states
    newest = jnp.max(shard_max, axis=0)
    weights = jnp.exp(shard_max - newest[None])
    return (newest, jnp.sum(numer * weights[..., None], axis=0), jnp.sum(denom * weights, axis=0))


def body(
    queries, span_keys, span_values, cache_keys, cache_values, page_table, page_counts, span_start
):
    own_rows = queries.shape[0]
    shard_id = lax.axis_index("seq")
    start = span_start[0]
    group = H // KVH
    width = queries.shape[1] // H
    factor = width ** (-0.5)
    own_positions = start + shard_id * own_rows + jnp.arange(own_rows, dtype=jnp.int32)
    query_rot = rotate(queries, own_positions, H).astype(jnp.bfloat16)
    span_rot = rotate(span_keys, own_positions, KVH).astype(jnp.bfloat16)
    all_queries = lax.all_gather(query_rot, "seq", axis=0, tiled=True)
    block_keys, block_values = side_by_side((span_rot, span_values), "seq", 0, 1)
    total_rows = all_queries.shape[0]
    key_count = cache_keys.shape[0]
    row_ids = jnp.arange(key_count, dtype=jnp.int32)
    slot_ids = row_ids // PAGE
    positions = jnp.repeat(page_table, PAGE) * PAGE + row_ids % PAGE
    usable = (slot_ids < page_counts[0]) & (positions < start)
    keys_rot = rotate(cache_keys, positions, KVH).astype(jnp.bfloat16)
    query_heads = all_queries.reshape(total_rows, KVH, group, width)
    key_heads = keys_rot.reshape(key_count, KVH, width)
    value_heads = cache_values.reshape(key_count, KVH, width)
    row_blocks = lax.axis_size("seq") // KVH
    piece = key_count // row_blocks
    key_parts = (
        key_heads.reshape(row_blocks, piece, KVH, width)
        .transpose(0, 2, 1, 3)
        .reshape(row_blocks * KVH, piece, width)
    )
    value_parts = (
        value_heads.reshape(row_blocks, piece, KVH, width)
        .transpose(0, 2, 1, 3)
        .reshape(row_blocks * KVH, piece, width)
    )
    flag_parts = jnp.broadcast_to(
        usable.astype(jnp.int32).reshape(row_blocks, 1, piece), (row_blocks, KVH, piece)
    ).reshape(row_blocks * KVH, piece)
    got_keys, got_values, got_flags = (
        *sent_together((key_parts, value_parts), "seq", 0, 1, 2),
        lax.all_to_all(flag_parts, "seq", split_axis=0, concat_axis=1, tiled=True),
    )
    head_id = shard_id % KVH
    query_one = lax.dynamic_index_in_dim(query_heads, head_id, 1, keepdims=False)
    steps_count = got_keys.shape[1] // key_count

    def one_block(block_id):
        offset = block_id * key_count
        key_one = lax.dynamic_slice_in_dim(got_keys[0], offset, key_count, 0)
        value_one = lax.dynamic_slice_in_dim(got_values[0], offset, key_count, 0)
        live = (lax.dynamic_slice_in_dim(got_flags[0], offset, key_count, 0) > 0)[None, None, :]
        scores = (
            jnp.einsum("tgd,sd->tgs", query_one, key_one, preferred_element_type=jnp.float32)
            * factor
        )
        best = jnp.max(jnp.where(live, scores, masked_low), axis=-1)
        weights = jnp.where(live, jnp.exp(scores - best[..., None]), 0.0)
        denom = jnp.sum(weights, axis=-1)
        numer = jnp.einsum(
            "tgs,sd->tgd",
            weights.astype(jnp.bfloat16),
            value_one,
            preferred_element_type=jnp.float32,
        )
        return (best, numer, denom)

    head_max, head_num, head_den = merge_states(
        lax.map(one_block, jnp.arange(steps_count, dtype=jnp.int32))
    )
    received = (
        lax.all_to_all(head_max[None], "seq", split_axis=1, concat_axis=0, tiled=True),
        lax.all_to_all(head_num[None], "seq", split_axis=1, concat_axis=0, tiled=True),
        lax.all_to_all(head_den[None], "seq", split_axis=1, concat_axis=0, tiled=True),
    )
    sources = received[0].shape[0] // KVH
    shaped = tuple((item.reshape((sources, KVH) + item.shape[1:]) for item in received))
    own_max, own_num, own_den = merge_states(shaped)
    own_queries = query_rot.reshape(own_rows, KVH, group, width)
    block_heads = block_keys.reshape(total_rows, KVH, width)
    block_vals = block_values.reshape(total_rows, KVH, width)
    self_scores = (
        jnp.einsum("tkgd,skd->ktgs", own_queries, block_heads, preferred_element_type=jnp.float32)
        * factor
    )
    causal = (jnp.arange(total_rows, dtype=jnp.int32)[None, :] <= own_positions[:, None] - start)[
        None, :, None, :
    ]
    self_max = jnp.max(jnp.where(causal, self_scores, masked_low), axis=-1)
    self_weights = jnp.where(causal, jnp.exp(self_scores - self_max[..., None]), 0.0)
    self_den = jnp.sum(self_weights, axis=-1)
    self_num = jnp.einsum(
        "ktgs,skd->ktgd",
        self_weights.astype(jnp.bfloat16),
        block_vals,
        preferred_element_type=jnp.float32,
    )
    both = jnp.maximum(own_max, self_max)
    first_weight = jnp.exp(own_max - both)
    second_weight = jnp.exp(self_max - both)
    total_num = own_num * first_weight[..., None] + self_num * second_weight[..., None]
    total_den = own_den * first_weight + self_den * second_weight
    result = total_num / total_den[..., None]
    return result.transpose(1, 0, 2, 3).reshape(own_rows, H * width).astype(jnp.bfloat16)


def solution(mesh):
    in_specs = (
        P(("groups", "seq"), None),
        P(("groups", "seq"), None),
        P(("groups", "seq"), None),
        P(("groups", "seq"), None),
        P(("groups", "seq"), None),
        P(("groups", "seq")),
        P(("groups", "seq")),
        P("groups"),
    )
    out_specs = P(("groups", "seq"), None)
    return jax.shard_map(body, mesh=mesh, in_specs=in_specs, out_specs=out_specs, check_vma=False)
```

profile of v0, /device:TPU:513, one launch (start us, length us, event | category | flops | bytes accessed | tf_op | source)
XLA Modules:
  0.0 285.1 jit_solution(14791817281463338072)
XLA Ops:
  11.0 27.4 %all-to-all-start = ((s32[128,1,16]{2,1,0:T(1,128)}), s32[128,1,16]{2,1,0:T(1,128)S(1)}, u32[]{:S(2)}, u32[]{:S(2)}) async-start(s32[128,1,16]{2,1,0:T(1,128)} %bitcast.11), calls=%async_computation | async-start | bytes 131072 | tf_op jit(solution)/shard_map/all_to_all | solution.py:104
  38.5 1.1 convert_bitcast_fusion
  41.6 1.2 pad_maximum_fusion
  42.8 7.7 %all-to-all-done = s32[128,1,16]{2,1,0:T(1,128)S(1)} async-done(((s32[128,1,16]{2,1,0:T(1,128)}), s32[128,1,16]{2,1,0:T(1,128)S(1)}, u32[]{:S(2)}, u32[]{:S(2)}) %all-to-all-start) | async-done | bytes 8224 | tf_op jit(solution)/shard_map/all_to_all | solution.py:104
  50.5 8.9 %all-to-all-start.1 = ((bf16[128,16,256]{2,1,0:T(8,128)(2,1)}), bf16[128,16,256]{2,1,0:T(8,128)(2,1)S(1)}, u32[]{:S(2)}, u32[]{:S(2)}) async-start(bf16[128,16,256]{2,1,0:T(8,128)(2,1)} %pad_maximum_fusion), calls=%async_computation.1 | async-start | bytes 2097152 | tf_op jit(solution)/shard_map/all_to_all | solution.py:25
  61.2 28.4 %all-to-all-done.1 = bf16[128,16,256]{2,1,0:T(8,128)(2,1)S(1)} async-done(((bf16[128,16,256]{2,1,0:T(8,128)(2,1)}), bf16[128,16,256]{2,1,0:T(8,128)(2,1)S(1)}, u32[]{:S(2)}, u32[]{:S(2)}) %all-to-all-start.1) | async-done | bytes 1048608 | tf_op jit(solution)/shard_map/all_to_all | solution.py:25
  89.6 35.2 %all-gather.4.cloned.1.call-done = bf16[128,1,8192]{2,1,0:T(2,128)(2,1)} async-done(((bf16[1,1,8192]{2,1,0:T(2,128)(2,1)}), bf16[128,1,8192]{2,1,0:T(2,128)(2,1)}) %all-gather.4.cloned.1.call-update) | async-done | bytes 2097168 | tf_op jit(solution)/shard_map/all_gather | solution.py:75
  124.8 8.8 %copy.61 = bf16[128,1,8192]{0,2,1:T(8,128)(2,1)S(1)} copy(bf16[128,1,8192]{2,1,0:T(2,128)(2,1)} %all-gather.4.cloned.1.call-done) | data formatting | bytes 4194304 | tf_op jit(solution)/shard_map/all_gather | solution.py:75
  133.8 24.7 %while.14 = (s32[]{:T(128)}, f32[8,128,8]{1,2,0:T(8,128)S(1)}, f32[8,128,8,128]{3,1,2,0:T(8,128)}, f32[8,128,8]{1,2,0:T(8,128)S(1)}, s32[8]{0:T(128)S(1)}, /*ind...) while((s32[]{:T(128)}, f32[8,128,8]{1,2,0:T(8,128)S(1)}, ...), condition=%wide.region_3.4_spmd, body=%wide.region_0.3_spmd.sunk | while | flops 136575232 | bytes 4099271 | solution.py:131
  135.4 1.2 fusion.46
  138.5 1.3 fusion.46
  141.6 1.3 fusion.46
  144.7 1.3 fusion.46
  147.8 1.3 fusion.46
  150.9 1.3 fusion.46
  154.0 1.2 fusion.46
  157.1 1.3 fusion.46
  159.3 11.8 %all-to-all-start.4 = ((f32[1,128,8]{2,0,1:T(1,128)}), f32[1,128,8]{2,0,1:T(1,128)S(1)}, u32[]{:S(2)}, u32[]{:S(2)}) async-start(f32[1,128,8]{2,0,1:T(1,128)} %copy.76), calls=%async_computation.4 | async-start | bytes 131072 | tf_op jit(solution)/shard_map/all_to_all | solution.py:136
  171.2 54.0 %all-gather.1 = bf16[128,1,2048]{2,1,0:T(2,128)(2,1)S(1)} all-gather(bf16[1,1,2048]{2,1,0:T(2,128)(2,1)S(1)} %maximum_bitcast_fusion), channel_id=1, replica_groups=mesh['groups'=2,'seq'=128] {'seq'}, dimensions={0}, use_global_device_ids=true | all-gather | bytes 528384 | tf_op jit(solution)/shard_map/all_gather | solution.py:18
  226.2 11.1 %all-to-all-start.3 = ((f32[1,128,8]{2,0,1:T(1,128)}), f32[1,128,8]{2,0,1:T(1,128)S(1)}, u32[]{:S(2)}, u32[]{:S(2)}) async-start(f32[1,128,8]{2,0,1:T(1,128)} %copy.65), calls=%async_computation.3 | async-start | bytes 131072 | tf_op jit(solution)/shard_map/all_to_all | solution.py:134
  237.3 2.9 %multiply_reduce_fusion = f32[128,8,128]{2,0,1:T(8,128)S(1)} fusion(f32[8,128,8,128]{3,1,2,0:T(8,128)} %get-tuple-element.54, f32[8,128,8]{1,2,0:T(8,128)S(1)} %get-tuple-element.106), kind=kLoop, calls=%fused_computation.21 | loop fusion | flops 1966080 | bytes 4751360 | tf_op jit(solution)/shard_map/reduce_sum | solution.py:60
  241.3 8.0 %all-to-all-done.3 = f32[1,128,8]{2,0,1:T(1,128)S(1)} async-done(((f32[1,128,8]{2,0,1:T(1,128)}), f32[1,128,8]{2,0,1:T(1,128)S(1)}, u32[]{:S(2)}, u32[]{:S(2)}) %all-to-all-start.3) | async-done | bytes 4128 | tf_op jit(solution)/shard_map/all_to_all | solution.py:134
  249.3 8.3 %all-to-all-start.2 = ((f32[1,128,8,128]{3,2,0,1:T(8,128)}), f32[1,128,8,128]{3,2,0,1:T(8,128)S(1)}, u32[]{:S(2)}, u32[]{:S(2)}) async-start(f32[1,128,8,128]{3,2,0,1:T(8,128)} %copy.64), calls=%async_computation.2 | async-start | bytes 1048576 | tf_op jit(solution)/shard_map/all_to_all | solution.py:135
  259.3 17.8 %all-to-all-done.2 = f32[1,128,8,128]{3,2,0,1:T(8,128)S(1)} async-done(((f32[1,128,8,128]{3,2,0,1:T(8,128)}), f32[1,128,8,128]{3,2,0,1:T(8,128)S(1)}, u32[]{:S(2)}, u32[]{:S(2)}) %all-to-all-start.2) | async-done | bytes 524320 | tf_op jit(solution)/shard_map/all_to_all | solution.py:135
  (113 shorter events, 21.9 us)
Async XLA Ops:
  6.5 118.3 %all-gather.4.cloned.1.call-start = ((), (), s32[]{:S(2)}) async-start(), calls=%async_computation.5 | async-start | bytes 4227072 | tf_op jit(solution)/shard_map/all_gather | solution.py:75
  11.0 39.5 %all-to-all-start = ((s32[128,1,16]{2,1,0:T(1,128)}), s32[128,1,16]{2,1,0:T(1,128)S(1)}, u32[]{:S(2)}, u32[]{:S(2)}) async-start(s32[128,1,16]{2,1,0:T(1,128)} %bitcast.11), calls=%async_computation | async-start | bytes 131072 | tf_op jit(solution)/shard_map/all_to_all | solution.py:104
  39.6 1.7 copy-start
  41.2 18.3 %copy-start.1 = (bf16[1,1024]{1,0:T(2,128)(2,1)S(1)}, bf16[1,1024]{1,0:T(2,128)(2,1)}, u32[]{:S(2)}) copy-start(bf16[1,1024]{1,0:T(2,128)(2,1)} %param.11) | copy-start | bytes 6148
  41.2 18.4 %copy-start.2 = (bf16[1,1024]{1,0:T(2,128)(2,1)S(1)}, bf16[1,1024]{1,0:T(2,128)(2,1)}, u32[]{:S(2)}) copy-start(bf16[1,1024]{1,0:T(2,128)(2,1)} %param.12) | copy-start | bytes 6148
  50.5 39.1 %all-to-all-start.1 = ((bf16[128,16,256]{2,1,0:T(8,128)(2,1)}), bf16[128,16,256]{2,1,0:T(8,128)(2,1)S(1)}, u32[]{:S(2)}, u32[]{:S(2)}) async-start(bf16[128,16,256]{2,1,0:T(8,128)(2,1)} %pad_maximum_fusion), calls=%async_computation.1 | async-start | bytes 2097152 | tf_op jit(solution)/shard_map/all_to_all | solution.py:25
  159.3 66.9 %all-to-all-start.4 = ((f32[1,128,8]{2,0,1:T(1,128)}), f32[1,128,8]{2,0,1:T(1,128)S(1)}, u32[]{:S(2)}, u32[]{:S(2)}) async-start(f32[1,128,8]{2,0,1:T(1,128)} %copy.76), calls=%async_computation.4 | async-start | bytes 131072 | tf_op jit(solution)/shard_map/all_to_all | solution.py:136
  226.2 23.1 %all-to-all-start.3 = ((f32[1,128,8]{2,0,1:T(1,128)}), f32[1,128,8]{2,0,1:T(1,128)S(1)}, u32[]{:S(2)}, u32[]{:S(2)}) async-start(f32[1,128,8]{2,0,1:T(1,128)} %copy.65), calls=%async_computation.3 | async-start | bytes 131072 | tf_op jit(solution)/shard_map/all_to_all | solution.py:134
  249.3 27.9 %all-to-all-start.2 = ((f32[1,128,8,128]{3,2,0,1:T(8,128)}), f32[1,128,8,128]{3,2,0,1:T(8,128)S(1)}, u32[]{:S(2)}, u32[]{:S(2)}) async-start(f32[1,128,8,128]{3,2,0,1:T(8,128)} %copy.64), calls=%async_computation.2 | async-start | bytes 1048576 | tf_op jit(solution)/shard_map/all_to_all | solution.py:135
Sparse Core Ops, SparseCore 0:
  9.9 114.8 all-gather.3
where the time goes:
time: 286 us; the launch traced here: 285 us
  waiting for transfers between devices  97.1 us (34%)
  starting transfers between devices  67.5 us (24%)
  blocking collectives  54 us (19%)
  local copies, waits for them, and re-layouts  21.1 us (7%)
  between operations  15.1 us (5%)
  matrix products  13.1 us (5%)
  other arithmetic  11.7 us (4%)
  loops' own time  5.53 us (2%)
    all_gather x1, blocking collectives, side_by_side(): filled = lax.all_gather(both, axis, axis=dim, tiled=True)  54 us
    all_gather x1, waiting for transfers between devices, body(): all_queries = lax.all_gather(query_rot, 'seq', axis=0, tiled=True)  35.2 us
    all_to_all x1, waiting for transfers between devices, sent_together(): lax.all_to_all(both, axis, split_axis=split_dim, concat_axis=concat_dim,...  28.4 us
    all_to_all x1, starting transfers between devices, body(): lax.all_to_all(flag_parts, 'seq', split_axis=0, concat_axis=1, tiled=True)  27.4 us
    all_to_all x1, waiting for transfers between devices, body(): lax.all_to_all(head_num[None], 'seq', split_axis=1, concat_axis=0, tiled=...  17.8 us
    all_to_all x1, starting transfers between devices, body(): lax.all_to_all(head_den[None], 'seq', split_axis=1, concat_axis=0, tiled=...  11.8 us
    all_to_all x1, starting transfers between devices, body(): lax.all_to_all(head_max[None], 'seq', split_axis=1, concat_axis=0, tiled=...  11.1 us
    dot_general x8, matrix products, one_block(): jnp.einsum('tgs,sd->tgd', weights.astype(jnp.bfloat16), value_one, prefer...  10 us
  transfers between devices with their start and end apart: 6, of which 5 were waited for; matrix products, arithmetic and copies ran while one was open for 5% of the time, Pallas kernels for 0%

commit v1 on v0

v1 whole, which is shorter than its diff:
```python
import functools
import math

import jax
import jax.numpy as jnp
import numpy as np
from jax import lax
from jax.experimental import pallas as pl
from jax.experimental.pallas import tpu as pltpu
from jax.sharding import PartitionSpec as P

H = 64
KVH = 8
PAGE = 16
GROUP = H // KVH
ROPE_BASE = 1000000.0
DEAD = -1e30
FLOOR = -1e29
CLASSES = 4
MESH = pl.DeviceIdType.MESH
F32 = jnp.float32
BF16 = jnp.bfloat16


def rope_table(width, rows):
    half = width // 2
    freq = ROPE_BASE ** (-(np.arange(half, dtype=np.float64) * 2.0 / width))
    turns = np.concatenate([freq, freq]) / (2.0 * np.pi)
    pieces, rest = [], turns
    for _ in range(2):
        scale = 2.0 ** (np.floor(np.log2(rest)) - 7.0)
        part = np.floor(rest / scale) * scale
        pieces.append(part)
        rest = rest - part
    pieces.append(rest)
    sign = np.concatenate([-np.ones(half), np.ones(half)])
    angle = np.arange(rows, dtype=np.float64)[:, None] * np.concatenate([freq, freq])[None, :]
    pad = np.zeros((8 - len(pieces) - 1, width))
    return np.concatenate(
        [np.stack(pieces), sign[None], pad, np.cos(angle), np.sin(angle) * sign[None]]
    ).astype(np.float32)


def cos_sin(position, table_ref):
    def part(k):
        turn = position * table_ref[k : k + 1, :]
        return turn - jnp.floor(turn)

    turn = part(0) + part(1) + part(2)
    turn = turn - jnp.floor(turn + 0.5)
    angle = turn * (2.0 * math.pi)
    return jnp.cos(angle), jnp.sin(angle) * table_ref[3:4, :]


def kernel(
    side,
    start_ref,
    count_ref,
    pages_ref,
    table_ref,
    q_hbm,
    sk_hbm,
    sv_hbm,
    k_hbm,
    v_hbm,
    out_ref,
    q_raw,
    sk_raw,
    sv_raw,
    k_raw,
    q_rows,
    cos_ref,
    sin_ref,
    kx,
    vx,
    kall,
    vall,
    kspan,
    vspan,
    span_f32,
    bias_ref,
    qsrc,
    q1,
    q2,
    scores,
    o1src,
    s1src,
    o1,
    s1,
    o2src,
    s2src,
    o2,
    s2,
    wts,
    local_sem,
    kv_send,
    kv_recv,
    q1_send,
    q1_recv,
    q2_send,
    q2_recv,
    o1_send,
    o1_recv,
    o2_send,
    o2_recv,
):
    width = out_ref.shape[1]
    rows = k_hbm.shape[0]
    half_rows = rows // 2
    units = kall.shape[0]
    row_toks = 2 * side
    piece = row_toks * GROUP
    me = lax.axis_index("seq")
    core = me % 2
    x = (me // 2) % side
    y = me // (2 * side)

    def at(px, py, pc):
        return ((py % side) * side + (px % side)) * 2 + pc

    copies = [
        pltpu.make_async_copy(q_hbm, q_raw, local_sem.at[0]),
        pltpu.make_async_copy(sk_hbm, sk_raw, local_sem.at[1]),
        pltpu.make_async_copy(sv_hbm, sv_raw, local_sem.at[2]),
        pltpu.make_async_copy(k_hbm, k_raw, local_sem.at[3]),
    ]
    v_copies = []
    for h in range(KVH):
        for hf in range(2):
            v_copies.append(
                pltpu.make_async_copy(
                    v_hbm.at[pl.ds(hf * half_rows, half_rows), pl.ds(h * width, width)],
                    vx.at[h, hf, pl.ds(0, half_rows), :],
                    local_sem.at[4 + 2 * h + hf],
                )
            )
    for copy in copies + v_copies:
        copy.start()

    barrier = pltpu.get_barrier_semaphore()

    def greet(device):
        pl.semaphore_signal(barrier, inc=1, device_id={"seq": device}, device_id_type=MESH)

    for dx in range(1, side):
        for pc in range(2):
            greet(at(x + dx, y, pc))
    greet(at(x, y, 1 - core))
    for dy in range(1, side):
        greet(at(x, y + dy, core))
    greet(at(x, y + 1, 1 - core))
    greet(at(x, y + side - 1, 1 - core))
    partners = 2 * (side - 1) + 1 + (side - 1) + 2

    start = start_ref[0]
    count = count_ref[0]

    own_pos = (start + me).astype(F32)
    own_cos, own_sin = cos_sin(jnp.full((8, width), own_pos, F32), table_ref)
    copies[0].wait()
    q_all = q_raw[...].astype(F32)
    for r in range(H):
        q_rows[r : r + 1, :] = q_all[:, r * width : (r + 1) * width]
    for e in range(2):
        for pc in range(2):
            for b in range(2):
                head = 2 * (e + 2 * b) + pc
                part = q_rows[head * GROUP : (head + 1) * GROUP, :]
                turned = part * own_cos + pltpu.roll(part, width // 2, 1) * own_sin
                qsrc[e, pc, b] = turned.astype(BF16)

    pl.semaphore_wait(barrier, partners)

    def q1_copy(px, pc):
        return pltpu.make_async_remote_copy(
            src_ref=qsrc.at[px % 2, pc],
            dst_ref=q1.at[:, 2 * x + core],
            send_sem=q1_send.at[2 * px + pc],
            recv_sem=q1_recv.at[2 * x + core],
            device_id={"seq": at(px, y, pc)},
            device_id_type=MESH,
        )

    def q1_arrival(px, pc):
        return pltpu.make_async_remote_copy(
            src_ref=qsrc.at[0, 0],
            dst_ref=q1.at[:, 2 * px + pc],
            send_sem=q1_send.at[2 * px + pc],
            recv_sem=q1_recv.at[2 * px + pc],
            device_id={"seq": at(px, y, pc)},
            device_id_type=MESH,
        )

    far_first = [side // 2]
    for step in range(side // 2 - 1, 0, -1):
        far_first += [step, side - step]
    near_first = far_first[::-1]
    row_partners = [((x + dx) % side, pc) for dx in far_first for pc in range(2)]
    row_partners.append((x, 1 - core))
    for px, pc in row_partners:
        q1_copy(px, pc).start()
    for b in range(2):
        q1[b, 2 * x + core] = qsrc[x % 2, core, b]

    f_me = (x + 2 * y) % CLASSES
    tile_row = lax.broadcasted_iota(jnp.int32, (16, width), 0)
    lane = lax.broadcasted_iota(jnp.int32, (1, width), 1)
    biases = []
    for hf in range(2):
        page = jnp.zeros((1, width), jnp.int32)
        for j in range(half_rows // PAGE):
            page = jnp.where(lane // PAGE == j, pages_ref[hf * (half_rows // PAGE) + j], page)
        slot = hf * (half_rows // PAGE) + lane // PAGE
        usable = (slot < count) & (page * PAGE + lane % PAGE < start)
        biases.append(jnp.where(usable, 0.0, DEAD).astype(F32))

    copies[2].wait()
    sv_all = sv_raw[...].astype(F32)
    for h in range(KVH):
        own_v = jnp.broadcast_to(sv_all[:, h * width : (h + 1) * width], (16, width))
        vx[h, 0, half_rows : half_rows + 16, :] = jnp.where(tile_row == 0, own_v, 0.0).astype(BF16)
        vx[h, 1, half_rows : half_rows + 16, :] = jnp.zeros((16, width), BF16)

    def kv_copies(which, buf, landing):
        out = []

        def add(index, head, halves, slot, device):
            src = buf.at[head] if halves is None else buf.at[head, halves]
            dst = landing.at[pl.ds(slot, 2)] if halves is None else landing.at[slot]
            out.append(
                pltpu.make_async_remote_copy(
                    src_ref=src,
                    dst_ref=dst,
                    send_sem=kv_send.at[which, index[0]],
                    recv_sem=kv_recv.at[which, index[1]],
                    device_id={"seq": device},
                    device_id_type=MESH,
                )
            )

        for pc in range(2):
            head = 2 * ((f_me + 1) % CLASSES) + pc
            add((1 + pc, 1 + core), head, None, 4 + 2 * core, at(x + 1, y, pc))
            head = 2 * ((f_me + 3) % CLASSES) + pc
            add((3 + pc, 3 + core), head, None, 8 + 2 * core, at(x + side - 1, y, pc))
            head = 2 * ((f_me + 2) % CLASSES) + pc
            add((5 + pc, 5 + core), head, 0, 12 + core, at(x, y + 1, pc))
            add((7 + pc, 7 + core), head, 1, 14 + core, at(x, y + side - 1, pc))
        head = 2 * f_me + (1 - core)
        add((0, 0), head, None, 2 * core, at(x, y, 1 - core))
        return out

    def kv_arrivals(which, buf, landing):
        out = []

        def add(index, double, slot, device):
            out.append(
                pltpu.make_async_remote_copy(
                    src_ref=buf.at[0] if double else buf.at[0, 0],
                    dst_ref=landing.at[pl.ds(slot, 2)] if double else landing.at[slot],
                    send_sem=kv_send.at[which, index],
                    recv_sem=kv_recv.at[which, index],
                    device_id={"seq": device},
                    device_id_type=MESH,
                )
            )

        add(0, True, 2 * (1 - core), at(x, y, 1 - core))
        for pc in range(2):
            add(1 + pc, True, 4 + 2 * pc, at(x + side - 1, y, pc))
            add(3 + pc, True, 8 + 2 * pc, at(x + 1, y, pc))
            add(5 + pc, False, 12 + pc, at(x, y + side - 1, pc))
            add(7 + pc, False, 14 + pc, at(x, y + 1, pc))
        return out

    for copy in v_copies:
        copy.wait()
    v_sends = kv_copies(1, vx, vall)
    for copy in v_sends:
        copy.start()
    my_head = 2 * f_me + core
    for hf in range(2):
        vall[2 * core + hf] = vx[my_head, hf]

    page_row = lax.broadcasted_iota(jnp.int32, (16, width), 0)
    page_pos = jnp.zeros((16, width), jnp.int32)
    for j in range(rows // PAGE):
        page_pos = jnp.where(page_row == j, pages_ref[j] * PAGE, page_pos)
    page_cos, page_sin = cos_sin(page_pos.astype(F32), table_ref)
    row_cos = table_ref[8 : 8 + PAGE, :]
    row_sin = table_ref[8 + PAGE : 8 + 2 * PAGE, :]
    for j in range(rows // PAGE):
        pc_, ps_ = page_cos[j : j + 1, :], page_sin[j : j + 1, :]
        cos_ref[j * PAGE : (j + 1) * PAGE, :] = pc_ * row_cos - ps_ * row_sin
        sin_ref[j * PAGE : (j + 1) * PAGE, :] = ps_ * row_cos + pc_ * row_sin
    copies[1].wait()
    sk_all = sk_raw[...].astype(F32)
    copies[3].wait()
    for h in range(KVH):
        span = jnp.broadcast_to(sk_all[:, h * width : (h + 1) * width], (8, width))
        span = span * own_cos + pltpu.roll(span, width // 2, 1) * own_sin
        span = jnp.broadcast_to(span[0:1, :], (16, width))
        for hf in range(2):
            first = span if hf == 0 else jnp.zeros((16, width), F32)
            tile = jnp.where(tile_row == 0, first, jnp.where(tile_row == 1, biases[hf], 0.0))
            kx[h, hf, half_rows : half_rows + 16, :] = tile.astype(BF16)

    @pl.loop(0, KVH)
    def _(h):
        cols = pl.ds(pl.multiple_of(h * width, width), width)
        for hf in range(2):
            span_rows = slice(hf * half_rows, (hf + 1) * half_rows)
            part = k_raw[span_rows, cols].astype(F32)
            turned = part * cos_ref[span_rows, :]
            turned = turned + pltpu.roll(part, width // 2, 1) * sin_ref[span_rows, :]
            kx[h, hf, 0:half_rows, :] = turned.astype(BF16)

    k_sends = kv_copies(0, kx, kall)
    for copy in k_sends:
        copy.start()
    for hf in range(2):
        kall[2 * core + hf] = kx[my_head, hf]

    for px, pc in row_partners:
        q1_arrival(px, pc).wait_recv()

    def bit(py):
        return (x // 2 + py) % 2

    def q2_copy(py):
        return pltpu.make_async_remote_copy(
            src_ref=q1.at[bit(py)],
            dst_ref=q2.at[y],
            send_sem=q2_send.at[py],
            recv_sem=q2_recv.at[y],
            device_id={"seq": at(x, py, core)},
            device_id_type=MESH,
        )

    def q2_arrival(py):
        return pltpu.make_async_remote_copy(
            src_ref=q1.at[0],
            dst_ref=q2.at[py],
            send_sem=q2_send.at[py],
            recv_sem=q2_recv.at[py],
            device_id={"seq": at(x, py, core)},
            device_id_type=MESH,
        )

    for dy in far_first:
        q2_copy((y + dy) % side).start()
    q2[y] = q1[bit(y)]

    for arrival in kv_arrivals(1, vx, vall) + kv_arrivals(0, kx, kall):
        arrival.wait_recv()
    span_units = [0, 2, 4, 6, 8, 10, 12, 13]
    span_toks = [
        at(x, y, 0),
        at(x, y, 1),
        at(x + side - 1, y, 0),
        at(x + side - 1, y, 1),
        at(x + 1, y, 0),
        at(x + 1, y, 1),
        at(x, y + side - 1, 0),
        at(x, y + side - 1, 1),
    ]
    for u in range(units):
        tile = kall[u, half_rows : half_rows + 16, :].astype(F32)
        bias_ref[:, u * half_rows : (u + 1) * half_rows] = tile[1:2, :]
        if u in span_units:
            k = span_units.index(u)
            span_f32[0, k : k + 1, :] = tile[0:1, :]
            tile = vall[u, half_rows : half_rows + 16, :].astype(F32)
            span_f32[1, k : k + 1, :] = tile[0:1, :]
    kspan[...] = jnp.zeros_like(kspan)
    vspan[...] = jnp.zeros_like(vspan)
    zero8 = jnp.zeros((8, width), F32)
    kspan[0:16, :] = jnp.concatenate([span_f32[0], zero8]).astype(BF16)
    vspan[0:16, :] = jnp.concatenate([span_f32[1], zero8]).astype(BF16)
    span_tok = jnp.full((1, width), 1 << 20, jnp.int32)
    for k, tok in enumerate(span_toks):
        span_tok = jnp.where(lane == k, tok, span_tok)

    exponent = width**-0.5 / math.log(2.0)
    contract = (((1,), (1,)), ((), ()))
    chunk = 2 * half_rows

    def o1_copies(py):
        return [
            pltpu.make_async_remote_copy(
                src_ref=src.at[py],
                dst_ref=dst.at[y],
                send_sem=o1_send.at[k, py],
                recv_sem=o1_recv.at[k, y],
                device_id={"seq": at(x, py, core)},
                device_id_type=MESH,
            )
            for k, (src, dst) in enumerate(((o1src, o1), (s1src, s1)))
        ]

    def o1_arrivals(py):
        return [
            pltpu.make_async_remote_copy(
                src_ref=src.at[py],
                dst_ref=dst.at[py],
                send_sem=o1_send.at[k, py],
                recv_sem=o1_recv.at[k, py],
                device_id={"seq": at(x, py, core)},
                device_id_type=MESH,
            )
            for k, (src, dst) in enumerate(((o1src, o1), (s1src, s1)))
        ]

    def attend(py):
        query = q2[py].astype(F32).reshape(piece, width).astype(BF16)
        best = None
        for u in range(0, units, 2):
            keys = kall[u : u + 2, 0:half_rows, :].reshape(chunk, width)
            s = lax.dot_general(query, keys, contract, preferred_element_type=F32)
            s = s + bias_ref[:, u * half_rows : (u + 2) * half_rows]
            scores[:, u * half_rows : (u + 2) * half_rows] = s
            for k in range(chunk // width):
                part = s[:, k * width : (k + 1) * width]
                best = part if best is None else jnp.maximum(best, part)
        s = lax.dot_general(query, kspan[...], contract, preferred_element_type=F32)
        q_tok = py * row_toks + lax.broadcasted_iota(jnp.int32, (piece, width), 0) // GROUP
        s_span = jnp.where(span_tok <= q_tok, s, DEAD)
        best = jnp.maximum(best, s_span)
        top = jnp.maximum(jnp.max(best, axis=1, keepdims=True), FLOOR)
        w = jnp.exp2((s_span - top) * exponent)
        total = w
        num = jnp.dot(w.astype(BF16), vspan[...], preferred_element_type=F32)
        for u in range(0, units, 2):
            s = scores[:, u * half_rows : (u + 2) * half_rows]
            w = jnp.exp2((s - top) * exponent)
            for k in range(chunk // width):
                total = total + w[:, k * width : (k + 1) * width]
            vals = vall[u : u + 2, 0:half_rows, :].reshape(chunk, width)
            num = num + jnp.dot(w.astype(BF16), vals, preferred_element_type=F32)
        den = jnp.sum(total, axis=1, keepdims=True)
        cols = lax.broadcasted_iota(jnp.int32, (piece, width), 1)
        stat = jnp.where(cols == 0, top, jnp.where(cols == 1, den, 0.0))
        return num.astype(BF16), stat.T[0:8, :]

    num, stat = attend(y)
    o1[y] = num
    s1[y] = stat

    @pl.loop(1, side)
    def _(k):
        dy = jnp.where(k % 2 == 1, (k + 1) // 2, side - k // 2)
        py = (y + dy) % side
        q2_arrival(py).wait_recv()
        num, stat = attend(py)
        o1src[py] = num
        s1src[py] = stat
        for copy in o1_copies(py):
            copy.start()

    for dy in near_first:
        for arrival in o1_arrivals((y + dy) % side):
            arrival.wait_recv()
    tops, dens = [], []
    weight_rows = []
    srcs = []
    for b in range(2):
        ys = [(x // 2 + b) % 2 + 2 * k for k in range(side // 2)]
        stats = [s1[py] for py in ys]
        top = functools.reduce(jnp.maximum, [s[0:1, :] for s in stats])
        ws = [jnp.exp2((s[0:1, :] - top) * exponent) for s in stats]
        den = sum(w * s[1:2, :] for w, s in zip(ws, stats))
        tops.append(top)
        dens.append(den)
        weight_rows += ws
        srcs.append(ys)
    stacked = jnp.concatenate(weight_rows, axis=0)
    wide = jnp.concatenate([stacked, jnp.zeros((width - 8, width), F32)], axis=0)
    columns = wide.T
    row_id = lax.broadcasted_iota(jnp.int32, (8, width), 0)
    merged_stat = jnp.zeros((8, width), F32)
    for b in range(2):
        total = None
        for k, py in enumerate(srcs[b]):
            part = o1[py].astype(F32) * columns[:, 4 * b + k : 4 * b + k + 1]
            total = part if total is None else total + part
        o2src[b] = total.reshape(row_toks, GROUP, width).astype(BF16)
        merged_stat = jnp.where(row_id == 2 * b, tops[b], merged_stat)
        merged_stat = jnp.where(row_id == 2 * b + 1, dens[b], merged_stat)
    s2src[...] = merged_stat

    def o2_copies(px, pc):
        tok = 2 * px + pc
        return [
            pltpu.make_async_remote_copy(
                src_ref=src,
                dst_ref=dst.at[2 * x + core],
                send_sem=o2_send.at[k, tok],
                recv_sem=o2_recv.at[k, 2 * x + core],
                device_id={"seq": at(px, y, pc)},
                device_id_type=MESH,
            )
            for k, (src, dst) in enumerate(((o2src.at[:, tok], o2), (s2src, s2)))
        ]

    def o2_arrivals(px, pc):
        tok = 2 * px + pc
        return [
            pltpu.make_async_remote_copy(
                src_ref=src,
                dst_ref=dst.at[tok],
                send_sem=o2_send.at[k, tok],
                recv_sem=o2_recv.at[k, tok],
                device_id={"seq": at(px, y, pc)},
                device_id_type=MESH,
            )
            for k, (src, dst) in enumerate(((o2src.at[:, 0], o2), (s2src, s2)))
        ]

    for px, pc in row_partners:
        for copy in o2_copies(px, pc):
            copy.start()
    o2[2 * x + core] = o2src[:, 2 * x + core]
    s2[2 * x + core] = merged_stat
    for px, pc in row_partners:
        for arrival in o2_arrivals(px, pc):
            arrival.wait_recv()

    normal = []
    for e in range(2):
        for pc in range(2):
            for b in range(2):
                stats = [s2[2 * (e + 2 * k) + pc] for k in range(side // 2)]
                top = functools.reduce(jnp.maximum, [s[2 * b : 2 * b + 1, :] for s in stats])
                ws = [jnp.exp2((s[2 * b : 2 * b + 1, :] - top) * exponent) for s in stats]
                den = sum(w * s[2 * b + 1 : 2 * b + 2, :] for w, s in zip(ws, stats))
                normal += [w / den for w in ws]
    wts[...] = jnp.zeros_like(wts)
    for k, w in enumerate(normal):
        wts[k : k + 1, :] = w
    wts[...] = wts[...].T
    mine = wts[pl.ds(pl.multiple_of((2 * x + core) * GROUP, GROUP), GROUP), :]
    for e in range(2):
        for pc in range(2):
            for b in range(2):
                total = None
                for k in range(side // 2):
                    col = ((e * 2 + pc) * 2 + b) * (side // 2) + k
                    part = o2[2 * (e + 2 * k) + pc, b].astype(F32) * mine[:, col : col + 1]
                    total = part if total is None else total + part
                head = 2 * (e + 2 * b) + pc
                out_ref[head * GROUP : (head + 1) * GROUP, :] = total

    for px, pc in row_partners:
        q1_copy(px, pc).wait_send()
        for copy in o2_copies(px, pc):
            copy.wait_send()
    for dy in near_first:
        q2_copy((y + dy) % side).wait_send()
        for copy in o1_copies((y + dy) % side):
            copy.wait_send()
    for copy in v_sends + k_sends:
        copy.wait_send()


def solution(mesh):
    seq = mesh.shape["seq"]
    side = math.isqrt(seq // 2)

    def body(
        queries, span_keys, span_values, cache_keys, cache_values, page_table, page_counts, span_start
    ):
        width = queries.shape[1] // H
        rows = cache_keys.shape[0]
        half = rows // 2
        row_toks = 2 * side
        piece = row_toks * GROUP
        table = jnp.asarray(rope_table(width, PAGE))
        units = 16
        vm = pltpu.VMEM
        dma = pltpu.SemaphoreType.DMA
        smem = pl.BlockSpec(memory_space=pltpu.SMEM)
        vmem = pl.BlockSpec(memory_space=pltpu.VMEM)
        hbm = pl.BlockSpec(memory_space=pl.ANY)
        scratch = [
            vm((1, H * width), BF16),
            vm((1, KVH * width), BF16),
            vm((1, KVH * width), BF16),
            vm((rows, KVH * width), BF16),
            vm((H, width), F32),
            vm((rows, width), F32),
            vm((rows, width), F32),
            vm((KVH, 2, half + 16, width), BF16),
            vm((KVH, 2, half + 16, width), BF16),
            vm((units, half + 16, width), BF16),
            vm((units, half + 16, width), BF16),
            vm((width, width), BF16),
            vm((width, width), BF16),
            vm((2, 8, width), F32),
            vm((1, units * half), F32),
            vm((2, 2, 2, GROUP, width), BF16),
            vm((2, row_toks, GROUP, width), BF16),
            vm((side, row_toks, GROUP, width), BF16),
            vm((piece, units * half), F32),
            vm((side, piece, width), BF16),
            vm((side, 8, width), F32),
            vm((side, piece, width), BF16),
            vm((side, 8, width), F32),
            vm((2, row_toks, GROUP, width), BF16),
            vm((8, width), F32),
            vm((row_toks, 2, GROUP, width), BF16),
            vm((row_toks, 8, width), F32),
            vm((width, width), F32),
            dma((4 + 2 * KVH,)),
            dma((2, 9)),
            dma((2, 9)),
            dma((row_toks,)),
            dma((row_toks,)),
            dma((side,)),
            dma((side,)),
            dma((2, side)),
            dma((2, side)),
            dma((2, row_toks)),
            dma((2, row_toks)),
        ]
        out = pl.pallas_call(
            functools.partial(kernel, side),
            out_shape=jax.ShapeDtypeStruct((H, width), F32),
            in_specs=[smem, smem, smem, vmem, hbm, hbm, hbm, hbm, hbm],
            out_specs=vmem,
            scratch_shapes=scratch,
            compiler_params=pltpu.CompilerParams(collective_id=0, has_side_effects=True),
            name="paged_prefix",
        )(
            span_start,
            page_counts,
            page_table,
            table,
            queries,
            span_keys,
            span_values,
            cache_keys,
            cache_values,
        )
        return out.astype(BF16).reshape(queries.shape)

    in_specs = (
        P(("groups", "seq"), None),
        P(("groups", "seq"), None),
        P(("groups", "seq"), None),
        P(("groups", "seq"), None),
        P(("groups", "seq"), None),
        P(("groups", "seq")),
        P(("groups", "seq")),
        P("groups"),
    )
    out_specs = P(("groups", "seq"), None)
    return jax.shard_map(body, mesh=mesh, in_specs=in_specs, out_specs=out_specs, check_vma=False)
```

time: 286 us -> 60 us (0.21)
  waiting for transfers between devices: 97.1 us -> 0 us
  starting transfers between devices: 67.5 us -> 0 us
  Pallas kernels: 0 us -> 57.1 us
  blocking collectives: 54 us -> 0 us
  local copies, waits for them, and re-layouts: 21.1 us -> 0.64 us
  between operations: 15.1 us -> 1.31 us
  matrix products: 13.1 us -> 0 us
  other arithmetic: 11.7 us -> 0.76 us
  loops' own time: 5.53 us -> 0 us
    all_to_all x5 -> x0, starting transfers between devices: 67.5 us -> none  [the longest x1 27.4 us: body(): lax.all_to_all(flag_parts, 'seq', split_axis=0, concat_axis=1, tiled=True)]
    all_to_all x5 -> x0, waiting for transfers between devices: 61.9 us -> none  [the longest x1 28.4 us: sent_together(): lax.all_to_all(both, axis, split_axis=split_dim, concat_axis=concat_dim,...]
    pallas_call x0 -> x1, Pallas kernels: none -> 57.1 us  [body(): pl.pallas_call(functools.partial(kernel, side), out_shape=jax.ShapeDtypeS...]
    all_gather x1 -> x0, blocking collectives: 54 us -> none  [side_by_side(): filled = lax.all_gather(both, axis, axis=dim, tiled=True)]
    all_gather x1 -> x0, waiting for transfers between devices: 35.2 us -> none  [body(): all_queries = lax.all_gather(query_rot, 'seq', axis=0, tiled=True)]
    dot_general x18 -> x0, matrix products: 13.1 us -> none  [the longest x8 10 us: one_block(): jnp.einsum('tgs,sd->tgd', weights.astype(jnp.bfloat16), value_one, prefer...]
    all_gather x1 -> x0, local copies, waits for them, and re-layouts: 8.77 us -> none  [body(): all_queries = lax.all_gather(query_rot, 'seq', axis=0, tiled=True)]
    another operation x1 -> x0, loops' own time: 5.53 us -> none  [body(): lax.map(one_block, jnp.arange(steps_count, dtype=jnp.int32))]
  transfers between devices with their start and end apart: 6 -> 0, of which waited for: 5 -> 0; matrix products, arithmetic and copies ran while one was open for 5% -> 0% of each run, Pallas kernels for 0% -> 0%
where the time goes in v1:
time: 60 us; the launch traced here: 59.8 us
  Pallas kernels  57.1 us (95%)
  between operations  1.31 us (2%)
  other arithmetic  0.76 us (1%)
  local copies, waits for them, and re-layouts  0.64 us (1%)
    pallas_call x1, Pallas kernels, body(): pl.pallas_call(functools.partial(kernel, side), out_shape=jax.ShapeDtypeS...  57.1 us

profile of v1, /device:TPU:513, one launch (start us, length us, event | category | flops | bytes accessed | tf_op | source)
XLA Modules:
  0.0 59.8 jit_solution(18073325446754291134)
XLA Ops:
  1.3 57.1 %paged_prefix.1 = f32[64,128]{1,0:T(8,128)} custom-call(s32[1]{0:T(128)S(6)} %copy.14.start_ref, s32[1]{0:T(128)S(6)} %copy.13.count_ref, s32[16]{0:T(128)} %pages_ref.1, f32[40,128]{1,0:T(8,128)} %constant.2.clone.table_ref, bf16[1,8192]{1,0:T(2,128)(2,1)} %q_hbm.1, bf16[1,1024]{1,0:T(2,128)(2,1)} %sk_hbm.1, bf16[1,1024]{1,0:T(2,128)(2,1)} %sv_hbm.1, ...), custom_call_target="tpu_custom_call" | custom-call | tf_op jit(solution)/shard_map/paged_prefix/pallas_call | solution.py:625
  58.4 0.8 %convert_bitcast_fusion = bf16[1,1,64,128]{3,2,1,0:T(8,128)(2,1)S(1)} fusion(f32[64,128]{1,0:T(8,128)} %paged_prefix.1), kind=kLoop, calls=%fused_computation.1 | loop fusion | flops 8192 | bytes 49152
  59.1 0.6 %copy.12 = bf16[1,1,64,128]{3,1,2,0:T(2,128)(2,1)} copy(bf16[1,1,64,128]{3,2,1,0:T(8,128)(2,1)S(1)} %convert_bitcast_fusion) | data formatting | bytes 32768

commit v2 on v1

v2 whole, which is shorter than its diff:
```python
import functools
import math

import jax
import jax.numpy as jnp
import numpy as np
from jax import lax
from jax.experimental import pallas as pl
from jax.experimental.pallas import tpu as pltpu
from jax.sharding import PartitionSpec as P

H = 64
KVH = 8
PAGE = 16
GROUP = H // KVH
ROPE_BASE = 1000000.0
DEAD = -1e30
FLOOR = -1e29
CLASSES = 4
MESH = pl.DeviceIdType.MESH
F32 = jnp.float32
BF16 = jnp.bfloat16


def rope_table(width, rows):
    half = width // 2
    freq = ROPE_BASE ** (-(np.arange(half, dtype=np.float64) * 2.0 / width))
    turns = np.concatenate([freq, freq]) / (2.0 * np.pi)
    pieces, rest = [], turns
    for _ in range(2):
        scale = 2.0 ** (np.floor(np.log2(rest)) - 7.0)
        part = np.floor(rest / scale) * scale
        pieces.append(part)
        rest = rest - part
    pieces.append(rest)
    sign = np.concatenate([-np.ones(half), np.ones(half)])
    angle = np.arange(rows, dtype=np.float64)[:, None] * np.concatenate([freq, freq])[None, :]
    pad = np.zeros((8 - len(pieces) - 1, width))
    return np.concatenate(
        [np.stack(pieces), sign[None], pad, np.cos(angle), np.sin(angle) * sign[None]]
    ).astype(np.float32)


def cos_sin(position, table_ref):
    def part(k):
        turn = position * table_ref[k : k + 1, :]
        return turn - jnp.floor(turn)

    turn = part(0) + part(1) + part(2)
    turn = turn - jnp.floor(turn + 0.5)
    angle = turn * (2.0 * math.pi)
    return jnp.cos(angle), jnp.sin(angle) * table_ref[3:4, :]


def kernel(
    side,
    start_ref,
    count_ref,
    pages_ref,
    table_ref,
    q_hbm,
    sk_hbm,
    sv_hbm,
    k_hbm,
    v_hbm,
    out_ref,
    q_raw,
    sk_raw,
    sv_raw,
    k_raw,
    q_rows,
    cos_ref,
    sin_ref,
    kx,
    vx,
    kall,
    vall,
    kspan,
    vspan,
    span_f32,
    bias_ref,
    qsrc,
    q1,
    q2,
    scores,
    o1src,
    s1src,
    o1,
    s1,
    o2src,
    s2src,
    o2,
    s2,
    wts,
    local_sem,
    kv_send,
    kv_recv,
    q1_send,
    q1_recv,
    q2_send,
    q2_recv,
    o1_send,
    o1_recv,
    o2_send,
    o2_recv,
):
    width = q_rows.shape[1]
    rows = k_hbm.shape[0]
    half_rows = rows // 2
    units = kall.shape[0]
    row_toks = 2 * side
    piece = row_toks * GROUP
    me = lax.axis_index("seq")
    core = me % 2
    x = (me // 2) % side
    y = me // (2 * side)
    u = jnp.where(core == 0, x, y)
    v = jnp.where(core == 0, y, x)
    other = 1 - core

    def dev(pu, pv, pc):
        pu, pv = pu % side, pv % side
        px = jnp.where(core == 0, pu, pv)
        py = jnp.where(core == 0, pv, pu)
        return (py * side + px) * 2 + pc

    def remote(src, dst, send, recv, device):
        return pltpu.make_async_remote_copy(
            src_ref=src,
            dst_ref=dst,
            send_sem=send,
            recv_sem=recv,
            device_id={"seq": device},
            device_id_type=MESH,
        )

    copies = [
        pltpu.make_async_copy(q_hbm, q_raw, local_sem.at[0]),
        pltpu.make_async_copy(sk_hbm, sk_raw, local_sem.at[1]),
        pltpu.make_async_copy(sv_hbm, sv_raw, local_sem.at[2]),
        pltpu.make_async_copy(k_hbm, k_raw, local_sem.at[3]),
    ]
    v_copies = []
    for h in range(KVH):
        for hf in range(2):
            v_copies.append(
                pltpu.make_async_copy(
                    v_hbm.at[pl.ds(hf * half_rows, half_rows), pl.ds(h * width, width)],
                    vx.at[h, hf, pl.ds(0, half_rows), :],
                    local_sem.at[4 + 2 * h + hf],
                )
            )
    for copy in copies + v_copies:
        copy.start()

    barrier = pltpu.get_barrier_semaphore()

    def greet(device):
        pl.semaphore_signal(barrier, inc=1, device_id={"seq": device}, device_id_type=MESH)

    for d in range(1, side):
        for pc in range(2):
            greet(dev(u + d, v, pc))
            greet(dev(u, v + d, pc))
    greet(dev(u, v, other))
    partners = 4 * (side - 1) + 1

    start = start_ref[0]
    count = count_ref[0]

    own_pos = (start + me).astype(F32)
    own_cos, own_sin = cos_sin(jnp.full((8, width), own_pos, F32), table_ref)
    copies[0].wait()
    q_all = q_raw[...].astype(F32)
    for r in range(H):
        q_rows[r : r + 1, :] = q_all[:, r * width : (r + 1) * width]
    for net in range(2):
        for e in range(2):
            for b in range(2):
                head = CLASSES * net + e + 2 * b
                part = q_rows[head * GROUP : (head + 1) * GROUP, :]
                turned = part * own_cos + pltpu.roll(part, width // 2, 1) * own_sin
                qsrc[net, e, b] = turned.astype(BF16)

    pl.semaphore_wait(barrier, partners)

    far_first = [side // 2]
    for step in range(side // 2 - 1, 0, -1):
        far_first += [step, side - step]
    near_first = far_first[::-1]
    q1_copies = []
    for d in far_first + [0]:
        if d:
            pu = (u + d) % side
            q1_copies.append(
                remote(
                    qsrc.at[core, pu % 2],
                    q1.at[:, 2 * u + core],
                    q1_send.at[2 * d],
                    q1_recv.at[2 * u + core],
                    dev(pu, v, core),
                )
            )
        pv = (v + d) % side
        q1_copies.append(
            remote(
                qsrc.at[other, pv % 2],
                q1.at[:, 2 * v + core],
                q1_send.at[2 * d + 1],
                q1_recv.at[2 * v + core],
                dev(u, pv, other),
            )
        )
    for copy in q1_copies:
        copy.start()
    for b in range(2):
        q1[b, 2 * u + core] = qsrc[core, u % 2, b]

    line_slots = [2 * ((u + d) % side) + pc for d in near_first for pc in range(2)]
    line_slots.append(2 * u + other)

    tile_row = lax.broadcasted_iota(jnp.int32, (16, width), 0)
    lane = lax.broadcasted_iota(jnp.int32, (1, width), 1)
    half_pages = half_rows // PAGE
    biases = []
    for hf in range(2):
        page = jnp.zeros((1, width), jnp.int32)
        for j in range(half_pages):
            page = jnp.where(lane // PAGE == j, pages_ref[hf * half_pages + j], page)
        slot = hf * half_pages + lane // PAGE
        usable = (slot < count) & (page * PAGE + lane % PAGE < start)
        biases.append(jnp.where(usable, 0.0, DEAD).astype(F32))

    copies[2].wait()
    sv_all = sv_raw[...].astype(F32)
    for h in range(KVH):
        own_v = jnp.broadcast_to(sv_all[:, h * width : (h + 1) * width], (16, width))
        vx[h, 0, half_rows : half_rows + 16, :] = jnp.where(tile_row == 0, own_v, 0.0).astype(BF16)
        vx[h, 1, half_rows : half_rows + 16, :] = jnp.zeros((16, width), BF16)

    def kv_copies(which, buf, landing):
        out = []

        def add(there, here, head, half, slot, device):
            src = buf.at[head] if half is None else buf.at[head, half]
            dst = landing.at[pl.ds(slot, 2)] if half is None else landing.at[slot]
            out.append(remote(src, dst, kv_send.at[which, here], kv_recv.at[which, there], device))

        for own in (True, False):
            net = core if own else other
            nu, nv = (u, v) if own else (v, u)
            here = 0 if own else 1

            def at(pu, pv, own=own, net=net):
                return dev(pu, pv, net) if own else dev(pv, pu, net)

            base = nu + 2 * nv
            head = CLASSES * net + (base + 1) % CLASSES
            add(1 + core, 1 + here, head, None, 4 + 2 * core, at(nu + 1, nv))
            head = CLASSES * net + (base + 3) % CLASSES
            add(3 + core, 3 + here, head, None, 8 + 2 * core, at(nu + side - 1, nv))
            head = CLASSES * net + (base + 2) % CLASSES
            add(5 + core, 5 + here, head, 0, 12 + core, at(nu, nv + 1))
            add(7 + core, 7 + here, head, 1, 14 + core, at(nu, nv + side - 1))
            if not own:
                add(0, 0, CLASSES * net + base % CLASSES, None, 2 * core, at(nu, nv))
        return out

    def kv_arrivals(which, buf, landing):
        out = []

        def add(index, double, slot):
            out.append(
                remote(
                    buf.at[0] if double else buf.at[0, 0],
                    landing.at[pl.ds(slot, 2)] if double else landing.at[slot],
                    kv_send.at[which, index],
                    kv_recv.at[which, index],
                    dev(u, v, other),
                )
            )

        add(0, True, 2 * other)
        for pc in range(2):
            add(1 + pc, True, 4 + 2 * pc)
            add(3 + pc, True, 8 + 2 * pc)
            add(5 + pc, False, 12 + pc)
            add(7 + pc, False, 14 + pc)
        return out

    for copy in v_copies:
        copy.wait()
    v_sends = kv_copies(1, vx, vall)
    for copy in v_sends:
        copy.start()
    my_head = CLASSES * core + (u + 2 * v) % CLASSES
    for hf in range(2):
        vall[2 * core + hf] = vx[my_head, hf]

    page_pos = jnp.zeros((16, width), jnp.int32)
    for j in range(rows // PAGE):
        page_pos = jnp.where(tile_row == j, pages_ref[j] * PAGE, page_pos)
    page_cos, page_sin = cos_sin(page_pos.astype(F32), table_ref)
    row_cos = table_ref[8 : 8 + PAGE, :]
    row_sin = table_ref[8 + PAGE : 8 + 2 * PAGE, :]
    for j in range(rows // PAGE):
        pc_, ps_ = page_cos[j : j + 1, :], page_sin[j : j + 1, :]
        cos_ref[j * PAGE : (j + 1) * PAGE, :] = pc_ * row_cos - ps_ * row_sin
        sin_ref[j * PAGE : (j + 1) * PAGE, :] = ps_ * row_cos + pc_ * row_sin
    copies[1].wait()
    sk_all = sk_raw[...].astype(F32)
    copies[3].wait()
    for h in range(KVH):
        span = jnp.broadcast_to(sk_all[:, h * width : (h + 1) * width], (8, width))
        span = span * own_cos + pltpu.roll(span, width // 2, 1) * own_sin
        span = jnp.broadcast_to(span[0:1, :], (16, width))
        for hf in range(2):
            first = span if hf == 0 else jnp.zeros((16, width), F32)
            tile = jnp.where(tile_row == 0, first, jnp.where(tile_row == 1, biases[hf], 0.0))
            kx[h, hf, half_rows : half_rows + 16, :] = tile.astype(BF16)

    @pl.loop(0, KVH)
    def _(h):
        cols = pl.ds(pl.multiple_of(h * width, width), width)
        for hf in range(2):
            span_rows = slice(hf * half_rows, (hf + 1) * half_rows)
            part = k_raw[span_rows, cols].astype(F32)
            turned = part * cos_ref[span_rows, :]
            turned = turned + pltpu.roll(part, width // 2, 1) * sin_ref[span_rows, :]
            kx[h, hf, 0:half_rows, :] = turned.astype(BF16)

    k_sends = kv_copies(0, kx, kall)
    for copy in k_sends:
        copy.start()
    for hf in range(2):
        kall[2 * core + hf] = kx[my_head, hf]

    for slot in line_slots:
        remote(
            qsrc.at[0, 0], q1.at[:, slot], q1_send.at[slot], q1_recv.at[slot], dev(u, v, other)
        ).wait_recv()

    def bit(pv):
        return (u // 2 + pv) % 2

    q2_sends = []
    for d in far_first:
        pv = (v + d) % side
        q2_sends.append(
            remote(q1.at[bit(pv)], q2.at[v], q2_send.at[pv], q2_recv.at[v], dev(u, pv, core))
        )
    for copy in q2_sends:
        copy.start()
    q2[v] = q1[bit(v)]

    def q2_arrival(pv):
        return remote(q1.at[0], q2.at[pv], q2_send.at[pv], q2_recv.at[pv], dev(u, pv, core))

    for copy in q1_copies:
        copy.wait_send()
    for arrival in kv_arrivals(1, vx, vall) + kv_arrivals(0, kx, kall):
        arrival.wait_recv()
    span_units = [0, 2, 4, 6, 8, 10, 12, 13]
    span_toks = [
        dev(pu, pv, pc)
        for pu, pv in ((u, v), (u + side - 1, v), (u + 1, v), (u, v + side - 1))
        for pc in range(2)
    ]
    for unit in range(units):
        tile = kall[unit, half_rows : half_rows + 16, :].astype(F32)
        bias_ref[:, unit * half_rows : (unit + 1) * half_rows] = tile[1:2, :]
        if unit in span_units:
            k = span_units.index(unit)
            span_f32[0, k : k + 1, :] = tile[0:1, :]
            tile = vall[unit, half_rows : half_rows + 16, :].astype(F32)
            span_f32[1, k : k + 1, :] = tile[0:1, :]
    kspan[...] = jnp.zeros_like(kspan)
    vspan[...] = jnp.zeros_like(vspan)
    zero8 = jnp.zeros((8, width), F32)
    kspan[0:16, :] = jnp.concatenate([span_f32[0], zero8]).astype(BF16)
    vspan[0:16, :] = jnp.concatenate([span_f32[1], zero8]).astype(BF16)
    span_tok = jnp.full((1, width), 1 << 20, jnp.int32)
    for k, tok in enumerate(span_toks):
        span_tok = jnp.where(lane == k, tok, span_tok)

    exponent = width**-0.5 / math.log(2.0)
    contract = (((1,), (1,)), ((), ()))
    chunk = 2 * half_rows
    pair = 2 * piece

    def o1_copies(pv):
        return [
            remote(src.at[pv], dst.at[v], o1_send.at[k, pv], o1_recv.at[k, v], dev(u, pv, core))
            for k, (src, dst) in enumerate(((o1src, o1), (s1src, s1)))
        ]

    def o1_arrivals(pv):
        return [
            remote(src.at[pv], dst.at[pv], o1_send.at[k, pv], o1_recv.at[k, pv], dev(u, pv, core))
            for k, (src, dst) in enumerate(((o1src, o1), (s1src, s1)))
        ]

    slot_of = lax.broadcasted_iota(jnp.int32, (piece, 1), 0) // GROUP

    def token_of(pv):
        along = jnp.where(core == 0, 2, 2 * side)
        across = jnp.where(core == 0, 2 * side, 2)
        return (slot_of // 2) * along + pv * across + slot_of % 2

    def attend(pvs):
        query = jnp.concatenate(
            [q2[pv].astype(F32).reshape(piece, width).astype(BF16) for pv in pvs]
        )
        best = None
        for unit in range(0, units, 2):
            keys = kall[unit : unit + 2, 0:half_rows, :].reshape(chunk, width)
            s = lax.dot_general(query, keys, contract, preferred_element_type=F32)
            s = s + bias_ref[:, unit * half_rows : (unit + 2) * half_rows]
            scores[:, unit * half_rows : (unit + 2) * half_rows] = s
            for k in range(chunk // width):
                part = s[:, k * width : (k + 1) * width]
                best = part if best is None else jnp.maximum(best, part)
        s = lax.dot_general(query, kspan[...], contract, preferred_element_type=F32)
        q_tok = jnp.concatenate([token_of(pv) for pv in pvs])
        s_span = jnp.where(span_tok <= q_tok, s, DEAD)
        best = jnp.maximum(best, s_span)
        top = jnp.maximum(jnp.max(best, axis=1, keepdims=True), FLOOR)
        w = jnp.exp2((s_span - top) * exponent)
        total = w
        num = jnp.dot(w.astype(BF16), vspan[...], preferred_element_type=F32)
        for unit in range(0, units, 2):
            s = scores[:, unit * half_rows : (unit + 2) * half_rows]
            w = jnp.exp2((s - top) * exponent)
            for k in range(chunk // width):
                total = total + w[:, k * width : (k + 1) * width]
            vals = vall[unit : unit + 2, 0:half_rows, :].reshape(chunk, width)
            num = num + jnp.dot(w.astype(BF16), vals, preferred_element_type=F32)
        den = jnp.sum(total, axis=1, keepdims=True)
        cols = lax.broadcasted_iota(jnp.int32, (pair, width), 1)
        stat = jnp.where(cols == 0, top, jnp.where(cols == 1, den, 0.0))
        for k, pv in enumerate(pvs):
            part = num[k * piece : (k + 1) * piece].astype(BF16)
            part_stat = stat[k * piece : (k + 1) * piece].T[0:2, :]
            o1src[pv] = part
            s1src[pv] = part_stat

            @pl.when(pv != v)
            def _(pv=pv):
                for copy in o1_copies(pv):
                    copy.start()

            @pl.when(pv == v)
            def _(pv=pv, part=part, part_stat=part_stat):
                o1[pv] = part
                s1[pv] = part_stat

    @pl.loop(0, side // 2)
    def _(k):
        pvs = [k + 1, jnp.where(k == side // 2 - 1, 0, side - 1 - k)]
        for pv in pvs:

            @pl.when(pv != v)
            def _(pv=pv):
                q2_arrival(pv).wait_recv()

        attend(pvs)

    for copy in v_sends + k_sends + q2_sends:
        copy.wait_send()
    for d in near_first:
        for arrival in o1_arrivals((v + d) % side):
            arrival.wait_recv()
    tops, dens, weight_rows, srcs = [], [], [], []
    for b in range(2):
        vs = [(u // 2 + b) % 2 + 2 * k for k in range(side // 2)]
        stats = [s1[pv] for pv in vs]
        top = functools.reduce(jnp.maximum, [s[0:1, :] for s in stats])
        ws = [jnp.exp2((s[0:1, :] - top) * exponent) for s in stats]
        den = sum(w * s[1:2, :] for w, s in zip(ws, stats))
        tops.append(top)
        dens.append(den)
        weight_rows += ws
        srcs.append(vs)
    stacked = jnp.concatenate(weight_rows, axis=0)
    wide = jnp.concatenate([stacked, jnp.zeros((width - 8, width), F32)], axis=0)
    columns = wide.T
    for b in range(2):
        total = None
        for k, pv in enumerate(srcs[b]):
            part = o1[pv].astype(F32) * columns[:, 4 * b + k : 4 * b + k + 1]
            total = part if total is None else total + part
        o2src[b] = total.reshape(row_toks, GROUP, width).astype(BF16)
        s2src[2 * b : 2 * b + 1, :] = tops[b]
        s2src[2 * b + 1 : 2 * b + 2, :] = dens[b]

    line = core * side + u
    o2_sends = []
    for d in far_first + [0]:
        for own in (True, False):
            if d == 0 and own:
                continue
            pu = (u + d) % side
            pc = core if own else other
            slot = 2 * pu + pc
            for k, (src, dst) in enumerate(((o2src.at[:, slot], o2), (s2src, s2))):
                o2_sends.append(
                    remote(
                        src, dst.at[line], o2_send.at[k, slot], o2_recv.at[k, line], dev(pu, v, pc)
                    )
                )
    for copy in o2_sends:
        copy.start()
    o2[line] = o2src[:, 2 * u + core]
    s2[line] = s2src[...]
    for d in near_first:
        for copy in o1_copies((v + d) % side):
            copy.wait_send()
    o2_lines = [core * side + (u + d) % side for d in near_first]
    o2_lines += [other * side + (v + d) % side for d in near_first + [0]]
    for src_line in o2_lines:
        for k, (src, dst) in enumerate(((o2src.at[:, 0], o2), (s2src, s2))):
            remote(
                src,
                dst.at[src_line],
                o2_send.at[k, src_line],
                o2_recv.at[k, src_line],
                dev(u, v, other),
            ).wait_recv()

    normal = []
    for net in range(2):
        for e in range(2):
            for b in range(2):
                stats = [s2[net * side + e + 2 * k] for k in range(side // 2)]
                top = functools.reduce(jnp.maximum, [s[2 * b : 2 * b + 1, :] for s in stats])
                ws = [jnp.exp2((s[2 * b : 2 * b + 1, :] - top) * exponent) for s in stats]
                den = sum(w * s[2 * b + 1 : 2 * b + 2, :] for w, s in zip(ws, stats))
                normal += [w / den for w in ws]
    wts[...] = jnp.zeros_like(wts)
    for k, w in enumerate(normal):
        wts[k : k + 1, :] = w
    wts[...] = wts[...].T
    slots = (2 * x + core, 2 * y + core)
    for net in range(2):
        mine = wts[pl.ds(pl.multiple_of(slots[net] * GROUP, GROUP), GROUP), :]
        for e in range(2):
            for b in range(2):
                total = None
                for k in range(side // 2):
                    col = ((net * 2 + e) * 2 + b) * (side // 2) + k
                    part = o2[net * side + e + 2 * k, b].astype(F32) * mine[:, col : col + 1]
                    total = part if total is None else total + part
                head = CLASSES * net + e + 2 * b
                for g in range(GROUP):
                    at = (head * GROUP + g) * width
                    out_ref[:, at : at + width] = total[g : g + 1, :]
    for copy in o2_sends:
        copy.wait_send()


def solution(mesh):
    seq = mesh.shape["seq"]
    side = math.isqrt(seq // 2)

    def body(
        queries, span_keys, span_values, cache_keys, cache_values, page_table, page_counts, span_start
    ):
        width = queries.shape[1] // H
        rows = cache_keys.shape[0]
        half = rows // 2
        row_toks = 2 * side
        piece = row_toks * GROUP
        table = jnp.asarray(rope_table(width, PAGE))
        units = 16
        vm = pltpu.VMEM
        dma = pltpu.SemaphoreType.DMA
        smem = pl.BlockSpec(memory_space=pltpu.SMEM)
        vmem = pl.BlockSpec(memory_space=pltpu.VMEM)
        hbm = pl.BlockSpec(memory_space=pl.ANY)
        scratch = [
            vm((1, H * width), BF16),
            vm((1, KVH * width), BF16),
            vm((1, KVH * width), BF16),
            vm((rows, KVH * width), BF16),
            vm((H, width), F32),
            vm((rows, width), F32),
            vm((rows, width), F32),
            vm((KVH, 2, half + 16, width), BF16),
            vm((KVH, 2, half + 16, width), BF16),
            vm((units, half + 16, width), BF16),
            vm((units, half + 16, width), BF16),
            vm((width, width), BF16),
            vm((width, width), BF16),
            vm((2, 8, width), F32),
            vm((1, units * half), F32),
            vm((2, 2, 2, GROUP, width), BF16),
            vm((2, row_toks, GROUP, width), BF16),
            vm((side, row_toks, GROUP, width), BF16),
            vm((2 * piece, units * half), F32),
            vm((side, piece, width), BF16),
            vm((side, 2, width), F32),
            vm((side, piece, width), BF16),
            vm((side, 2, width), F32),
            vm((2, row_toks, GROUP, width), BF16),
            vm((4, width), F32),
            vm((row_toks, 2, GROUP, width), BF16),
            vm((row_toks, 4, width), F32),
            vm((width, width), F32),
            dma((4 + 2 * KVH,)),
            dma((2, 9)),
            dma((2, 9)),
            dma((row_toks,)),
            dma((row_toks,)),
            dma((side,)),
            dma((side,)),
            dma((2, side)),
            dma((2, side)),
            dma((2, row_toks)),
            dma((2, row_toks)),
        ]
        out = pl.pallas_call(
            functools.partial(kernel, side),
            out_shape=jax.ShapeDtypeStruct(queries.shape, F32),
            in_specs=[smem, smem, smem, vmem, hbm, hbm, hbm, hbm, hbm],
            out_specs=vmem,
            scratch_shapes=scratch,
            compiler_params=pltpu.CompilerParams(collective_id=0, has_side_effects=True),
            name="paged_prefix",
        )(
            span_start,
            page_counts,
            page_table,
            table,
            queries,
            span_keys,
            span_values,
            cache_keys,
            cache_values,
        )
        return out.astype(BF16)

    in_specs = (
        P(("groups", "seq"), None),
        P(("groups", "seq"), None),
        P(("groups", "seq"), None),
        P(("groups", "seq"), None),
        P(("groups", "seq"), None),
        P(("groups", "seq")),
        P(("groups", "seq")),
        P("groups"),
    )
    out_specs = P(("groups", "seq"), None)
    return jax.shard_map(body, mesh=mesh, in_specs=in_specs, out_specs=out_specs, check_vma=False)
```

time: 60 us -> 54 us (0.900)
  Pallas kernels: 57.1 us -> 51.1 us
  local copies, waits for them, and re-layouts: 0.64 us -> 0 us
  other arithmetic: 0.76 us -> 1.4 us
    pallas_call x1, Pallas kernels: 57.1 us -> 51.1 us  [body(): pl.pallas_call(functools.partial(kernel, side), out_shape=jax.ShapeDtypeS...]
    convert_element_type x0 -> x1, other arithmetic: none -> 1.4 us  [body(): return out.astype(BF16)]
    unnamed x1 -> x0, other arithmetic: 0.76 us -> none
    unnamed x1 -> x0, local copies, waits for them, and re-layouts: 0.64 us -> none
where the time goes in v2:
time: 54 us; the launch traced here: 53.8 us
  Pallas kernels  51.1 us (95%)
  other arithmetic  1.4 us (3%)
  between operations  1.3 us (2%)
    pallas_call x1, Pallas kernels, body(): pl.pallas_call(functools.partial(kernel, side), out_shape=jax.ShapeDtypeS...  51.1 us
    convert_element_type x1, other arithmetic, body(): return out.astype(BF16)  1.4 us

profile of v2, /device:TPU:513, one launch (start us, length us, event | category | flops | bytes accessed | tf_op | source)
XLA Modules:
  0.0 53.8 jit_solution(13646593077583029295)
XLA Ops:
  1.3 51.1 %paged_prefix.1 = f32[1,8192]{1,0:T(1,128)} custom-call(s32[1]{0:T(128)S(6)} %copy.11.start_ref, s32[1]{0:T(128)S(6)} %copy.10.count_ref, s32[16]{0:T(128)} %pages_ref.1, f32[40,128]{1,0:T(8,128)} %constant.2.clone.table_ref, bf16[1,8192]{1,0:T(2,128)(2,1)} %q_hbm.1, bf16[1,1024]{1,0:T(2,128)(2,1)} %sk_hbm.1, bf16[1,1024]{1,0:T(2,128)(2,1)} %sv_hbm.1, ...), custom_call_target="tpu_custom_call" | custom-call | tf_op jit(solution)/shard_map/paged_prefix/pallas_call | solution.py:621
  52.4 1.4 %convert_element_type.3 = bf16[1,8192]{1,0:T(2,128)(2,1)} convert(f32[1,8192]{1,0:T(1,128)} %paged_prefix.1) | non-fusion elementwise | flops 8192 | bytes 49152 | tf_op jit(solution)/shard_map/convert_element_type | solution.py:640

commit v3 on v2

v3 whole, which is shorter than its diff:
```python
import functools
import math

import jax
import jax.numpy as jnp
import numpy as np
from jax import lax
from jax.experimental import pallas as pl
from jax.experimental.pallas import tpu as pltpu
from jax.sharding import PartitionSpec as P

H = 64
KVH = 8
PAGE = 16
GROUP = H // KVH
ROPE_BASE = 1000000.0
DEAD = -1e30
FLOOR = -1e29
CLASSES = 4
MESH = pl.DeviceIdType.MESH
F32 = jnp.float32
BF16 = jnp.bfloat16
EXTRA = 16


def rope_table(width, rows):
    half = width // 2
    freq = ROPE_BASE ** (-(np.arange(half, dtype=np.float64) * 2.0 / width))
    turns = np.concatenate([freq, freq]) / (2.0 * np.pi)
    pieces, rest = [], turns
    for _ in range(2):
        scale = 2.0 ** (np.floor(np.log2(rest)) - 7.0)
        part = np.floor(rest / scale) * scale
        pieces.append(part)
        rest = rest - part
    pieces.append(rest)
    sign = np.concatenate([-np.ones(half), np.ones(half)])
    angle = np.arange(rows, dtype=np.float64)[:, None] * np.concatenate([freq, freq])[None, :]
    pad = np.zeros((8 - len(pieces) - 1, width))
    return np.concatenate(
        [np.stack(pieces), sign[None], pad, np.cos(angle), np.sin(angle) * sign[None]]
    ).astype(np.float32)


def cos_sin(position, table_ref):
    def part(k):
        turn = position * table_ref[k : k + 1, :]
        return turn - jnp.floor(turn)

    turn = part(0) + part(1) + part(2)
    turn = turn - jnp.floor(turn + 0.5)
    angle = turn * (2.0 * math.pi)
    return jnp.cos(angle), jnp.sin(angle) * table_ref[3:4, :]


def in_three(value):
    high = value.astype(BF16).astype(F32)
    middle = (value - high).astype(BF16).astype(F32)
    return [high, middle, value - high - middle]


def kernel(
    side,
    start_hbm,
    count_hbm,
    pages_hbm,
    table_hbm,
    q_hbm,
    sk_hbm,
    sv_hbm,
    k_hbm,
    v_hbm,
    out_ref,
    start_ref,
    count_ref,
    pages_ref,
    table_ref,
    q_raw,
    sk_raw,
    sv_raw,
    k_raw,
    q_rows,
    cos_ref,
    sin_ref,
    kx,
    vx,
    kall,
    vall,
    vturned,
    kbias,
    rows16,
    kspan,
    vspan,
    qsrc,
    q1,
    q2,
    scores,
    o1src,
    o1,
    o2src,
    o2,
    local_sem,
    kv_send,
    kv_recv,
    q1_send,
    q1_recv,
    q2_send,
    q2_recv,
    o1_send,
    o1_recv,
    o2_send,
    o2_recv,
    told,
    side_in,
):
    width = q_rows.shape[1]
    rows = k_hbm.shape[0]
    half_rows = rows // 2
    units = kall.shape[0]
    toks = 2 * side
    piece = toks * GROUP
    me = lax.axis_index("seq")
    core = me % 2
    x = (me // 2) % side
    y = me // (2 * side)
    u = jnp.where(core == 0, x, y)
    v = jnp.where(core == 0, y, x)
    other = 1 - core

    def chip(px, py, pc):
        return ((py % side) * side + px % side) * 2 + pc

    def dev(pu, pv, pc):
        return chip(jnp.where(core == 0, pu, pv), jnp.where(core == 0, pv, pu), pc)

    def remote(src, dst, send, recv, device):
        return pltpu.make_async_remote_copy(
            src_ref=src,
            dst_ref=dst,
            send_sem=send,
            recv_sem=recv,
            device_id={"seq": device},
            device_id_type=MESH,
        )

    def sent(ref, sem):
        remote(ref, ref, sem, sem, chip(x, y, other)).wait_send()

    def landed(ref, sem):
        remote(ref, ref, sem, sem, chip(x, y, other)).wait_recv()

    local = {
        name: pltpu.make_async_copy(src, dst, local_sem.at[k])
        for k, (name, src, dst) in enumerate(
            (
                ("start", start_hbm, start_ref),
                ("count", count_hbm, count_ref),
                ("pages", pages_hbm, pages_ref),
                ("table", table_hbm, table_ref),
                ("q", q_hbm, q_raw),
                ("sk", sk_hbm, sk_raw),
                ("sv", sv_hbm, sv_raw),
                ("k", k_hbm, k_raw),
            )
        )
    }
    for copy in local.values():
        copy.start()
    for h in range(KVH):
        for hf in range(2):
            pltpu.make_async_copy(
                v_hbm.at[pl.ds(hf * half_rows, half_rows), pl.ds(h * width, width)],
                vx.at[h, hf],
                local_sem.at[len(local)],
            ).start()

    barrier = pltpu.get_barrier_semaphore()

    def signal(sem, device):
        pl.semaphore_signal(sem, inc=1, device_id={"seq": device}, device_id_type=MESH)

    for d in (1, side - 1):
        signal(barrier, chip(x + d, y, 0))
        signal(barrier, chip(x, y + d, 0))

    @pl.when(core == 1)
    def _():
        signal(barrier, chip(x, y, 0))
        for d in range(1, side):
            signal(barrier, chip(x + d, y, 1))
            signal(barrier, chip(x, y + d, 1))

    for name in ("start", "count", "pages", "table", "q"):
        local[name].wait()
    start = start_ref[0]
    count = count_ref[0]
    own_pos = (start + me).astype(F32)
    own_cos, own_sin = cos_sin(jnp.full((8, width), own_pos, F32), table_ref)
    q_all = q_raw[...].astype(F32)
    for r in range(H):
        q_rows[r : r + 1, :] = q_all[:, r * width : (r + 1) * width]
    for net in range(2):
        for e in range(2):
            for b in range(2):
                head = CLASSES * net + e + 2 * b
                part = q_rows[head * GROUP : (head + 1) * GROUP, :]
                turned = part * own_cos + pltpu.roll(part, width // 2, 1) * own_sin
                qsrc[net, e, b] = turned.astype(BF16)

    @pl.when(core == 0)
    def _():
        pl.semaphore_wait(barrier, 2 * 4 + 1)
        signal(told, chip(x, y, 1))

    @pl.when(core == 1)
    def _():
        pl.semaphore_wait(told, 1)

    def send_cache(which, buf, landing):
        def send(head, half, slot, device):
            src = buf.at[head] if half is None else buf.at[head, half]
            dst = landing.at[pl.ds(slot, 2)] if half is None else landing.at[slot]
            remote(src, dst, kv_send.at[which], kv_recv.at[which], device).start()

        for own in (True, False):
            net = core if own else other
            nu, nv = (u, v) if own else (v, u)

            def at(pu, pv, own=own, net=net):
                return dev(pu, pv, net) if own else dev(pv, pu, net)

            base = nu + 2 * nv
            head = CLASSES * net + (base + 1) % CLASSES
            send(head, None, 4 + 2 * core, at(nu + 1, nv))
            head = CLASSES * net + (base + 3) % CLASSES
            send(head, None, 8 + 2 * core, at(nu + side - 1, nv))
            head = CLASSES * net + (base + 2) % CLASSES
            send(head, 0, 12 + core, at(nu, nv + 1))
            send(head, 1, 14 + core, at(nu, nv + side - 1))
            if not own:
                send(CLASSES * net + base % CLASSES, None, 2 * core, at(nu, nv))

    my_head = CLASSES * core + (u + 2 * v) % CLASSES

    pltpu.make_async_copy(vx, vx, local_sem.at[len(local)]).wait()
    send_cache(1, vx, vall)
    for hf in range(2):
        vall[2 * core + hf] = vx[my_head, hf]

    tile_row = lax.broadcasted_iota(jnp.int32, (EXTRA, width), 0)
    lane = lax.broadcasted_iota(jnp.int32, (1, width), 1)
    half_pages = half_rows // PAGE
    biases = []
    for hf in range(2):
        page = jnp.zeros((1, width), jnp.int32)
        for j in range(half_pages):
            page = jnp.where(lane // PAGE == j, pages_ref[hf * half_pages + j], page)
        slot = hf * half_pages + lane // PAGE
        usable = (slot < count) & (page * PAGE + lane % PAGE < start)
        biases.append(jnp.where(usable, 0.0, DEAD).astype(F32))
    page_pos = jnp.zeros((16, width), jnp.int32)
    for j in range(rows // PAGE):
        page_pos = jnp.where(tile_row == j, pages_ref[j] * PAGE, page_pos)
    page_cos, page_sin = cos_sin(page_pos.astype(F32), table_ref)
    row_cos = table_ref[8 : 8 + PAGE, :]
    row_sin = table_ref[8 + PAGE : 8 + 2 * PAGE, :]
    for j in range(rows // PAGE):
        pc_, ps_ = page_cos[j : j + 1, :], page_sin[j : j + 1, :]
        cos_ref[j * PAGE : (j + 1) * PAGE, :] = pc_ * row_cos - ps_ * row_sin
        sin_ref[j * PAGE : (j + 1) * PAGE, :] = ps_ * row_cos + pc_ * row_sin
    for name in ("sk", "sv", "k"):
        local[name].wait()
    sk_all = sk_raw[...].astype(F32)
    sv_all = sv_raw[...].astype(F32)
    for h in range(KVH):
        span = jnp.broadcast_to(sk_all[:, h * width : (h + 1) * width], (8, width))
        span = span * own_cos + pltpu.roll(span, width // 2, 1) * own_sin
        span = jnp.broadcast_to(span[0:1, :], (EXTRA, width))
        value = jnp.broadcast_to(sv_all[:, h * width : (h + 1) * width], (EXTRA, width))
        for hf in range(2):
            tile = jnp.where(tile_row == 0, span, jnp.where(tile_row == 2, value, 0.0))
            tile = jnp.where(tile_row == 1, biases[hf], tile)
            kx[h, hf, half_rows : half_rows + EXTRA, :] = tile.astype(BF16)

    @pl.loop(0, KVH)
    def _(h):
        cols = pl.ds(pl.multiple_of(h * width, width), width)
        for hf in range(2):
            span_rows = slice(hf * half_rows, (hf + 1) * half_rows)
            part = k_raw[span_rows, cols].astype(F32)
            turned = part * cos_ref[span_rows, :]
            turned = turned + pltpu.roll(part, width // 2, 1) * sin_ref[span_rows, :]
            kx[h, hf, 0:half_rows, :] = turned.astype(BF16)

    far_first = [side // 2]
    for step in range(side // 2 - 1, 0, -1):
        far_first += [step, side - step]

    @pl.when(core == 1)
    def _():
        pl.semaphore_wait(barrier, 2 * (side - 1))
        signal(told, chip(x, y, 0))

    @pl.when(core == 0)
    def _():
        pl.semaphore_wait(told, 1)
        for d in far_first:
            signal(side_in, chip(x + d, y, 1))
            signal(side_in, chip(x, y + d, 1))

    def send_q1(net, along, device):
        spot = 2 * (x if net == 0 else y) + core
        remote(
            qsrc.at[net, along % 2], q1.at[net, :, spot], q1_send, q1_recv.at[net], device
        ).start()

    for d in far_first:
        send_q1(0, (x + d) % side, chip(x + d, y, 1))
        send_q1(1, (y + d) % side, chip(x, y + d, 1))

    @pl.when(core == 0)
    def _():
        send_q1(0, x, chip(x, y, 1))
        send_q1(1, y, chip(x, y, 1))

    send_cache(0, kx, kall)
    for hf in range(2):
        kall[2 * core + hf] = kx[my_head, hf]

    @pl.when(core == 1)
    def _():
        for net, spot in ((0, 2 * x + 1), (1, 2 * y + 1)):
            for b in range(2):
                q1[net, b, spot] = qsrc[net, (x if net == 0 else y) % 2, b]
        pl.semaphore_wait(side_in, 2 * (side - 1))
        for net in range(2):
            landed(q1.at[net, :, pl.ds(0, toks - 1)], q1_recv.at[net])
            nu, nv = (x, y) if net == 0 else (y, x)

            def send_q2(pv, device, net=net, nu=nu, nv=nv):
                remote(
                    q1.at[net, (nu // 2 + pv) % 2],
                    q2.at[nv],
                    q2_send.at[net],
                    q2_recv.at[nv],
                    device,
                ).start()

            for d in far_first:
                pv = (nv + d) % side
                send_q2(pv, chip(x, pv, 0) if net == 0 else chip(pv, y, 1))
            if net == 0:
                send_q2(y, chip(x, y, 0))
            else:
                q2[x] = q1[1, (y // 2 + x) % 2]

    landed(vall.at[pl.ds(0, units - 2)], kv_recv.at[1])
    for unit in range(units):
        vturned[:, unit * half_rows : (unit + 1) * half_rows] = vall[unit].T

    landed(kall.at[pl.ds(0, units - 2)], kv_recv.at[0])
    span_units = [0, 2, 4, 6, 8, 10, 12, 13]
    span_toks = [
        dev(pu, pv, pc)
        for pu, pv in ((u, v), (u + side - 1, v), (u + 1, v), (u, v + side - 1))
        for pc in range(2)
    ]
    rows16[...] = jnp.zeros_like(rows16)
    for unit in range(units):
        tile = kall[unit, half_rows : half_rows + EXTRA, :].astype(F32)
        rows16[0, unit : unit + 1, :] = tile[1:2, :]
        if unit in span_units:
            k = span_units.index(unit)
            rows16[1, k : k + 1, :] = tile[0:1, :]
            rows16[2, k : k + 1, :] = tile[2:3, :]
    zeros = jnp.zeros((width - 16, width), F32)
    bias_cols = jnp.concatenate([rows16[0], zeros]).T
    for unit in range(units):
        turned = bias_cols if unit == 0 else pltpu.roll(bias_cols, width - unit, 1)
        kbias[unit * half_rows : (unit + 1) * half_rows, :] = turned.astype(BF16)
    kspan[...] = rows16[1].astype(BF16)
    vspan[...] = jnp.concatenate([rows16[2], zeros]).T.astype(BF16)
    span_tok = jnp.full((16, piece), 1 << 20, jnp.int32)
    for k, tok in enumerate(span_toks):
        span_tok = jnp.where(tile_row == k, tok, span_tok)

    exponent = width**-0.5 / math.log(2.0)
    contract = (((1,), (1,)), ((), ()))
    chunk = 2 * half_rows
    cols = 2 * piece

    def send_o1(pv):
        remote(
            o1src.at[pv], o1.at[core, v], o1_send, o1_recv.at[core], dev(u, pv, 1)
        ).start()

    col_slot = lax.broadcasted_iota(jnp.int32, (1, piece), 1) // GROUP
    tok_along = jnp.where(core == 0, 2, 2 * side)
    tok_across = jnp.where(core == 0, 2 * side, 2)
    col_tok = (col_slot // 2) * tok_along + col_slot % 2
    one_hot = jnp.where(lax.broadcasted_iota(jnp.int32, (cols, width), 1) == 0, 1.0, 0.0).astype(BF16)

    def attend(pvs):
        query = jnp.concatenate(
            [q2[pv].astype(F32).reshape(piece, width).astype(BF16) for pv in pvs]
        )
        query = jnp.concatenate([query, one_hot], axis=1)
        s = lax.dot_general(kspan[...], query[:, :width], contract, preferred_element_type=F32)
        live = jnp.concatenate([span_tok <= col_tok + pv * tok_across for pv in pvs], axis=1)
        s_span = jnp.where(live, s, DEAD)
        best = jnp.maximum(s_span[0:8], s_span[8:16])
        for k in range(units // 2):
            keys = kall[2 * k : 2 * k + 2, 0:half_rows, :].reshape(chunk, width)
            keys = jnp.concatenate([keys, kbias[k * chunk : (k + 1) * chunk, :]], axis=1)
            s = lax.dot_general(keys, query, contract, preferred_element_type=F32)
            scores[k * chunk : (k + 1) * chunk, :] = s
            best = jnp.maximum(best, jnp.max(s.reshape(chunk // 8, 8, cols), axis=0))
        top = jnp.maximum(jnp.max(best, axis=0, keepdims=True), FLOOR)
        w = jnp.exp2((s_span - top) * exponent)
        total = w[0:8] + w[8:16]
        w = jnp.concatenate([w, jnp.zeros((width - 16, cols), F32)])
        num = jnp.dot(vspan[...], w.astype(BF16), preferred_element_type=F32)
        for k in range(units // 2):
            w = jnp.exp2((scores[k * chunk : (k + 1) * chunk, :] - top) * exponent)
            total = total + jnp.sum(w.reshape(chunk // 8, 8, cols), axis=0)
            num = num + jnp.dot(
                vturned[:, k * chunk : (k + 1) * chunk],
                w.astype(BF16),
                preferred_element_type=F32,
            )
        den = jnp.sum(total, axis=0, keepdims=True)
        stat = jnp.concatenate(in_three(top) + in_three(den) + [jnp.zeros((EXTRA - 6, cols), F32)])
        for k, pv in enumerate(pvs):
            lanes = slice(k * piece, (k + 1) * piece)
            o1src[pv, 0:width, :] = num[:, lanes].astype(BF16)
            o1src[pv, width : width + EXTRA, :] = stat[:, lanes].astype(BF16)

            @pl.when((pv != v) | (core == 0))
            def _(pv=pv):
                send_o1(pv)

            @pl.when((pv == v) & (core == 1))
            def _(pv=pv):
                o1[1, pv] = o1src[pv]

    @pl.loop(0, side // 2)
    def _(k):
        pvs = [k + 1, (k + 1 + side // 2) % side]
        for pv in pvs:

            @pl.when((pv != v) | (core == 0))
            def _(pv=pv):
                landed(q2.at[pv], q2_recv.at[pv])

        attend(pvs)

    sent(vall.at[pl.ds(0, units - 2)], kv_send.at[1])
    sent(kall.at[pl.ds(0, units - 2)], kv_send.at[0])

    @pl.when(core == 0)
    def _():
        sent(q1.at[0], q1_send)
        sent(o1.at[0], o1_send)

    @pl.when(core == 1)
    def _():
        sent(q1.at[0, :, pl.ds(0, toks - 2)], q1_send)
        sent(q2, q2_send.at[0])
        sent(q2.at[pl.ds(0, side - 1)], q2_send.at[1])
        for net in range(2):
            landed(o1.at[net] if net == 0 else o1.at[net, pl.ds(0, side - 1)], o1_recv.at[net])
            nu = x if net == 0 else y
            stats = []
            for b in range(2):
                vs = [(nu // 2 + b) % 2 + 2 * k for k in range(side // 2)]
                tiles = [o1[net, pv, width : width + EXTRA, :].astype(F32) for pv in vs]
                tops = [t[0:1] + t[1:2] + t[2:3] for t in tiles]
                dens = [t[3:4] + t[4:5] + t[5:6] for t in tiles]
                top = functools.reduce(jnp.maximum, tops)
                ws = [jnp.exp2((t - top) * exponent) for t in tops]
                stats += in_three(top) + in_three(sum(w * d for w, d in zip(ws, dens)))
                total = None
                for w, pv in zip(ws, vs):
                    part = o1[net, pv, 0:width, :].astype(F32) * w
                    total = part if total is None else total + part
                o2src[net, :, b] = total.T.reshape(toks, GROUP, width).astype(BF16)
            stat = jnp.concatenate(stats + [jnp.zeros((width - len(stats), piece), F32)]).T
            o2src[net, :, 2] = stat.reshape(toks, GROUP, width).astype(BF16)
            line = x if net == 0 else side + y

            def send_o2(slot, device, net=net, line=line):
                remote(o2src.at[net, slot], o2.at[line], o2_send, o2_recv, device).start()

            for d in far_first:
                for pc in range(2):
                    if net == 0:
                        px = (x + d) % side
                        send_o2(2 * px + pc, chip(px, y, pc))
                    else:
                        py = (y + d) % side
                        send_o2(2 * py + pc, chip(x, py, pc))
            send_o2(2 * nu, chip(x, y, 0))
            o2[line] = o2src[net, 2 * nu + 1]
        sent(o1.at[0, pl.ds(0, side - 1)], o1_send)
        landed(o2.at[pl.ds(0, toks - 2)], o2_recv)
        sent(o2src.at[:, pl.ds(0, toks - 1)], o2_send)

    @pl.when(core == 0)
    def _():
        landed(o2, o2_recv)

    tops, dens = [[], []], [[], []]
    for src in range(toks):
        tile = o2[src, 2].astype(F32)
        tile = tile + pltpu.roll(tile, width - 1, 1) + pltpu.roll(tile, width - 2, 1)
        for b in range(2):
            tops[b].append(jnp.broadcast_to(tile[:, 6 * b : 6 * b + 1], (GROUP, width)))
            dens[b].append(jnp.broadcast_to(tile[:, 6 * b + 3 : 6 * b + 4], (GROUP, width)))
    for net in range(2):
        for e in range(2):
            srcs = [net * side + e + 2 * k for k in range(side // 2)]
            for b in range(2):
                top = functools.reduce(jnp.maximum, [tops[b][s] for s in srcs])
                ws = [jnp.exp2((tops[b][s] - top) * exponent) for s in srcs]
                den = sum(w * dens[b][s] for w, s in zip(ws, srcs))
                num = sum(w * o2[s, b].astype(F32) for w, s in zip(ws, srcs))
                head = CLASSES * net + e + 2 * b
                out_ref[head * GROUP : (head + 1) * GROUP, :] = num / den


def solution(mesh):
    seq = mesh.shape["seq"]
    side = math.isqrt(seq // 2)

    def body(
        queries, span_keys, span_values, cache_keys, cache_values, page_table, page_counts, span_start
    ):
        width = queries.shape[1] // H
        rows = cache_keys.shape[0]
        half = rows // 2
        toks = 2 * side
        piece = toks * GROUP
        table = jnp.asarray(rope_table(width, PAGE))
        units = 16
        vm = pltpu.VMEM
        dma = pltpu.SemaphoreType.DMA
        hbm = pl.BlockSpec(memory_space=pl.ANY)
        scratch = [
            pltpu.SMEM(span_start.shape, jnp.int32),
            pltpu.SMEM(page_counts.shape, jnp.int32),
            pltpu.SMEM(page_table.shape, jnp.int32),
            vm(table.shape, F32),
            vm((1, H * width), BF16),
            vm((1, KVH * width), BF16),
            vm((1, KVH * width), BF16),
            vm((rows, KVH * width), BF16),
            vm((H, width), F32),
            vm((rows, width), F32),
            vm((rows, width), F32),
            vm((KVH, 2, half + EXTRA, width), BF16),
            vm((KVH, 2, half, width), BF16),
            vm((units, half + EXTRA, width), BF16),
            vm((units, half, width), BF16),
            vm((width, units * half), BF16),
            vm((units * half, width), BF16),
            vm((3, 16, width), F32),
            vm((16, width), BF16),
            vm((width, width), BF16),
            vm((2, 2, 2, GROUP, width), BF16),
            vm((2, 2, toks, GROUP, width), BF16),
            vm((side, toks, GROUP, width), BF16),
            vm((units * half, 2 * piece), F32),
            vm((side, width + EXTRA, piece), BF16),
            vm((2, side, width + EXTRA, piece), BF16),
            vm((2, toks, 3, GROUP, width), BF16),
            vm((toks, 3, GROUP, width), BF16),
            dma((9,)),
            dma((2,)),
            dma((2,)),
            dma(()),
            dma((2,)),
            dma((2,)),
            dma((side,)),
            dma(()),
            dma((2,)),
            dma(()),
            dma(()),
            pltpu.SemaphoreType.REGULAR,
            pltpu.SemaphoreType.REGULAR,
        ]
        out = pl.pallas_call(
            functools.partial(kernel, side),
            out_shape=pltpu.VMEM((H, width), F32),
            in_specs=[hbm] * 9,
            out_specs=pl.BlockSpec(memory_space=pltpu.VMEM),
            scratch_shapes=scratch,
            compiler_params=pltpu.CompilerParams(collective_id=0, has_side_effects=True),
            name="paged_prefix",
        )(
            span_start,
            page_counts,
            page_table,
            table,
            queries,
            span_keys,
            span_values,
            cache_keys,
            cache_values,
        )
        return out.reshape(queries.shape).astype(BF16)

    in_specs = (
        P(("groups", "seq"), None),
        P(("groups", "seq"), None),
        P(("groups", "seq"), None),
        P(("groups", "seq"), None),
        P(("groups", "seq"), None),
        P(("groups", "seq")),
        P(("groups", "seq")),
        P("groups"),
    )
    out_specs = P(("groups", "seq"), None)
    return jax.shard_map(body, mesh=mesh, in_specs=in_specs, out_specs=out_specs, check_vma=False)
```

time: 54 us -> 49.4 us (0.915)
  Pallas kernels: 51.1 us -> 47.3 us
  other arithmetic: 1.4 us -> 0.01 us
  local copies, waits for them, and re-layouts: 0 us -> 0.64 us
    pallas_call x1, Pallas kernels: 51.1 us -> 47.3 us  [body(): pl.pallas_call(functools.partial(kernel, side), out_shape=pltpu.VMEM((H,...]
    convert_element_type x1 -> x0, other arithmetic: 1.4 us -> none  [body(): return out.astype(BF16)]
    unnamed x0 -> x1, local copies, waits for them, and re-layouts: none -> 0.64 us
where the time goes in v3:
time: 49.4 us; the launch traced here: 49.3 us
  Pallas kernels  47.3 us (96%)
  between operations  1.31 us (3%)
  local copies, waits for them, and re-layouts  0.64 us (1%)
    pallas_call x1, Pallas kernels, body(): pl.pallas_call(functools.partial(kernel, side), out_shape=pltpu.VMEM((H,...  47.3 us

profile of v3, /device:TPU:513, one launch (start us, length us, event | category | flops | bytes accessed | tf_op | source)
XLA Modules:
  0.0 49.3 jit_solution(13681399310842158754)
XLA Ops:
  1.3 47.3 %paged_prefix.1 = f32[64,128]{1,0:T(8,128)S(1)} custom-call(s32[1]{0:T(128)S(6)} %copy.14.start_hbm, s32[1]{0:T(128)S(6)} %copy.13.count_hbm, s32[16]{0:T(128)} %pages_hbm.1, f32[40,128]{1,0:T(8,128)} %constant.2.clone.table_hbm, bf16[1,8192]{1,0:T(2,128)(2,1)} %q_hbm.1, bf16[1,1024]{1,0:T(2,128)(2,1)} %sk_hbm.1, bf16[1,1024]{1,0:T(2,128)(2,1)} %sv_hbm.1, ...), custom_call_target="tpu_custom_call" | custom-call | tf_op jit(solution)/shard_map/paged_prefix/pallas_call | solution.py:591
  48.6 0.6 %copy.12 = bf16[1,1,64,128]{3,1,2,0:T(2,128)(2,1)} copy(bf16[1,1,64,128]{3,2,1,0:T(8,128)(2,1)S(1)} %convert_bitcast_fusion) | data formatting | bytes 32768
  (1 shorter events, 0.0 us)

commit v4 on v3

--- a/solution.py
+++ b/solution.py
@@ -102,6 +102,7 @@
     local_sem,
     kv_send,
     kv_recv,
+    q0_sem,
     q1_send,
     q1_recv,
     q2_send,
@@ -111,7 +112,11 @@
     o2_send,
     o2_recv,
     told,
+    told_far,
+    near_side,
     side_in,
+    span_scores,
+    tops,
 ):
     width = q_rows.shape[1]
     rows = k_hbm.shape[0]
@@ -179,13 +184,13 @@
     def signal(sem, device):
         pl.semaphore_signal(sem, inc=1, device_id={"seq": device}, device_id_type=MESH)
 
-    for d in (1, side - 1):
-        signal(barrier, chip(x + d, y, 0))
-        signal(barrier, chip(x, y + d, 0))
+    neighbours = ((1, 0), (side - 1, 0), (0, 1), (0, side - 1))
 
     @pl.when(core == 1)
     def _():
         signal(barrier, chip(x, y, 0))
+        for dx, dy in neighbours:
+            signal(barrier, chip(x + dx, y + dy, 0))
         for d in range(1, side):
             signal(barrier, chip(x + d, y, 1))
             signal(barrier, chip(x, y + d, 1))
@@ -205,47 +210,54 @@
                 head = CLASSES * net + e + 2 * b
                 part = q_rows[head * GROUP : (head + 1) * GROUP, :]
                 turned = part * own_cos + pltpu.roll(part, width // 2, 1) * own_sin
-                qsrc[net, e, b] = turned.astype(BF16)
+                qsrc[net, e, b, core] = turned.astype(BF16)
 
     @pl.when(core == 0)
     def _():
-        pl.semaphore_wait(barrier, 2 * 4 + 1)
+        pl.semaphore_wait(barrier, 4 + 1)
         signal(told, chip(x, y, 1))
+        for dx, dy in neighbours:
+            signal(near_side, chip(x + dx, y + dy, 1))
+        remote(qsrc.at[:, :, :, 0], qsrc.at[:, :, :, 0], q0_sem, q0_sem, chip(x, y, 1)).start()
 
     @pl.when(core == 1)
     def _():
         pl.semaphore_wait(told, 1)
 
-    def send_cache(which, buf, landing):
+    def send_cache(which, net):
+        buf, landing = (kx, kall) if which == 0 else (vx, vall)
+
         def send(head, half, slot, device):
             src = buf.at[head] if half is None else buf.at[head, half]
             dst = landing.at[pl.ds(slot, 2)] if half is None else landing.at[slot]
             remote(src, dst, kv_send.at[which], kv_recv.at[which], device).start()
 
-        for own in (True, False):
-            net = core if own else other
-            nu, nv = (u, v) if own else (v, u)
-
-            def at(pu, pv, own=own, net=net):
-                return dev(pu, pv, net) if own else dev(pv, pu, net)
-
-            base = nu + 2 * nv
-            head = CLASSES * net + (base + 1) % CLASSES
-            send(head, None, 4 + 2 * core, at(nu + 1, nv))
-            head = CLASSES * net + (base + 3) % CLASSES
-            send(head, None, 8 + 2 * core, at(nu + side - 1, nv))
-            head = CLASSES * net + (base + 2) % CLASSES
-            send(head, 0, 12 + core, at(nu, nv + 1))
-            send(head, 1, 14 + core, at(nu, nv + side - 1))
-            if not own:
-                send(CLASSES * net + base % CLASSES, None, 2 * core, at(nu, nv))
-
-    my_head = CLASSES * core + (u + 2 * v) % CLASSES
+        nu, nv = (x, y) if net == 0 else (y, x)
+
+        def at(pu, pv):
+            return chip(pu, pv, 0) if net == 0 else chip(pv, pu, 1)
+
+        base = nu + 2 * nv
+        head = CLASSES * net + (base + 1) % CLASSES
+        send(head, None, 4 + 2 * core, at(nu + 1, nv))
+        head = CLASSES * net + (base + 3) % CLASSES
+        send(head, None, 8 + 2 * core, at(nu + side - 1, nv))
+        head = CLASSES * net + (base + 2) % CLASSES
+        send(head, 0, 12 + core, at(nu, nv + 1))
+        send(head, 1, 14 + core, at(nu, nv + side - 1))
+        head = CLASSES * net + base % CLASSES
+
+        @pl.when(core == net)
+        def _():
+            for hf in range(2):
+                landing[2 * core + hf] = buf[head, hf]
+
+        @pl.when(core != net)
+        def _():
+            send(head, None, 2 * core, at(nu, nv))
 
     pltpu.make_async_copy(vx, vx, local_sem.at[len(local)]).wait()
-    send_cache(1, vx, vall)
-    for hf in range(2):
-        vall[2 * core + hf] = vx[my_head, hf]
+    send_cache(1, 1)
 
     tile_row = lax.broadcasted_iota(jnp.int32, (EXTRA, width), 0)
     lane = lax.broadcasted_iota(jnp.int32, (1, width), 1)
@@ -282,59 +294,63 @@
             tile = jnp.where(tile_row == 1, biases[hf], tile)
             kx[h, hf, half_rows : half_rows + EXTRA, :] = tile.astype(BF16)
 
-    @pl.loop(0, KVH)
-    def _(h):
-        cols = pl.ds(pl.multiple_of(h * width, width), width)
-        for hf in range(2):
-            span_rows = slice(hf * half_rows, (hf + 1) * half_rows)
-            part = k_raw[span_rows, cols].astype(F32)
-            turned = part * cos_ref[span_rows, :]
-            turned = turned + pltpu.roll(part, width // 2, 1) * sin_ref[span_rows, :]
-            kx[h, hf, 0:half_rows, :] = turned.astype(BF16)
+    @pl.loop(0, KVH // 2)
+    def _(step):
+        for h in (2 * step, 2 * step + 1):
+            cols = pl.ds(pl.multiple_of(h * width, width), width)
+            for hf in range(2):
+                span_rows = slice(hf * half_rows, (hf + 1) * half_rows)
+                part = k_raw[span_rows, cols].astype(F32)
+                turned = part * cos_ref[span_rows, :]
+                turned = turned + pltpu.roll(part, width // 2, 1) * sin_ref[span_rows, :]
+                kx[h, hf, 0:half_rows, :] = turned.astype(BF16)
 
     far_first = [side // 2]
     for step in range(side // 2 - 1, 0, -1):
         far_first += [step, side - step]
 
-    @pl.when(core == 1)
-    def _():
-        pl.semaphore_wait(barrier, 2 * (side - 1))
-        signal(told, chip(x, y, 0))
-
     @pl.when(core == 0)
     def _():
+        send_cache(0, 1)
         pl.semaphore_wait(told, 1)
+        send_cache(1, 0)
+        send_cache(0, 0)
+        pl.semaphore_wait(told_far, 1)
         for d in far_first:
             signal(side_in, chip(x + d, y, 1))
             signal(side_in, chip(x, y + d, 1))
 
-    def send_q1(net, along, device):
-        spot = 2 * (x if net == 0 else y) + core
-        remote(
-            qsrc.at[net, along % 2], q1.at[net, :, spot], q1_send, q1_recv.at[net], device
-        ).start()
-
-    for d in far_first:
-        send_q1(0, (x + d) % side, chip(x + d, y, 1))
-        send_q1(1, (y + d) % side, chip(x, y + d, 1))
-
-    @pl.when(core == 0)
-    def _():
-        send_q1(0, x, chip(x, y, 1))
-        send_q1(1, y, chip(x, y, 1))
-
-    send_cache(0, kx, kall)
-    for hf in range(2):
-        kall[2 * core + hf] = kx[my_head, hf]
-
     @pl.when(core == 1)
     def _():
-        for net, spot in ((0, 2 * x + 1), (1, 2 * y + 1)):
+        pl.semaphore_wait(near_side, 4)
+        signal(told, chip(x, y, 0))
+        send_cache(1, 0)
+        pl.semaphore_wait(barrier, 2 * (side - 1))
+        signal(told_far, chip(x, y, 0))
+        landed(qsrc.at[:, :, :, 0], q0_sem)
+        for d in far_first:
+            for net in range(2):
+                place = x if net == 0 else y
+                along = (place + d) % side
+                remote(
+                    qsrc.at[net, along % 2],
+                    q1.at[net, :, pl.ds(2 * place, 2)],
+                    q1_send,
+                    q1_recv.at[net],
+                    chip(along, y, 1) if net == 0 else chip(x, along, 1),
+                ).start()
+        send_cache(0, 1)
+        send_cache(0, 0)
+
+    @pl.when(core == 1)
+    def _():
+        for net, place in ((0, x), (1, y)):
             for b in range(2):
-                q1[net, b, spot] = qsrc[net, (x if net == 0 else y) % 2, b]
+                for pc in range(2):
+                    q1[net, b, 2 * place + pc] = qsrc[net, place % 2, b, pc]
         pl.semaphore_wait(side_in, 2 * (side - 1))
         for net in range(2):
-            landed(q1.at[net, :, pl.ds(0, toks - 1)], q1_recv.at[net])
+            landed(q1.at[net, :, pl.ds(0, toks - 2)], q1_recv.at[net])
             nu, nv = (x, y) if net == 0 else (y, x)
 
             def send_q2(pv, device, net=net, nu=nu, nv=nv):
@@ -400,6 +416,10 @@
     col_tok = (col_slot // 2) * tok_along + col_slot % 2
     one_hot = jnp.where(lax.broadcasted_iota(jnp.int32, (cols, width), 1) == 0, 1.0, 0.0).astype(BF16)
 
+    half_units = units // 2
+    half_cache = half_units * half_rows
+    always = me < 4 * side * side
+
     def attend(pvs):
         query = jnp.concatenate(
             [q2[pv].astype(F32).reshape(piece, width).astype(BF16) for pv in pvs]
@@ -408,32 +428,44 @@
         s = lax.dot_general(kspan[...], query[:, :width], contract, preferred_element_type=F32)
         live = jnp.concatenate([span_tok <= col_tok + pv * tok_across for pv in pvs], axis=1)
         s_span = jnp.where(live, s, DEAD)
+        span_scores[...] = s_span
         best = jnp.maximum(s_span[0:8], s_span[8:16])
-        for k in range(units // 2):
-            keys = kall[2 * k : 2 * k + 2, 0:half_rows, :].reshape(chunk, width)
-            keys = jnp.concatenate([keys, kbias[k * chunk : (k + 1) * chunk, :]], axis=1)
+        for p in range(2):
+            span = slice(p * half_cache, (p + 1) * half_cache)
+            keys = kall[p * half_units : (p + 1) * half_units, 0:half_rows, :]
+            keys = jnp.concatenate([keys.reshape(half_cache, width), kbias[span, :]], axis=1)
             s = lax.dot_general(keys, query, contract, preferred_element_type=F32)
-            scores[k * chunk : (k + 1) * chunk, :] = s
-            best = jnp.maximum(best, jnp.max(s.reshape(chunk // 8, 8, cols), axis=0))
-        top = jnp.maximum(jnp.max(best, axis=0, keepdims=True), FLOOR)
-        w = jnp.exp2((s_span - top) * exponent)
-        total = w[0:8] + w[8:16]
-        w = jnp.concatenate([w, jnp.zeros((width - 16, cols), F32)])
-        num = jnp.dot(vspan[...], w.astype(BF16), preferred_element_type=F32)
-        for k in range(units // 2):
-            w = jnp.exp2((scores[k * chunk : (k + 1) * chunk, :] - top) * exponent)
-            total = total + jnp.sum(w.reshape(chunk // 8, 8, cols), axis=0)
-            num = num + jnp.dot(
-                vturned[:, k * chunk : (k + 1) * chunk],
-                w.astype(BF16),
-                preferred_element_type=F32,
+            scores[span, :] = s
+            best = jnp.maximum(best, jnp.max(s.reshape(-1, 8, cols), axis=0))
+        tops[...] = jnp.maximum(jnp.max(best, axis=0, keepdims=True), FLOOR)
+
+        @pl.when(always)
+        def _():
+            top = tops[...]
+            w = jnp.exp2((span_scores[...] - top) * exponent)
+            total = w[0:8] + w[8:16]
+            w = jnp.concatenate([w, jnp.zeros((width - 16, cols), F32)])
+            nums = [jnp.dot(vspan[...], w.astype(BF16), preferred_element_type=F32), None]
+            for k in range(units // 2):
+                w = jnp.exp2((scores[k * chunk : (k + 1) * chunk, :] - top) * exponent)
+                total = total + jnp.sum(w.reshape(chunk // 8, 8, cols), axis=0)
+                part = jnp.dot(
+                    vturned[:, k * chunk : (k + 1) * chunk],
+                    w.astype(BF16),
+                    preferred_element_type=F32,
+                )
+                nums[k % 2] = part if nums[k % 2] is None else nums[k % 2] + part
+            num = nums[0] + nums[1]
+            den = jnp.sum(total, axis=0, keepdims=True)
+            stat = jnp.concatenate(
+                in_three(top) + in_three(den) + [jnp.zeros((EXTRA - 6, cols), F32)]
             )
-        den = jnp.sum(total, axis=0, keepdims=True)
-        stat = jnp.concatenate(in_three(top) + in_three(den) + [jnp.zeros((EXTRA - 6, cols), F32)])
-        for k, pv in enumerate(pvs):
-            lanes = slice(k * piece, (k + 1) * piece)
-            o1src[pv, 0:width, :] = num[:, lanes].astype(BF16)
-            o1src[pv, width : width + EXTRA, :] = stat[:, lanes].astype(BF16)
+            for k, pv in enumerate(pvs):
+                lanes = slice(k * piece, (k + 1) * piece)
+                o1src[pv, 0:width, :] = num[:, lanes].astype(BF16)
+                o1src[pv, width : width + EXTRA, :] = stat[:, lanes].astype(BF16)
+
+        for pv in pvs:
 
             @pl.when((pv != v) | (core == 0))
             def _(pv=pv):
@@ -445,7 +477,7 @@
 
     @pl.loop(0, side // 2)
     def _(k):
-        pvs = [k + 1, (k + 1 + side // 2) % side]
+        pvs = [(v + jnp.where(k == 0, 0, side // 2 - k)) % side, (v + side // 2 + k) % side]
         for pv in pvs:
 
             @pl.when((pv != v) | (core == 0))
@@ -459,12 +491,12 @@
 
     @pl.when(core == 0)
     def _():
-        sent(q1.at[0], q1_send)
+        sent(qsrc.at[:, :, :, 0], q0_sem)
         sent(o1.at[0], o1_send)
 
     @pl.when(core == 1)
     def _():
-        sent(q1.at[0, :, pl.ds(0, toks - 2)], q1_send)
+        sent(q1.at[:, :, pl.ds(0, toks - 2)], q1_send)
         sent(q2, q2_send.at[0])
         sent(q2.at[pl.ds(0, side - 1)], q2_send.at[1])
         for net in range(2):
@@ -566,7 +598,7 @@
             vm((3, 16, width), F32),
             vm((16, width), BF16),
             vm((width, width), BF16),
-            vm((2, 2, 2, GROUP, width), BF16),
+            vm((2, 2, 2, 2, GROUP, width), BF16),
             vm((2, 2, toks, GROUP, width), BF16),
             vm((side, toks, GROUP, width), BF16),
             vm((units * half, 2 * piece), F32),
@@ -578,6 +610,7 @@
             dma((2,)),
             dma((2,)),
             dma(()),
+            dma(()),
             dma((2,)),
             dma((2,)),
             dma((side,)),
@@ -587,6 +620,10 @@
             dma(()),
             pltpu.SemaphoreType.REGULAR,
             pltpu.SemaphoreType.REGULAR,
+            pltpu.SemaphoreType.REGULAR,
+            pltpu.SemaphoreType.REGULAR,
+            vm((16, 2 * piece), F32),
+            vm((1, 2 * piece), F32),
         ]
         out = pl.pallas_call(
             functools.partial(kernel, side),

time: 49.4 us -> 45.7 us (0.925)
  Pallas kernels: 47.3 us -> 43.6 us
    pallas_call x1, Pallas kernels: 47.3 us -> 43.6 us  [body(): pl.pallas_call(functools.partial(kernel, side), out_shape=pltpu.VMEM((H,...]
where the time goes in v4:
time: 45.7 us; the launch traced here: 45.6 us
  Pallas kernels  43.6 us (95%)
  between operations  1.31 us (3%)
  local copies, waits for them, and re-layouts  0.64 us (1%)
    pallas_call x1, Pallas kernels, body(): pl.pallas_call(functools.partial(kernel, side), out_shape=pltpu.VMEM((H,...  43.6 us

profile of v4, /device:TPU:513, one launch (start us, length us, event | category | flops | bytes accessed | tf_op | source)
XLA Modules:
  0.0 45.6 jit_solution(6332755363426009656)
XLA Ops:
  1.3 43.6 %paged_prefix.1 = f32[64,128]{1,0:T(8,128)S(1)} custom-call(s32[1]{0:T(128)S(6)} %copy.14.start_hbm, s32[1]{0:T(128)S(6)} %copy.13.count_hbm, s32[16]{0:T(128)} %pages_hbm.1, f32[40,128]{1,0:T(8,128)} %constant.2.clone.table_hbm, bf16[1,8192]{1,0:T(2,128)(2,1)} %q_hbm.1, bf16[1,1024]{1,0:T(2,128)(2,1)} %sk_hbm.1, bf16[1,1024]{1,0:T(2,128)(2,1)} %sv_hbm.1, ...), custom_call_target="tpu_custom_call" | custom-call | tf_op jit(solution)/shard_map/paged_prefix/pallas_call | solution.py:628
  44.9 0.6 %copy.12 = bf16[1,1,64,128]{3,1,2,0:T(2,128)(2,1)} copy(bf16[1,1,64,128]{3,2,1,0:T(8,128)(2,1)S(1)} %convert_bitcast_fusion) | data formatting | bytes 32768
  (1 shorter events, 0.0 us)

commit v5 on v4

--- a/solution.py
+++ b/solution.py
@@ -86,6 +86,8 @@
     vx,
     kall,
     vall,
+    kall0,
+    vall0,
     vturned,
     kbias,
     rows16,
@@ -94,7 +96,8 @@
     qsrc,
     q1,
     q2,
-    scores,
+    scores_a,
+    scores_b,
     o1src,
     o1,
     o2src,
@@ -102,6 +105,7 @@
     local_sem,
     kv_send,
     kv_recv,
+    on_send,
     q0_sem,
     q1_send,
     q1_recv,
@@ -113,10 +117,13 @@
     o2_recv,
     told,
     told_far,
-    near_side,
-    side_in,
-    span_scores,
-    tops,
+    side_row,
+    side_col,
+    side_col0,
+    span_a,
+    span_b,
+    top_a,
+    top_b,
 ):
     width = q_rows.shape[1]
     rows = k_hbm.shape[0]
@@ -212,52 +219,82 @@
                 turned = part * own_cos + pltpu.roll(part, width // 2, 1) * own_sin
                 qsrc[net, e, b, core] = turned.astype(BF16)
 
+    far_first = [side // 2]
+    for step in range(side // 2 - 1, 0, -1):
+        far_first += [step, side - step]
+
+    def send_q1(toks_sent, slot, sem):
+        for d in far_first:
+            for net in range(2):
+                place = x if net == 0 else y
+                along = (place + d) % side
+                remote(
+                    qsrc.at[net, along % 2, :, toks_sent],
+                    q1.at[net, :, slot(place)],
+                    sem,
+                    q1_recv.at[net],
+                    chip(along, y, 1) if net == 0 else chip(x, along, 1),
+                ).start()
+
     @pl.when(core == 0)
     def _():
         pl.semaphore_wait(barrier, 4 + 1)
         signal(told, chip(x, y, 1))
-        for dx, dy in neighbours:
-            signal(near_side, chip(x + dx, y + dy, 1))
         remote(qsrc.at[:, :, :, 0], qsrc.at[:, :, :, 0], q0_sem, q0_sem, chip(x, y, 1)).start()
 
-    @pl.when(core == 1)
-    def _():
-        pl.semaphore_wait(told, 1)
-
-    def send_cache(which, net):
-        buf, landing = (kx, kall) if which == 0 else (vx, vall)
-
-        def send(head, half, slot, device):
-            src = buf.at[head] if half is None else buf.at[head, half]
-            dst = landing.at[pl.ds(slot, 2)] if half is None else landing.at[slot]
-            remote(src, dst, kv_send.at[which], kv_recv.at[which], device).start()
-
-        nu, nv = (x, y) if net == 0 else (y, x)
-
-        def at(pu, pv):
-            return chip(pu, pv, 0) if net == 0 else chip(pv, pu, 1)
-
-        base = nu + 2 * nv
-        head = CLASSES * net + (base + 1) % CLASSES
-        send(head, None, 4 + 2 * core, at(nu + 1, nv))
-        head = CLASSES * net + (base + 3) % CLASSES
-        send(head, None, 8 + 2 * core, at(nu + side - 1, nv))
-        head = CLASSES * net + (base + 2) % CLASSES
-        send(head, 0, 12 + core, at(nu, nv + 1))
-        send(head, 1, 14 + core, at(nu, nv + side - 1))
-        head = CLASSES * net + base % CLASSES
-
-        @pl.when(core == net)
-        def _():
-            for hf in range(2):
-                landing[2 * core + hf] = buf[head, hf]
-
-        @pl.when(core != net)
-        def _():
-            send(head, None, 2 * core, at(nu, nv))
+        @pl.when(me == 0)
+        def _():
+            pl.semaphore_wait(told_far, 1)
+            send_q1(0, lambda place: 2 * place, q1_send)
+
+    def send_cache(which):
+        buf = (kx, vx)[which]
+        for net in range(2):
+            landing = ((kall0, vall0), (kall, vall))[net][which]
+
+            def send(head, half, slot, device, net=net, landing=landing):
+                src = buf.at[head] if half is None else buf.at[head, half]
+                dst = landing.at[pl.ds(slot, 2)] if half is None else landing.at[slot]
+                remote(src, dst, kv_send.at[which, net], kv_recv.at[which, net], device).start()
+
+            nu, nv = (x, y) if net == 0 else (y, x)
+
+            def at(pu, pv, net=net):
+                return chip(pu, pv, 1) if net == 0 else chip(pv, pu, 1)
+
+            base = nu + 2 * nv
+            head = CLASSES * net + (base + 1) % CLASSES
+            send(head, None, 4 + 2 * core, at(nu + 1, nv))
+            head = CLASSES * net + (base + 3) % CLASSES
+            send(head, None, 8 + 2 * core, at(nu + side - 1, nv))
+            head = CLASSES * net + (base + 2) % CLASSES
+            send(head, 0, 12 + core, at(nu, nv + 1))
+            send(head, 1, 14 + core, at(nu, nv + side - 1))
+        own = ((kall, vall)[which], (kall0, vall0)[which])
+        head0 = (x + 2 * y) % CLASSES
+        head1 = CLASSES + (y + 2 * x) % CLASSES
+
+        @pl.when(core == 0)
+        def _():
+            own[0][0:2] = buf[head0]
+            remote(
+                buf.at[head1],
+                own[0].at[pl.ds(0, 2)],
+                kv_send.at[which, 1],
+                kv_recv.at[which, 1],
+                chip(x, y, 1),
+            ).start()
+
+        @pl.when(core == 1)
+        def _():
+            own[0][2:4] = buf[head1]
+            own[1][2:4] = buf[head0]
 
     pltpu.make_async_copy(vx, vx, local_sem.at[len(local)]).wait()
-    send_cache(1, 1)
+
+    @pl.when(core == 0)
+    def _():
+        send_cache(1)
 
     tile_row = lax.broadcasted_iota(jnp.int32, (EXTRA, width), 0)
     lane = lax.broadcasted_iota(jnp.int32, (1, width), 1)
@@ -305,76 +342,163 @@
                 turned = turned + pltpu.roll(part, width // 2, 1) * sin_ref[span_rows, :]
                 kx[h, hf, 0:half_rows, :] = turned.astype(BF16)
 
-    far_first = [side // 2]
-    for step in range(side // 2 - 1, 0, -1):
-        far_first += [step, side - step]
-
     @pl.when(core == 0)
     def _():
-        send_cache(0, 1)
-        pl.semaphore_wait(told, 1)
-        send_cache(1, 0)
-        send_cache(0, 0)
-        pl.semaphore_wait(told_far, 1)
+        send_cache(0)
+        @pl.when(me > 1)
+        def _():
+            pl.semaphore_wait(told_far, 1)
+
         for d in far_first:
-            signal(side_in, chip(x + d, y, 1))
-            signal(side_in, chip(x, y + d, 1))
+            signal(side_row, chip(x + d, y, 1))
+
+        @pl.when(y == 0)
+        def _():
+            for d in far_first:
+                signal(side_col0, chip(x, y + d, 1))
+
+        @pl.when(y != 0)
+        def _():
+            for d in far_first:
+                signal(side_col, chip(x, y + d, 1))
 
     @pl.when(core == 1)
     def _():
-        pl.semaphore_wait(near_side, 4)
-        signal(told, chip(x, y, 0))
-        send_cache(1, 0)
-        pl.semaphore_wait(barrier, 2 * (side - 1))
+        @pl.when(me <= 1)
+        def _():
+            pl.semaphore_wait(barrier, 2 * (side - 1))
+            send_q1(1, lambda place: 2 * place + 1, q1_send)
+            send_cache(1)
+            send_cache(0)
+            pl.semaphore_wait(told, 1)
+
+        @pl.when(me > 1)
+        def _():
+            pl.semaphore_wait(told, 1)
+            send_cache(1)
+            pl.semaphore_wait(barrier, 2 * (side - 1))
+
         signal(told_far, chip(x, y, 0))
-        landed(qsrc.at[:, :, :, 0], q0_sem)
-        for d in far_first:
-            for net in range(2):
-                place = x if net == 0 else y
-                along = (place + d) % side
-                remote(
-                    qsrc.at[net, along % 2],
-                    q1.at[net, :, pl.ds(2 * place, 2)],
-                    q1_send,
-                    q1_recv.at[net],
-                    chip(along, y, 1) if net == 0 else chip(x, along, 1),
-                ).start()
-        send_cache(0, 1)
-        send_cache(0, 0)
+
+        @pl.when(me > 1)
+        def _():
+            landed(qsrc.at[:, :, :, 0], q0_sem)
+            send_q1(pl.ds(0, 2), lambda place: pl.ds(2 * place, 2), q1_send)
+
+        @pl.when(me > 1)
+        def _():
+            send_cache(0)
+
+    remote_units = units - 2
+    near_units = units - 4
 
     @pl.when(core == 1)
     def _():
+        @pl.when(me <= 1)
+        def _():
+            landed(qsrc.at[:, :, :, 0], q0_sem)
+
         for net, place in ((0, x), (1, y)):
             for b in range(2):
                 for pc in range(2):
                     q1[net, b, 2 * place + pc] = qsrc[net, place % 2, b, pc]
-        pl.semaphore_wait(side_in, 2 * (side - 1))
-        for net in range(2):
-            landed(q1.at[net, :, pl.ds(0, toks - 2)], q1_recv.at[net])
+        pl.semaphore_wait(side_col, jnp.where(y == 0, side - 1, side - 2))
+
+        def send_q2(net, pv):
             nu, nv = (x, y) if net == 0 else (y, x)
-
-            def send_q2(pv, device, net=net, nu=nu, nv=nv):
+            remote(
+                q1.at[net, (nu // 2 + pv) % 2],
+                q2.at[nv],
+                q2_send.at[net],
+                q2_recv.at[nv],
+                chip(x, pv, 0) if net == 0 else chip(pv, y, 1),
+            ).start()
+
+        def relay0():
+            landed(q1.at[0, :, pl.ds(0, toks - 2)], q1_recv.at[0])
+            for d in far_first:
+                pv = (y + d) % side
+
+                @pl.when(pv != 0)
+                def _(pv=pv):
+                    send_q2(0, pv)
+
+            send_q2(0, y)
+
+        def relay1():
+            landed(q1.at[1, :, pl.ds(0, toks - 2)], q1_recv.at[1])
+            for d in far_first:
+                send_q2(1, (x + d) % side)
+            q2[x] = q1[1, (y // 2 + x) % 2]
+
+        def hand_on():
+            for which, (src, dst) in ((1, (vall0, vall)), (0, (kall0, kall))):
+                landed(src.at[pl.ds(0, near_units)], kv_recv.at[which, 0])
+                span = pl.ds(2, remote_units)
                 remote(
-                    q1.at[net, (nu // 2 + pv) % 2],
-                    q2.at[nv],
-                    q2_send.at[net],
-                    q2_recv.at[nv],
-                    device,
+                    src.at[span],
+                    dst.at[span],
+                    on_send.at[which],
+                    kv_recv.at[which, 0],
+                    chip(x, y, 0),
                 ).start()
 
-            for d in far_first:
-                pv = (nv + d) % side
-                send_q2(pv, chip(x, pv, 0) if net == 0 else chip(pv, y, 1))
-            if net == 0:
-                send_q2(y, chip(x, y, 0))
-            else:
-                q2[x] = q1[1, (y // 2 + x) % 2]
-
-    landed(vall.at[pl.ds(0, units - 2)], kv_recv.at[1])
+        @pl.when(y != 0)
+        def _():
+            relay0()
+
+        @pl.when((y == 0) & (x != 0))
+        def _():
+            relay1()
+
+        line0 = jnp.where(y == 0, x, jnp.where(x == 0, y, 0))
+        far_line0 = (line0 > 1) & (line0 < side - 1)
+
+        @pl.when(far_line0)
+        def _():
+            hand_on()
+
+        def relay_top():
+            pl.semaphore_wait(side_col0, 1)
+            send_q2(0, 0)
+
+        @pl.when((x == 0) & (y != 0))
+        def _():
+            relay_top()
+
+        @pl.when((y != 0) | (x == 0))
+        def _():
+            relay1()
+
+        @pl.when(y == 0)
+        def _():
+            relay0()
+
+        @pl.when((x != 0) & (y != 0))
+        def _():
+            relay_top()
+
+        @pl.when(jnp.logical_not(far_line0))
+        def _():
+            hand_on()
+
+        landed(vall.at[pl.ds(0, remote_units)], kv_recv.at[1, 1])
+
+    @pl.when(core == 0)
+    def _():
+        landed(vall.at[pl.ds(0, remote_units)], kv_recv.at[1, 0])
+
     for unit in range(units):
         vturned[:, unit * half_rows : (unit + 1) * half_rows] = vall[unit].T
 
-    landed(kall.at[pl.ds(0, units - 2)], kv_recv.at[0])
+    @pl.when(core == 1)
+    def _():
+        landed(kall.at[pl.ds(0, remote_units)], kv_recv.at[0, 1])
+
+    @pl.when(core == 0)
+    def _():
+        landed(kall.at[pl.ds(0, remote_units)], kv_recv.at[0, 0])
+
     span_units = [0, 2, 4, 6, 8, 10, 12, 13]
     span_toks = [
         dev(pu, pv, pc)
@@ -416,11 +540,12 @@
     col_tok = (col_slot // 2) * tok_along + col_slot % 2
     one_hot = jnp.where(lax.broadcasted_iota(jnp.int32, (cols, width), 1) == 0, 1.0, 0.0).astype(BF16)
 
+    scores, span_scores, tops = (scores_a, scores_b), (span_a, span_b), (top_a, top_b)
     half_units = units // 2
     half_cache = half_units * half_rows
     always = me < 4 * side * side
 
-    def attend(pvs):
+    def score(pvs, buf):
         query = jnp.concatenate(
             [q2[pv].astype(F32).reshape(piece, width).astype(BF16) for pv in pvs]
         )
@@ -428,43 +553,55 @@
         s = lax.dot_general(kspan[...], query[:, :width], contract, preferred_element_type=F32)
         live = jnp.concatenate([span_tok <= col_tok + pv * tok_across for pv in pvs], axis=1)
         s_span = jnp.where(live, s, DEAD)
-        span_scores[...] = s_span
+        span_scores[buf][...] = s_span
         best = jnp.maximum(s_span[0:8], s_span[8:16])
         for p in range(2):
             span = slice(p * half_cache, (p + 1) * half_cache)
             keys = kall[p * half_units : (p + 1) * half_units, 0:half_rows, :]
             keys = jnp.concatenate([keys.reshape(half_cache, width), kbias[span, :]], axis=1)
             s = lax.dot_general(keys, query, contract, preferred_element_type=F32)
-            scores[span, :] = s
+            scores[buf][span, :] = s
             best = jnp.maximum(best, jnp.max(s.reshape(-1, 8, cols), axis=0))
-        tops[...] = jnp.maximum(jnp.max(best, axis=0, keepdims=True), FLOOR)
-
-        @pl.when(always)
-        def _():
-            top = tops[...]
-            w = jnp.exp2((span_scores[...] - top) * exponent)
-            total = w[0:8] + w[8:16]
-            w = jnp.concatenate([w, jnp.zeros((width - 16, cols), F32)])
-            nums = [jnp.dot(vspan[...], w.astype(BF16), preferred_element_type=F32), None]
-            for k in range(units // 2):
-                w = jnp.exp2((scores[k * chunk : (k + 1) * chunk, :] - top) * exponent)
-                total = total + jnp.sum(w.reshape(chunk // 8, 8, cols), axis=0)
-                part = jnp.dot(
-                    vturned[:, k * chunk : (k + 1) * chunk],
-                    w.astype(BF16),
-                    preferred_element_type=F32,
-                )
-                nums[k % 2] = part if nums[k % 2] is None else nums[k % 2] + part
-            num = nums[0] + nums[1]
-            den = jnp.sum(total, axis=0, keepdims=True)
-            stat = jnp.concatenate(
-                in_three(top) + in_three(den) + [jnp.zeros((EXTRA - 6, cols), F32)]
+        tops[buf][...] = jnp.maximum(jnp.max(best, axis=0, keepdims=True), FLOOR)
+
+    def weigh(pvs, buf):
+        top = tops[buf][...]
+        w = jnp.exp2((span_scores[buf][...] - top) * exponent)
+        total = w[0:8] + w[8:16]
+        w = jnp.concatenate([w, jnp.zeros((width - 16, cols), F32)])
+        nums = [jnp.dot(vspan[...], w.astype(BF16), preferred_element_type=F32), None]
+        for k in range(units // 2):
+            w = jnp.exp2((scores[buf][k * chunk : (k + 1) * chunk, :] - top) * exponent)
+            total = total + jnp.sum(w.reshape(chunk // 8, 8, cols), axis=0)
+            part = jnp.dot(
+                vturned[:, k * chunk : (k + 1) * chunk],
+                w.astype(BF16),
+                preferred_element_type=F32,
             )
-            for k, pv in enumerate(pvs):
-                lanes = slice(k * piece, (k + 1) * piece)
-                o1src[pv, 0:width, :] = num[:, lanes].astype(BF16)
-                o1src[pv, width : width + EXTRA, :] = stat[:, lanes].astype(BF16)
-
+            nums[k % 2] = part if nums[k % 2] is None else nums[k % 2] + part
+        num = nums[0] + nums[1]
+        den = jnp.sum(total, axis=0, keepdims=True)
+        stat = jnp.concatenate(in_three(top) + in_three(den) + [jnp.zeros((EXTRA - 6, cols), F32)])
+        for k, pv in enumerate(pvs):
+            lanes = slice(k * piece, (k + 1) * piece)
+            o1src[pv, 0:width, :] = num[:, lanes].astype(BF16)
+            o1src[pv, width : width + EXTRA, :] = stat[:, lanes].astype(BF16)
+
+    def pair(k):
+        last = (v + side - 1) % side
+        near = (v + jnp.where(k == 0, 0, side // 2 - k)) % side
+        far = (v + side // 2 + k) % side
+        near, far = [jnp.where(p == 0, last, p) for p in (near, far)]
+        return [near, jnp.where(k == side // 2 - 1, 0, far)]
+
+    def queries_in(pvs):
+        for pv in pvs:
+
+            @pl.when((pv != v) | (core == 0))
+            def _(pv=pv):
+                landed(q2.at[pv], q2_recv.at[pv])
+
+    def results_out(pvs):
         for pv in pvs:
 
             @pl.when((pv != v) | (core == 0))
@@ -475,30 +612,72 @@
             def _(pv=pv):
                 o1[1, pv] = o1src[pv]
 
-    @pl.loop(0, side // 2)
-    def _(k):
-        pvs = [(v + jnp.where(k == 0, 0, side // 2 - k)) % side, (v + side // 2 + k) % side]
-        for pv in pvs:
-
-            @pl.when((pv != v) | (core == 0))
-            def _(pv=pv):
-                landed(q2.at[pv], q2_recv.at[pv])
-
-        attend(pvs)
-
-    sent(vall.at[pl.ds(0, units - 2)], kv_send.at[1])
-    sent(kall.at[pl.ds(0, units - 2)], kv_send.at[0])
+    pairs = side // 2
+    queries_in(pair(0))
+    score(pair(0), 0)
+
+    for k in range(pairs - 2):
+        queries_in(pair(k + 1))
+
+        @pl.when(always)
+        def _(k=k):
+            score(pair(k + 1), (k + 1) % 2)
+            weigh(pair(k), k % 2)
+
+        results_out(pair(k))
+
+    @pl.when(always)
+    def _():
+        weigh(pair(pairs - 2), pairs % 2)
+
+    results_out(pair(pairs - 2))
+    queries_in(pair(pairs - 1))
+
+    @pl.when(always)
+    def _():
+        score(pair(pairs - 1), (pairs - 1) % 2)
+
+    @pl.when(always)
+    def _():
+        weigh(pair(pairs - 1), (pairs - 1) % 2)
+
+    results_out(pair(pairs - 1))
+
+    for which, buf in enumerate((kall, vall)):
+        sent(buf.at[pl.ds(0, near_units // 2)], kv_send.at[which, 0])
+
+        @pl.when(core == 0)
+        def _(which=which, buf=buf):
+            sent(buf.at[pl.ds(0, near_units // 2 + 2)], kv_send.at[which, 1])
+
+        @pl.when(core == 1)
+        def _(which=which, buf=buf):
+            sent(buf.at[pl.ds(0, near_units // 2)], kv_send.at[which, 1])
+            sent(buf.at[pl.ds(0, remote_units)], on_send.at[which])
 
     @pl.when(core == 0)
     def _():
         sent(qsrc.at[:, :, :, 0], q0_sem)
+
+        @pl.when(me == 0)
+        def _():
+            sent(q1.at[:, :, pl.ds(0, side - 1)], q1_send)
+
         sent(o1.at[0], o1_send)
 
     @pl.when(core == 1)
     def _():
-        sent(q1.at[:, :, pl.ds(0, toks - 2)], q1_send)
+        @pl.when(me <= 1)
+        def _():
+            sent(q1.at[:, :, pl.ds(0, side - 1)], q1_send)
+
+        @pl.when(me > 1)
+        def _():
+            sent(q1.at[:, :, pl.ds(0, toks - 2)], q1_send)
+
         sent(q2, q2_send.at[0])
         sent(q2.at[pl.ds(0, side - 1)], q2_send.at[1])
+        pl.semaphore_wait(side_row, side - 1)
         for net in range(2):
             landed(o1.at[net] if net == 0 else o1.at[net, pl.ds(0, side - 1)], o1_recv.at[net])
             nu = x if net == 0 else y
@@ -593,6 +772,8 @@
             vm((KVH, 2, half, width), BF16),
             vm((units, half + EXTRA, width), BF16),
             vm((units, half, width), BF16),
+            vm((units, half + EXTRA, width), BF16),
+            vm((units, half, width), BF16),
             vm((width, units * half), BF16),
             vm((units * half, width), BF16),
             vm((3, 16, width), F32),
@@ -602,12 +783,14 @@
             vm((2, 2, toks, GROUP, width), BF16),
             vm((side, toks, GROUP, width), BF16),
             vm((units * half, 2 * piece), F32),
+            vm((units * half, 2 * piece), F32),
             vm((side, width + EXTRA, piece), BF16),
             vm((2, side, width + EXTRA, piece), BF16),
             vm((2, toks, 3, GROUP, width), BF16),
             vm((toks, 3, GROUP, width), BF16),
             dma((9,)),
-            dma((2,)),
+            dma((2, 2)),
+            dma((2, 2)),
             dma((2,)),
             dma(()),
             dma(()),
@@ -622,7 +805,10 @@
             pltpu.SemaphoreType.REGULAR,
             pltpu.SemaphoreType.REGULAR,
             pltpu.SemaphoreType.REGULAR,
+            pltpu.SemaphoreType.REGULAR,
             vm((16, 2 * piece), F32),
+            vm((16, 2 * piece), F32),
+            vm((1, 2 * piece), F32),
             vm((1, 2 * piece), F32),
         ]
         out = pl.pallas_call(

time: 45.7 us -> 44.6 us (0.976)
  Pallas kernels: 43.6 us -> 42.5 us
    pallas_call x1, Pallas kernels: 43.6 us -> 42.5 us  [body(): pl.pallas_call(functools.partial(kernel, side), out_shape=pltpu.VMEM((H,...]
where the time goes in v5:
time: 44.6 us; the launch traced here: 44.5 us
  Pallas kernels  42.5 us (95%)
  between operations  1.31 us (3%)
  local copies, waits for them, and re-layouts  0.64 us (1%)
    pallas_call x1, Pallas kernels, body(): pl.pallas_call(functools.partial(kernel, side), out_shape=pltpu.VMEM((H,...  42.5 us

profile of v5, /device:TPU:513, one launch (start us, length us, event | category | flops | bytes accessed | tf_op | source)
XLA Modules:
  0.0 44.5 jit_solution(15358233771523644285)
XLA Ops:
  1.3 42.5 %paged_prefix.1 = f32[64,128]{1,0:T(8,128)S(1)} custom-call(s32[1]{0:T(128)S(6)} %copy.14.start_hbm, s32[1]{0:T(128)S(6)} %copy.13.count_hbm, s32[16]{0:T(128)} %pages_hbm.1, f32[40,128]{1,0:T(8,128)} %constant.2.clone.table_hbm, bf16[1,8192]{1,0:T(2,128)(2,1)} %q_hbm.1, bf16[1,1024]{1,0:T(2,128)(2,1)} %sk_hbm.1, bf16[1,1024]{1,0:T(2,128)(2,1)} %sv_hbm.1, ...), custom_call_target="tpu_custom_call" | custom-call | tf_op jit(solution)/shard_map/paged_prefix/pallas_call | solution.py:814
  43.9 0.6 %copy.12 = bf16[1,1,64,128]{3,1,2,0:T(2,128)(2,1)} copy(bf16[1,1,64,128]{3,2,1,0:T(8,128)(2,1)S(1)} %convert_bitcast_fusion) | data formatting | bytes 32768
  (1 shorter events, 0.0 us)

commit v6 on v5

--- a/solution.py
+++ b/solution.py
@@ -102,6 +102,11 @@
     o1,
     o2src,
     o2,
+    qlate,
+    q2l,
+    late_src,
+    o1l,
+    o2l,
     local_sem,
     kv_send,
     kv_recv,
@@ -115,6 +120,11 @@
     o1_recv,
     o2_send,
     o2_recv,
+    ql_recv,
+    q2l_send,
+    q2l_recv,
+    o1l_send,
+    o1l_recv,
     told,
     told_far,
     side_row,
@@ -223,16 +233,16 @@
     for step in range(side // 2 - 1, 0, -1):
         far_first += [step, side - step]
 
-    def send_q1(toks_sent, slot, sem):
+    def send_q1(toks_sent, landing, recv):
         for d in far_first:
             for net in range(2):
                 place = x if net == 0 else y
                 along = (place + d) % side
                 remote(
                     qsrc.at[net, along % 2, :, toks_sent],
-                    q1.at[net, :, slot(place)],
-                    sem,
-                    q1_recv.at[net],
+                    landing(net, place),
+                    q1_send,
+                    recv.at[net],
                     chip(along, y, 1) if net == 0 else chip(x, along, 1),
                 ).start()
 
@@ -242,10 +252,6 @@
         signal(told, chip(x, y, 1))
         remote(qsrc.at[:, :, :, 0], qsrc.at[:, :, :, 0], q0_sem, q0_sem, chip(x, y, 1)).start()
 
-        @pl.when(me == 0)
-        def _():
-            pl.semaphore_wait(told_far, 1)
-            send_q1(0, lambda place: 2 * place, q1_send)
 
     def send_cache(which):
         buf = (kx, vx)[which]
@@ -345,10 +351,7 @@
     @pl.when(core == 0)
     def _():
         send_cache(0)
-        @pl.when(me > 1)
-        def _():
-            pl.semaphore_wait(told_far, 1)
-
+        pl.semaphore_wait(told_far, 1)
         for d in far_first:
             signal(side_row, chip(x + d, y, 1))
 
@@ -364,29 +367,27 @@
 
     @pl.when(core == 1)
     def _():
-        @pl.when(me <= 1)
+        @pl.when(me == 1)
         def _():
             pl.semaphore_wait(barrier, 2 * (side - 1))
-            send_q1(1, lambda place: 2 * place + 1, q1_send)
+            send_q1(1, lambda net, place: q1.at[net, :, 2 * place + 1], q1_recv)
             send_cache(1)
             send_cache(0)
             pl.semaphore_wait(told, 1)
+            signal(told_far, chip(x, y, 0))
+            landed(qsrc.at[:, :, :, 0], q0_sem)
+            send_q1(0, lambda net, place: qlate.at[net], ql_recv)
+            qlate[0] = qsrc[0, 0, :, 0]
+            qlate[1] = qsrc[1, 0, :, 0]
 
         @pl.when(me > 1)
         def _():
             pl.semaphore_wait(told, 1)
             send_cache(1)
             pl.semaphore_wait(barrier, 2 * (side - 1))
-
-        signal(told_far, chip(x, y, 0))
-
-        @pl.when(me > 1)
-        def _():
+            signal(told_far, chip(x, y, 0))
             landed(qsrc.at[:, :, :, 0], q0_sem)
-            send_q1(pl.ds(0, 2), lambda place: pl.ds(2 * place, 2), q1_send)
-
-        @pl.when(me > 1)
-        def _():
+            send_q1(pl.ds(0, 2), lambda net, place: q1.at[net, :, pl.ds(2 * place, 2)], q1_recv)
             send_cache(0)
 
     remote_units = units - 2
@@ -394,14 +395,23 @@
 
     @pl.when(core == 1)
     def _():
-        @pl.when(me <= 1)
-        def _():
-            landed(qsrc.at[:, :, :, 0], q0_sem)
-
         for net, place in ((0, x), (1, y)):
             for b in range(2):
-                for pc in range(2):
-                    q1[net, b, 2 * place + pc] = qsrc[net, place % 2, b, pc]
+                q1[net, b, 2 * place + 1] = qsrc[net, place % 2, b, 1]
+
+        @pl.when(me > 1)
+        def _():
+            for net, place in ((0, x), (1, y)):
+                for b in range(2):
+                    q1[net, b, 2 * place] = qsrc[net, place % 2, b, 0]
+
+        for net, across in ((0, y), (1, x)):
+
+            @pl.when(across == 0)
+            def _(net=net):
+                for b in range(2):
+                    q1[net, b, 0] = jnp.zeros((GROUP, width), BF16)
+
         pl.semaphore_wait(side_col, jnp.where(y == 0, side - 1, side - 2))
 
         def send_q2(net, pv):
@@ -414,22 +424,30 @@
                 chip(x, pv, 0) if net == 0 else chip(pv, y, 1),
             ).start()
 
-        def relay0():
-            landed(q1.at[0, :, pl.ds(0, toks - 2)], q1_recv.at[0])
-            for d in far_first:
-                pv = (y + d) % side
-
-                @pl.when(pv != 0)
-                def _(pv=pv):
-                    send_q2(0, pv)
-
-            send_q2(0, y)
-
-        def relay1():
-            landed(q1.at[1, :, pl.ds(0, toks - 2)], q1_recv.at[1])
-            for d in far_first:
-                send_q2(1, (x + d) % side)
-            q2[x] = q1[1, (y // 2 + x) % 2]
+        def all_in(net, along, across):
+            short = (across == 0) & (along != 0)
+
+            @pl.when(short)
+            def _():
+                landed(q1.at[net, :, pl.ds(0, toks - 3)], q1_recv.at[net])
+
+            @pl.when(jnp.logical_not(short))
+            def _():
+                landed(q1.at[net, :, pl.ds(0, toks - 2)], q1_recv.at[net])
+
+        all_in(0, x, y)
+        for d in far_first:
+            pv = (y + d) % side
+
+            @pl.when(pv != 0)
+            def _(pv=pv):
+                send_q2(0, pv)
+
+        send_q2(0, y)
+        all_in(1, y, x)
+        for d in far_first:
+            send_q2(1, (x + d) % side)
+        q2[x] = q1[1, (y // 2 + x) % 2]
 
         def hand_on():
             for which, (src, dst) in ((1, (vall0, vall)), (0, (kall0, kall))):
@@ -443,42 +461,42 @@
                     chip(x, y, 0),
                 ).start()
 
+        line0 = jnp.where(y == 0, x, jnp.where(x == 0, y, 0))
+        by_chip0 = (line0 == 1) | (line0 == side - 1)
+
+        @pl.when(jnp.logical_not(by_chip0))
+        def _():
+            hand_on()
+
         @pl.when(y != 0)
         def _():
-            relay0()
-
-        @pl.when((y == 0) & (x != 0))
-        def _():
-            relay1()
-
-        line0 = jnp.where(y == 0, x, jnp.where(x == 0, y, 0))
-        far_line0 = (line0 > 1) & (line0 < side - 1)
-
-        @pl.when(far_line0)
-        def _():
-            hand_on()
-
-        def relay_top():
             pl.semaphore_wait(side_col0, 1)
             send_q2(0, 0)
 
-        @pl.when((x == 0) & (y != 0))
-        def _():
-            relay_top()
-
-        @pl.when((y != 0) | (x == 0))
-        def _():
-            relay1()
-
         @pl.when(y == 0)
         def _():
-            relay0()
-
-        @pl.when((x != 0) & (y != 0))
-        def _():
-            relay_top()
-
-        @pl.when(jnp.logical_not(far_line0))
+            @pl.when(x != 0)
+            def _():
+                landed(qlate.at[0], ql_recv.at[0])
+
+            for d in far_first + [0]:
+                remote(
+                    qlate.at[0, (x // 2 + d) % 2], q2l, q2l_send, q2l_recv, chip(x, d, 0)
+                ).start()
+
+        @pl.when(x == 0)
+        def _():
+            @pl.when(y != 0)
+            def _():
+                landed(qlate.at[1], ql_recv.at[1])
+
+            for d in far_first:
+                remote(
+                    qlate.at[1, (y // 2 + d) % 2], q2l, q2l_send, q2l_recv, chip(d, y, 1)
+                ).start()
+            q2l[...] = qlate[1, (y // 2) % 2]
+
+        @pl.when(by_chip0)
         def _():
             hand_on()
 
@@ -545,54 +563,60 @@
     half_cache = half_units * half_rows
     always = me < 4 * side * side
 
-    def score(pvs, buf):
-        query = jnp.concatenate(
-            [q2[pv].astype(F32).reshape(piece, width).astype(BF16) for pv in pvs]
-        )
-        query = jnp.concatenate([query, one_hot], axis=1)
+    def score(query, live, buf):
+        n = query.shape[0]
+        query = jnp.concatenate([query, one_hot[:n]], axis=1)
         s = lax.dot_general(kspan[...], query[:, :width], contract, preferred_element_type=F32)
-        live = jnp.concatenate([span_tok <= col_tok + pv * tok_across for pv in pvs], axis=1)
         s_span = jnp.where(live, s, DEAD)
-        span_scores[buf][...] = s_span
+        span_scores[buf][:, :n] = s_span
         best = jnp.maximum(s_span[0:8], s_span[8:16])
         for p in range(2):
             span = slice(p * half_cache, (p + 1) * half_cache)
             keys = kall[p * half_units : (p + 1) * half_units, 0:half_rows, :]
             keys = jnp.concatenate([keys.reshape(half_cache, width), kbias[span, :]], axis=1)
             s = lax.dot_general(keys, query, contract, preferred_element_type=F32)
-            scores[buf][span, :] = s
-            best = jnp.maximum(best, jnp.max(s.reshape(-1, 8, cols), axis=0))
-        tops[buf][...] = jnp.maximum(jnp.max(best, axis=0, keepdims=True), FLOOR)
-
-    def weigh(pvs, buf):
-        top = tops[buf][...]
-        w = jnp.exp2((span_scores[buf][...] - top) * exponent)
+            scores[buf][span, :n] = s
+            best = jnp.maximum(best, jnp.max(s.reshape(-1, 8, n), axis=0))
+        tops[buf][:, :n] = jnp.maximum(jnp.max(best, axis=0, keepdims=True), FLOOR)
+
+    def weigh(buf, n):
+        top = tops[buf][:, :n]
+        w = jnp.exp2((span_scores[buf][:, :n] - top) * exponent)
         total = w[0:8] + w[8:16]
-        w = jnp.concatenate([w, jnp.zeros((width - 16, cols), F32)])
+        w = jnp.concatenate([w, jnp.zeros((width - 16, n), F32)])
         nums = [jnp.dot(vspan[...], w.astype(BF16), preferred_element_type=F32), None]
         for k in range(units // 2):
-            w = jnp.exp2((scores[buf][k * chunk : (k + 1) * chunk, :] - top) * exponent)
-            total = total + jnp.sum(w.reshape(chunk // 8, 8, cols), axis=0)
+            w = jnp.exp2((scores[buf][k * chunk : (k + 1) * chunk, :n] - top) * exponent)
+            total = total + jnp.sum(w.reshape(chunk // 8, 8, n), axis=0)
             part = jnp.dot(
                 vturned[:, k * chunk : (k + 1) * chunk],
                 w.astype(BF16),
                 preferred_element_type=F32,
             )
             nums[k % 2] = part if nums[k % 2] is None else nums[k % 2] + part
-        num = nums[0] + nums[1]
         den = jnp.sum(total, axis=0, keepdims=True)
-        stat = jnp.concatenate(in_three(top) + in_three(den) + [jnp.zeros((EXTRA - 6, cols), F32)])
+        stat = jnp.concatenate(in_three(top) + in_three(den) + [jnp.zeros((EXTRA - 6, n), F32)])
+        return nums[0] + nums[1], stat
+
+    def score_pair(pvs, buf):
+        query = jnp.concatenate(
+            [q2[pv].astype(F32).reshape(piece, width).astype(BF16) for pv in pvs]
+        )
+        live = jnp.concatenate([span_tok <= col_tok + pv * tok_across for pv in pvs], axis=1)
+        score(query, live, buf)
+
+    def weigh_pair(pvs, buf):
+        num, stat = weigh(buf, cols)
         for k, pv in enumerate(pvs):
             lanes = slice(k * piece, (k + 1) * piece)
             o1src[pv, 0:width, :] = num[:, lanes].astype(BF16)
             o1src[pv, width : width + EXTRA, :] = stat[:, lanes].astype(BF16)
 
     def pair(k):
-        last = (v + side - 1) % side
-        near = (v + jnp.where(k == 0, 0, side // 2 - k)) % side
-        far = (v + side // 2 + k) % side
-        near, far = [jnp.where(p == 0, last, p) for p in (near, far)]
-        return [near, jnp.where(k == side // 2 - 1, 0, far)]
+        return [
+            (v + jnp.where(k == 0, 0, side // 2 - k)) % side,
+            (v + side // 2 + k) % side,
+        ]
 
     def queries_in(pvs):
         for pv in pvs:
@@ -614,34 +638,51 @@
 
     pairs = side // 2
     queries_in(pair(0))
-    score(pair(0), 0)
-
-    for k in range(pairs - 2):
+    score_pair(pair(0), 0)
+
+    for k in range(pairs - 1):
         queries_in(pair(k + 1))
 
         @pl.when(always)
         def _(k=k):
-            score(pair(k + 1), (k + 1) % 2)
-            weigh(pair(k), k % 2)
+            score_pair(pair(k + 1), (k + 1) % 2)
+            weigh_pair(pair(k), k % 2)
 
         results_out(pair(k))
 
     @pl.when(always)
     def _():
-        weigh(pair(pairs - 2), pairs % 2)
-
-    results_out(pair(pairs - 2))
-    queries_in(pair(pairs - 1))
+        weigh_pair(pair(pairs - 1), (pairs - 1) % 2)
+
+    results_out(pair(pairs - 1))
+
+    @pl.when((core == 0) | (x != 0))
+    def _():
+        landed(q2l, q2l_recv)
 
     @pl.when(always)
     def _():
-        score(pair(pairs - 1), (pairs - 1) % 2)
+        query = jnp.concatenate([q2l[...].astype(F32), jnp.zeros((piece - GROUP, width), F32)])
+        score(query.astype(BF16), span_tok <= 0, 0)
 
     @pl.when(always)
     def _():
-        weigh(pair(pairs - 1), (pairs - 1) % 2)
-
-    results_out(pair(pairs - 1))
+        num, stat = weigh(0, piece)
+        late_src[0] = num.T[0:GROUP].astype(BF16)
+        wide = jnp.concatenate([stat, jnp.zeros((width - EXTRA, piece), F32)])
+        late_src[1] = wide.T[0:GROUP].astype(BF16)
+
+    @pl.when(core == 0)
+    def _():
+        remote(late_src, o1l.at[0, y], o1l_send, o1l_recv.at[0], chip(x, 0, 1)).start()
+
+    @pl.when((core == 1) & (x != 0))
+    def _():
+        remote(late_src, o1l.at[1, x], o1l_send, o1l_recv.at[1], chip(0, y, 1)).start()
+
+    @pl.when((core == 1) & (x == 0))
+    def _():
+        o1l[1, 0] = late_src[...]
 
     for which, buf in enumerate((kall, vall)):
         sent(buf.at[pl.ds(0, near_units // 2)], kv_send.at[which, 0])
@@ -655,21 +696,30 @@
             sent(buf.at[pl.ds(0, near_units // 2)], kv_send.at[which, 1])
             sent(buf.at[pl.ds(0, remote_units)], on_send.at[which])
 
+    @pl.when((core == 0) | (x != 0))
+    def _():
+        sent(late_src, o1l_send)
+
     @pl.when(core == 0)
     def _():
         sent(qsrc.at[:, :, :, 0], q0_sem)
 
-        @pl.when(me == 0)
-        def _():
-            sent(q1.at[:, :, pl.ds(0, side - 1)], q1_send)
-
         sent(o1.at[0], o1_send)
 
     @pl.when(core == 1)
     def _():
-        @pl.when(me <= 1)
-        def _():
-            sent(q1.at[:, :, pl.ds(0, side - 1)], q1_send)
+        @pl.when(me == 1)
+        def _():
+            sent(q1.at[:, :, pl.ds(0, toks - 2)], q1_send)
+            sent(q2.at[0, pl.ds(0, toks - 1)], q2l_send)
+
+        @pl.when((me != 1) & (y == 0))
+        def _():
+            sent(q2.at[0, pl.ds(0, side)], q2l_send)
+
+        @pl.when((me != 1) & (x == 0))
+        def _():
+            sent(q2.at[0, pl.ds(0, side - 1)], q2l_send)
 
         @pl.when(me > 1)
         def _():
@@ -678,9 +728,26 @@
         sent(q2, q2_send.at[0])
         sent(q2.at[pl.ds(0, side - 1)], q2_send.at[1])
         pl.semaphore_wait(side_row, side - 1)
-        for net in range(2):
-            landed(o1.at[net] if net == 0 else o1.at[net, pl.ds(0, side - 1)], o1_recv.at[net])
-            nu = x if net == 0 else y
+        for step in range(2):
+            net = jnp.where(y == 0, step, 1 - step)
+            nu = jnp.where(net == 0, x, y)
+            across = jnp.where(net == 0, y, x)
+            line = net * side + nu
+
+            def owner(along, pc, net=net):
+                return chip(jnp.where(net == 0, along, x), jnp.where(net == 0, y, along), pc)
+
+            def send_o2(src, device, line=line):
+                remote(src, o2.at[line], o2_send, o2_recv, device).start()
+
+            @pl.when(net == 0)
+            def _():
+                landed(o1.at[0], o1_recv.at[0])
+
+            @pl.when(net == 1)
+            def _():
+                landed(o1.at[1, pl.ds(0, side - 1)], o1_recv.at[1])
+
             stats = []
             for b in range(2):
                 vs = [(nu // 2 + b) % 2 + 2 * k for k in range(side // 2)]
@@ -697,21 +764,59 @@
                 o2src[net, :, b] = total.T.reshape(toks, GROUP, width).astype(BF16)
             stat = jnp.concatenate(stats + [jnp.zeros((width - len(stats), piece), F32)]).T
             o2src[net, :, 2] = stat.reshape(toks, GROUP, width).astype(BF16)
-            line = x if net == 0 else side + y
-
-            def send_o2(slot, device, net=net, line=line):
-                remote(o2src.at[net, slot], o2.at[line], o2_send, o2_recv, device).start()
-
-            for d in far_first:
-                for pc in range(2):
-                    if net == 0:
-                        px = (x + d) % side
-                        send_o2(2 * px + pc, chip(px, y, pc))
-                    else:
-                        py = (y + d) % side
-                        send_o2(2 * py + pc, chip(x, py, pc))
-            send_o2(2 * nu, chip(x, y, 0))
+            for d in far_first + [0]:
+                along = (nu + d) % side
+
+                @pl.when((along != 0) | (across != 0))
+                def _(along=along):
+                    send_o2(o2src.at[net, 2 * along], owner(along, 0))
+
+                if d:
+                    send_o2(o2src.at[net, 2 * along + 1], owner(along, 1))
             o2[line] = o2src[net, 2 * nu + 1]
+
+            def late_parts(net):
+                nu = jnp.where(net == 0, x, y)
+
+                @pl.when(net == 0)
+                def _():
+                    landed(o1l.at[0], o1l_recv.at[0])
+
+                @pl.when(net == 1)
+                def _():
+                    landed(o1l.at[1, pl.ds(0, side - 1)], o1l_recv.at[1])
+
+                stat = jnp.zeros((GROUP, width), F32)
+                for b in range(2):
+                    vs = [(nu // 2 + b) % 2 + 2 * k for k in range(side // 2)]
+                    tops, dens = [], []
+                    for pv in vs:
+                        tile = o1l[net, pv, 1].astype(F32)
+                        tile = tile + pltpu.roll(tile, width - 1, 1) + pltpu.roll(tile, width - 2, 1)
+                        tops.append(jnp.broadcast_to(tile[:, 0:1], (GROUP, width)))
+                        dens.append(jnp.broadcast_to(tile[:, 3:4], (GROUP, width)))
+                    top = functools.reduce(jnp.maximum, tops)
+                    ws = [jnp.exp2((t - top) * exponent) for t in tops]
+                    den = sum(w * d for w, d in zip(ws, dens))
+                    num = sum(w * o1l[net, pv, 0].astype(F32) for w, pv in zip(ws, vs))
+                    o2l[net, b] = num.astype(BF16)
+                    for k, value in enumerate(in_three(top) + in_three(den)):
+                        stat = jnp.where(lane == 6 * b + k, value, stat)
+                o2l[net, 2] = stat.astype(BF16)
+                remote(
+                    o2l.at[net], o2.at[net * side + nu], o2_send, o2_recv, chip(0, 0, 0)
+                ).start()
+
+            @pl.when((across == 0) & (me != 1))
+            def _(net=net):
+                late_parts(net)
+
+        @pl.when(me == 1)
+        def _():
+            @pl.loop(0, 2)
+            def _(net):
+                late_parts(net)
+
         sent(o1.at[0, pl.ds(0, side - 1)], o1_send)
         landed(o2.at[pl.ds(0, toks - 2)], o2_recv)
         sent(o2src.at[:, pl.ds(0, toks - 1)], o2_send)
@@ -788,6 +893,11 @@
             vm((2, side, width + EXTRA, piece), BF16),
             vm((2, toks, 3, GROUP, width), BF16),
             vm((toks, 3, GROUP, width), BF16),
+            vm((2, 2, GROUP, width), BF16),
+            vm((GROUP, width), BF16),
+            vm((2, GROUP, width), BF16),
+            vm((2, side, 2, GROUP, width), BF16),
+            vm((2, 3, GROUP, width), BF16),
             dma((9,)),
             dma((2, 2)),
             dma((2, 2)),
@@ -801,6 +911,11 @@
             dma((2,)),
             dma(()),
             dma(()),
+            dma((2,)),
+            dma(()),
+            dma(()),
+            dma(()),
+            dma((2,)),
             pltpu.SemaphoreType.REGULAR,
             pltpu.SemaphoreType.REGULAR,
             pltpu.SemaphoreType.REGULAR,

time: 44.6 us -> 41.8 us (0.937)
  Pallas kernels: 42.5 us -> 39.7 us
    pallas_call x1, Pallas kernels: 42.5 us -> 39.7 us  [body(): pl.pallas_call(functools.partial(kernel, side), out_shape=pltpu.VMEM((H,...]
where the time goes in v6:
time: 41.8 us; the launch traced here: 41.7 us
  Pallas kernels  39.7 us (95%)
  between operations  1.31 us (3%)
  local copies, waits for them, and re-layouts  0.64 us (2%)
    pallas_call x1, Pallas kernels, body(): pl.pallas_call(functools.partial(kernel, side), out_shape=pltpu.VMEM((H,...  39.7 us

profile of v6, /device:TPU:513, one launch (start us, length us, event | category | flops | bytes accessed | tf_op | source)
XLA Modules:
  0.0 41.7 jit_solution(1436811689960515850)
XLA Ops:
  1.3 39.7 %paged_prefix.1 = f32[64,128]{1,0:T(8,128)S(1)} custom-call(s32[1]{0:T(128)S(6)} %copy.14.start_hbm, s32[1]{0:T(128)S(6)} %copy.13.count_hbm, s32[16]{0:T(128)} %pages_hbm.1, f32[40,128]{1,0:T(8,128)} %constant.2.clone.table_hbm, bf16[1,8192]{1,0:T(2,128)(2,1)} %q_hbm.1, bf16[1,1024]{1,0:T(2,128)(2,1)} %sk_hbm.1, bf16[1,1024]{1,0:T(2,128)(2,1)} %sv_hbm.1, ...), custom_call_target="tpu_custom_call" | custom-call | tf_op jit(solution)/shard_map/paged_prefix/pallas_call | solution.py:929
  41.1 0.6 %copy.12 = bf16[1,1,64,128]{3,1,2,0:T(2,128)(2,1)} copy(bf16[1,1,64,128]{3,2,1,0:T(8,128)(2,1)S(1)} %convert_bitcast_fusion) | data formatting | bytes 32768
  (1 shorter events, 0.0 us)

commit v7 on v6

--- a/solution.py
+++ b/solution.py
@@ -104,6 +104,7 @@
     o2,
     qlate,
     q2l,
+    q2x,
     late_src,
     o1l,
     o2l,
@@ -123,13 +124,14 @@
     ql_recv,
     q2l_send,
     q2l_recv,
+    q2x_send,
+    q2x_recv,
     o1l_send,
     o1l_recv,
     told,
     told_far,
     side_row,
     side_col,
-    side_col0,
     span_a,
     span_b,
     top_a,
@@ -202,6 +204,12 @@
         pl.semaphore_signal(sem, inc=1, device_id={"seq": device}, device_id_type=MESH)
 
     neighbours = ((1, 0), (side - 1, 0), (0, 1), (0, side - 1))
+    line0 = jnp.where(y == 0, x, jnp.where(x == 0, y, 0))
+    by_chip0 = (line0 == 1) | (line0 == side - 1)
+
+    @pl.when((core == 0) & by_chip0)
+    def _():
+        signal(barrier, chip(0, 0, 0))
 
     @pl.when(core == 1)
     def _():
@@ -248,25 +256,24 @@
 
     @pl.when(core == 0)
     def _():
-        pl.semaphore_wait(barrier, 4 + 1)
+        pl.semaphore_wait(barrier, jnp.where(me == 0, 4 + 4 + 1, 4 + 1))
         signal(told, chip(x, y, 1))
         remote(qsrc.at[:, :, :, 0], qsrc.at[:, :, :, 0], q0_sem, q0_sem, chip(x, y, 1)).start()
 
 
     def send_cache(which):
         buf = (kx, vx)[which]
-        for net in range(2):
-            landing = ((kall0, vall0), (kall, vall))[net][which]
-
-            def send(head, half, slot, device, net=net, landing=landing):
+
+        def send_all(net, landing, target):
+            def send(head, half, slot, device):
                 src = buf.at[head] if half is None else buf.at[head, half]
                 dst = landing.at[pl.ds(slot, 2)] if half is None else landing.at[slot]
                 remote(src, dst, kv_send.at[which, net], kv_recv.at[which, net], device).start()
 
             nu, nv = (x, y) if net == 0 else (y, x)
 
-            def at(pu, pv, net=net):
-                return chip(pu, pv, 1) if net == 0 else chip(pv, pu, 1)
+            def at(pu, pv):
+                return chip(pu, pv, target) if net == 0 else chip(pv, pu, target)
 
             base = nu + 2 * nv
             head = CLASSES * net + (base + 1) % CLASSES
@@ -276,6 +283,16 @@
             head = CLASSES * net + (base + 2) % CLASSES
             send(head, 0, 12 + core, at(nu, nv + 1))
             send(head, 1, 14 + core, at(nu, nv + side - 1))
+
+        @pl.when(me != 0)
+        def _():
+            send_all(0, (kall0, vall0)[which], 1)
+
+        @pl.when(me == 0)
+        def _():
+            send_all(0, (kall, vall)[which], 0)
+
+        send_all(1, (kall, vall)[which], 1)
         own = ((kall, vall)[which], (kall0, vall0)[which])
         head0 = (x + 2 * y) % CLASSES
         head1 = CLASSES + (y + 2 * x) % CLASSES
@@ -352,17 +369,11 @@
     def _():
         send_cache(0)
         pl.semaphore_wait(told_far, 1)
-        for d in far_first:
-            signal(side_row, chip(x + d, y, 1))
-
-        @pl.when(y == 0)
+
+        @pl.when(me != 0)
         def _():
             for d in far_first:
-                signal(side_col0, chip(x, y + d, 1))
-
-        @pl.when(y != 0)
-        def _():
-            for d in far_first:
+                signal(side_row, chip(x + d, y, 1))
                 signal(side_col, chip(x, y + d, 1))
 
     @pl.when(core == 1)
@@ -412,7 +423,7 @@
                 for b in range(2):
                     q1[net, b, 0] = jnp.zeros((GROUP, width), BF16)
 
-        pl.semaphore_wait(side_col, jnp.where(y == 0, side - 1, side - 2))
+        pl.semaphore_wait(side_col, jnp.where((x == 0) & (y != 0), side - 2, side - 1))
 
         def send_q2(net, pv):
             nu, nv = (x, y) if net == 0 else (y, x)
@@ -439,39 +450,54 @@
         for d in far_first:
             pv = (y + d) % side
 
-            @pl.when(pv != 0)
+            @pl.when((x != 0) | (pv != 0))
             def _(pv=pv):
                 send_q2(0, pv)
 
-        send_q2(0, y)
+            @pl.when((x == 0) & (pv == 0))
+            def _():
+                remote(q1.at[0, 0], q2x.at[y], q2_send.at[0], q2x_recv, chip(0, 0, 1)).start()
+
+        @pl.when(me != 1)
+        def _():
+            send_q2(0, y)
+
+        @pl.when(me == 1)
+        def _():
+            q2x[0] = q1[0, 0]
+
         all_in(1, y, x)
         for d in far_first:
             send_q2(1, (x + d) % side)
         q2[x] = q1[1, (y // 2 + x) % 2]
 
         def hand_on():
+            cases = [(jnp.logical_not(by_chip0), near_units, ((2, units),))]
+            for here, slots in (
+                ((y == 0) & (x == 1), (4, 6)),
+                ((y == 0) & (x == side - 1), (8, 10)),
+                ((x == 0) & (y == 1), (12, 13)),
+                ((x == 0) & (y == side - 1), (14, 15)),
+            ):
+                spans = ((2, slots[0]), (slots[1], units))
+                cases.append((here, near_units - slots[1] + slots[0], spans))
             for which, (src, dst) in ((1, (vall0, vall)), (0, (kall0, kall))):
-                landed(src.at[pl.ds(0, near_units)], kv_recv.at[which, 0])
-                span = pl.ds(2, remote_units)
-                remote(
-                    src.at[span],
-                    dst.at[span],
-                    on_send.at[which],
-                    kv_recv.at[which, 0],
-                    chip(x, y, 0),
-                ).start()
-
-        line0 = jnp.where(y == 0, x, jnp.where(x == 0, y, 0))
-        by_chip0 = (line0 == 1) | (line0 == side - 1)
-
-        @pl.when(jnp.logical_not(by_chip0))
-        def _():
-            hand_on()
-
-        @pl.when(y != 0)
-        def _():
-            pl.semaphore_wait(side_col0, 1)
-            send_q2(0, 0)
+                for here, amount, spans in cases:
+
+                    @pl.when(here)
+                    def _(which=which, src=src, dst=dst, amount=amount, spans=spans):
+                        landed(src.at[pl.ds(0, amount)], kv_recv.at[which, 0])
+                        for first, end in spans:
+                            span = pl.ds(first, end - first)
+                            remote(
+                                src.at[span],
+                                dst.at[span],
+                                on_send.at[which],
+                                kv_recv.at[which, 0],
+                                chip(x, y, 0),
+                            ).start()
+
+        hand_on()
 
         @pl.when(y == 0)
         def _():
@@ -495,10 +521,6 @@
                     qlate.at[1, (y // 2 + d) % 2], q2l, q2l_send, q2l_recv, chip(d, y, 1)
                 ).start()
             q2l[...] = qlate[1, (y // 2) % 2]
-
-        @pl.when(by_chip0)
-        def _():
-            hand_on()
 
         landed(vall.at[pl.ds(0, remote_units)], kv_recv.at[1, 1])
 
@@ -613,15 +635,15 @@
             o1src[pv, width : width + EXTRA, :] = stat[:, lanes].astype(BF16)
 
     def pair(k):
-        return [
-            (v + jnp.where(k == 0, 0, side // 2 - k)) % side,
-            (v + side // 2 + k) % side,
-        ]
+        late = (me <= 1) | by_chip0
+        near = (v + jnp.where(k == 0, 0, side // 2 - k)) % side
+        far = (v + side // 2 + k) % side
+        return [jnp.where(late, (side - k) % side, near), jnp.where(late, k + 1, far)]
 
     def queries_in(pvs):
         for pv in pvs:
 
-            @pl.when((pv != v) | (core == 0))
+            @pl.when(((pv != v) | (core == 0)) & (me != 0))
             def _(pv=pv):
                 landed(q2.at[pv], q2_recv.at[pv])
 
@@ -637,6 +659,10 @@
                 o1[1, pv] = o1src[pv]
 
     pairs = side // 2
+    @pl.when(me == 0)
+    def _():
+        landed(q2, q2_recv.at[0])
+
     queries_in(pair(0))
     score_pair(pair(0), 0)
 
@@ -649,6 +675,12 @@
             weigh_pair(pair(k), k % 2)
 
         results_out(pair(k))
+        if k == 0:
+
+            @pl.when(me == 1)
+            def _():
+                landed(q2x.at[pl.ds(0, side - 1)], q2x_recv)
+                remote(q2x, q2, q2x_send, q2_recv.at[0], chip(0, 0, 0)).start()
 
     @pl.when(always)
     def _():
@@ -672,17 +704,40 @@
         wide = jnp.concatenate([stat, jnp.zeros((width - EXTRA, piece), F32)])
         late_src[1] = wide.T[0:GROUP].astype(BF16)
 
-    @pl.when(core == 0)
-    def _():
-        remote(late_src, o1l.at[0, y], o1l_send, o1l_recv.at[0], chip(x, 0, 1)).start()
-
-    @pl.when((core == 1) & (x != 0))
-    def _():
-        remote(late_src, o1l.at[1, x], o1l_send, o1l_recv.at[1], chip(0, y, 1)).start()
-
-    @pl.when((core == 1) & (x == 0))
-    def _():
-        o1l[1, 0] = late_src[...]
+    late_slot = jnp.where(core == 0, y, x)
+    late_to = jnp.where(
+        core == 0,
+        jnp.where(x == 0, 0, chip(x, 0, 1)),
+        jnp.where(y == 0, 0, chip(0, y, 1)),
+    )
+    late_stays = (me == 0) | ((core == 1) & (x == 0) & (y != 0))
+
+    @pl.when(jnp.logical_not(late_stays))
+    def _():
+        remote(late_src, o1l.at[core, late_slot], o1l_send, o1l_recv.at[core], late_to).start()
+
+    @pl.when(late_stays)
+    def _():
+        o1l[core, late_slot] = late_src[...]
+
+    def merge_late(net, nu, out):
+        stat = jnp.zeros((GROUP, width), F32)
+        for b in range(2):
+            vs = [(nu // 2 + b) % 2 + 2 * k for k in range(side // 2)]
+            tops, dens = [], []
+            for pv in vs:
+                tile = o1l[net, pv, 1].astype(F32)
+                tile = tile + pltpu.roll(tile, width - 1, 1) + pltpu.roll(tile, width - 2, 1)
+                tops.append(jnp.broadcast_to(tile[:, 0:1], (GROUP, width)))
+                dens.append(jnp.broadcast_to(tile[:, 3:4], (GROUP, width)))
+            top = functools.reduce(jnp.maximum, tops)
+            ws = [jnp.exp2((t - top) * exponent) for t in tops]
+            den = sum(w * d for w, d in zip(ws, dens))
+            num = sum(w * o1l[net, pv, 0].astype(F32) for w, pv in zip(ws, vs))
+            out[b] = num.astype(BF16)
+            for k, value in enumerate(in_three(top) + in_three(den)):
+                stat = jnp.where(lane == 6 * b + k, value, stat)
+        out[2] = stat.astype(BF16)
 
     for which, buf in enumerate((kall, vall)):
         sent(buf.at[pl.ds(0, near_units // 2)], kv_send.at[which, 0])
@@ -694,9 +749,18 @@
         @pl.when(core == 1)
         def _(which=which, buf=buf):
             sent(buf.at[pl.ds(0, near_units // 2)], kv_send.at[which, 1])
-            sent(buf.at[pl.ds(0, remote_units)], on_send.at[which])
-
-    @pl.when((core == 0) | (x != 0))
+            for here, amount in (
+                (line0 * by_chip0 == 0, remote_units),
+                ((y == 0) & by_chip0, remote_units - 2),
+                ((x == 0) & by_chip0, remote_units - 1),
+            ):
+
+                @pl.when(here)
+                def _(which=which, buf=buf, amount=amount):
+                    sent(buf.at[pl.ds(0, amount)], on_send.at[which])
+
+
+    @pl.when(jnp.logical_not(late_stays))
     def _():
         sent(late_src, o1l_send)
 
@@ -725,11 +789,19 @@
         def _():
             sent(q1.at[:, :, pl.ds(0, toks - 2)], q1_send)
 
-        sent(q2, q2_send.at[0])
+        @pl.when(me == 1)
+        def _():
+            sent(q2.at[pl.ds(0, side - 1)], q2_send.at[0])
+            sent(q2x, q2x_send)
+
+        @pl.when(me != 1)
+        def _():
+            sent(q2, q2_send.at[0])
+
         sent(q2.at[pl.ds(0, side - 1)], q2_send.at[1])
-        pl.semaphore_wait(side_row, side - 1)
+        pl.semaphore_wait(side_row, jnp.where((y == 0) & (x != 0), side - 2, side - 1))
         for step in range(2):
-            net = jnp.where(y == 0, step, 1 - step)
+            net = jnp.where(jnp.minimum(y, side - y) <= jnp.minimum(x, side - x), step, 1 - step)
             nu = jnp.where(net == 0, x, y)
             across = jnp.where(net == 0, y, x)
             line = net * side + nu
@@ -775,9 +847,8 @@
                     send_o2(o2src.at[net, 2 * along + 1], owner(along, 1))
             o2[line] = o2src[net, 2 * nu + 1]
 
-            def late_parts(net):
-                nu = jnp.where(net == 0, x, y)
-
+            @pl.when((across == 0) & (me != 1))
+            def _(net=net, nu=nu, line=line):
                 @pl.when(net == 0)
                 def _():
                     landed(o1l.at[0], o1l_recv.at[0])
@@ -786,44 +857,25 @@
                 def _():
                     landed(o1l.at[1, pl.ds(0, side - 1)], o1l_recv.at[1])
 
-                stat = jnp.zeros((GROUP, width), F32)
-                for b in range(2):
-                    vs = [(nu // 2 + b) % 2 + 2 * k for k in range(side // 2)]
-                    tops, dens = [], []
-                    for pv in vs:
-                        tile = o1l[net, pv, 1].astype(F32)
-                        tile = tile + pltpu.roll(tile, width - 1, 1) + pltpu.roll(tile, width - 2, 1)
-                        tops.append(jnp.broadcast_to(tile[:, 0:1], (GROUP, width)))
-                        dens.append(jnp.broadcast_to(tile[:, 3:4], (GROUP, width)))
-                    top = functools.reduce(jnp.maximum, tops)
-                    ws = [jnp.exp2((t - top) * exponent) for t in tops]
-                    den = sum(w * d for w, d in zip(ws, dens))
-                    num = sum(w * o1l[net, pv, 0].astype(F32) for w, pv in zip(ws, vs))
-                    o2l[net, b] = num.astype(BF16)
-                    for k, value in enumerate(in_three(top) + in_three(den)):
-                        stat = jnp.where(lane == 6 * b + k, value, stat)
-                o2l[net, 2] = stat.astype(BF16)
-                remote(
-                    o2l.at[net], o2.at[net * side + nu], o2_send, o2_recv, chip(0, 0, 0)
-                ).start()
-
-            @pl.when((across == 0) & (me != 1))
-            def _(net=net):
-                late_parts(net)
-
-        @pl.when(me == 1)
-        def _():
-            @pl.loop(0, 2)
-            def _(net):
-                late_parts(net)
+                merge_late(net, nu, o2l)
+                send_o2(o2l, 0)
 
         sent(o1.at[0, pl.ds(0, side - 1)], o1_send)
         landed(o2.at[pl.ds(0, toks - 2)], o2_recv)
-        sent(o2src.at[:, pl.ds(0, toks - 1)], o2_send)
 
     @pl.when(core == 0)
     def _():
-        landed(o2, o2_recv)
+        @pl.when(me != 0)
+        def _():
+            landed(o2, o2_recv)
+
+        @pl.when(me == 0)
+        def _():
+            landed(o1l.at[0, pl.ds(0, side - 1)], o1l_recv.at[0])
+            landed(o1l.at[1], o1l_recv.at[1])
+            merge_late(0, 0, o2.at[0])
+            merge_late(1, 0, o2.at[side])
+            landed(o2.at[pl.ds(0, toks - 2)], o2_recv)
 
     tops, dens = [[], []], [[], []]
     for src in range(toks):
@@ -842,6 +894,14 @@
                 num = sum(w * o2[s, b].astype(F32) for w, s in zip(ws, srcs))
                 head = CLASSES * net + e + 2 * b
                 out_ref[head * GROUP : (head + 1) * GROUP, :] = num / den
+
+    @pl.when(me == 1)
+    def _():
+        sent(o2src.at[:, pl.ds(0, toks - 2)], o2_send)
+
+    @pl.when((core == 1) & (me != 1))
+    def _():
+        sent(o2src.at[:, pl.ds(0, toks - 1)], o2_send)
 
 
 def solution(mesh):
@@ -895,9 +955,10 @@
             vm((toks, 3, GROUP, width), BF16),
             vm((2, 2, GROUP, width), BF16),
             vm((GROUP, width), BF16),
+            vm((side, toks, GROUP, width), BF16),
             vm((2, GROUP, width), BF16),
             vm((2, side, 2, GROUP, width), BF16),
-            vm((2, 3, GROUP, width), BF16),
+            vm((3, GROUP, width), BF16),
             dma((9,)),
             dma((2, 2)),
             dma((2, 2)),
@@ -915,8 +976,9 @@
             dma(()),
             dma(()),
             dma(()),
+            dma(()),
+            dma(()),
             dma((2,)),
-            pltpu.SemaphoreType.REGULAR,
             pltpu.SemaphoreType.REGULAR,
             pltpu.SemaphoreType.REGULAR,
             pltpu.SemaphoreType.REGULAR,

time: 41.8 us -> 40.8 us (0.976)
  Pallas kernels: 39.7 us -> 38.6 us
    pallas_call x1, Pallas kernels: 39.7 us -> 38.6 us  [body(): pl.pallas_call(functools.partial(kernel, side), out_shape=pltpu.VMEM((H,...]
where the time goes in v7:
time: 40.8 us; the launch traced here: 40.6 us
  Pallas kernels  38.6 us (95%)
  between operations  1.31 us (3%)
  local copies, waits for them, and re-layouts  0.64 us (2%)
    pallas_call x1, Pallas kernels, body(): pl.pallas_call(functools.partial(kernel, side), out_shape=pltpu.VMEM((H,...  38.6 us

profile of v7, /device:TPU:513, one launch (start us, length us, event | category | flops | bytes accessed | tf_op | source)
XLA Modules:
  0.0 40.6 jit_solution(13246716292583751457)
XLA Ops:
  1.3 38.6 %paged_prefix.1 = f32[64,128]{1,0:T(8,128)S(1)} custom-call(s32[1]{0:T(128)S(6)} %copy.14.start_hbm, s32[1]{0:T(128)S(6)} %copy.13.count_hbm, s32[16]{0:T(128)} %pages_hbm.1, f32[40,128]{1,0:T(8,128)} %constant.2.clone.table_hbm, bf16[1,8192]{1,0:T(2,128)(2,1)} %q_hbm.1, bf16[1,1024]{1,0:T(2,128)(2,1)} %sk_hbm.1, bf16[1,1024]{1,0:T(2,128)(2,1)} %sv_hbm.1, ...), custom_call_target="tpu_custom_call" | custom-call | tf_op jit(solution)/shard_map/paged_prefix/pallas_call | solution.py:991
  39.9 0.6 %copy.12 = bf16[1,1,64,128]{3,1,2,0:T(2,128)(2,1)} copy(bf16[1,1,64,128]{3,2,1,0:T(8,128)(2,1)S(1)} %convert_bitcast_fusion) | data formatting | bytes 32768
  (1 shorter events, 0.0 us)

commit v8 on v7

--- a/solution.py
+++ b/solution.py
@@ -20,7 +20,7 @@
 MESH = pl.DeviceIdType.MESH
 F32 = jnp.float32
 BF16 = jnp.bfloat16
-EXTRA = 16
+EXTRA = 8
 
 
 def rope_table(width, rows):
@@ -61,8 +61,8 @@
 
 def kernel(
     side,
-    start_hbm,
-    count_hbm,
+    start_ref,
+    count_ref,
     pages_hbm,
     table_hbm,
     q_hbm,
@@ -71,8 +71,6 @@
     k_hbm,
     v_hbm,
     out_ref,
-    start_ref,
-    count_ref,
     pages_ref,
     table_ref,
     q_raw,
@@ -104,7 +102,6 @@
     o2,
     qlate,
     q2l,
-    q2x,
     late_src,
     o1l,
     o2l,
@@ -124,8 +121,6 @@
     ql_recv,
     q2l_send,
     q2l_recv,
-    q2x_send,
-    q2x_recv,
     o1l_send,
     o1l_recv,
     told,
@@ -177,8 +172,6 @@
         name: pltpu.make_async_copy(src, dst, local_sem.at[k])
         for k, (name, src, dst) in enumerate(
             (
-                ("start", start_hbm, start_ref),
-                ("count", count_hbm, count_ref),
                 ("pages", pages_hbm, pages_ref),
                 ("table", table_hbm, table_ref),
                 ("q", q_hbm, q_raw),
@@ -220,7 +213,7 @@
             signal(barrier, chip(x + d, y, 1))
             signal(barrier, chip(x, y + d, 1))
 
-    for name in ("start", "count", "pages", "table", "q"):
+    for name in ("pages", "table", "q"):
         local[name].wait()
     start = start_ref[0]
     count = count_ref[0]
@@ -320,6 +313,7 @@
         send_cache(1)
 
     tile_row = lax.broadcasted_iota(jnp.int32, (EXTRA, width), 0)
+    row16 = lax.broadcasted_iota(jnp.int32, (16, width), 0)
     lane = lax.broadcasted_iota(jnp.int32, (1, width), 1)
     half_pages = half_rows // PAGE
     biases = []
@@ -332,7 +326,7 @@
         biases.append(jnp.where(usable, 0.0, DEAD).astype(F32))
     page_pos = jnp.zeros((16, width), jnp.int32)
     for j in range(rows // PAGE):
-        page_pos = jnp.where(tile_row == j, pages_ref[j] * PAGE, page_pos)
+        page_pos = jnp.where(row16 == j, pages_ref[j] * PAGE, page_pos)
     page_cos, page_sin = cos_sin(page_pos.astype(F32), table_ref)
     row_cos = table_ref[8 : 8 + PAGE, :]
     row_sin = table_ref[8 + PAGE : 8 + 2 * PAGE, :]
@@ -454,18 +448,7 @@
             def _(pv=pv):
                 send_q2(0, pv)
 
-            @pl.when((x == 0) & (pv == 0))
-            def _():
-                remote(q1.at[0, 0], q2x.at[y], q2_send.at[0], q2x_recv, chip(0, 0, 1)).start()
-
-        @pl.when(me != 1)
-        def _():
-            send_q2(0, y)
-
-        @pl.when(me == 1)
-        def _():
-            q2x[0] = q1[0, 0]
-
+        send_q2(0, y)
         all_in(1, y, x)
         for d in far_first:
             send_q2(1, (x + d) % side)
@@ -515,6 +498,7 @@
             @pl.when(y != 0)
             def _():
                 landed(qlate.at[1], ql_recv.at[1])
+                send_q2(0, 0)
 
             for d in far_first:
                 remote(
@@ -562,7 +546,7 @@
     vspan[...] = jnp.concatenate([rows16[2], zeros]).T.astype(BF16)
     span_tok = jnp.full((16, piece), 1 << 20, jnp.int32)
     for k, tok in enumerate(span_toks):
-        span_tok = jnp.where(tile_row == k, tok, span_tok)
+        span_tok = jnp.where(row16 == k, tok, span_tok)
 
     exponent = width**-0.5 / math.log(2.0)
     contract = (((1,), (1,)), ((), ()))
@@ -635,15 +619,17 @@
             o1src[pv, width : width + EXTRA, :] = stat[:, lanes].astype(BF16)
 
     def pair(k):
-        late = (me <= 1) | by_chip0
-        near = (v + jnp.where(k == 0, 0, side // 2 - k)) % side
-        far = (v + side // 2 + k) % side
-        return [jnp.where(late, (side - k) % side, near), jnp.where(late, k + 1, far)]
+        late, away, half = (me <= 1) | by_chip0, jnp.where(v < side // 2, -1, 1), side // 2
+        a, b = [(0, 1), (half, half - 1), (1 - half, half - 2), (2 - half, -1)][k]
+        return [
+            jnp.where(late, (side - k) % side, (v + away * a + side) % side),
+            jnp.where(late, k + 1, (v + away * b + side) % side),
+        ]
 
     def queries_in(pvs):
         for pv in pvs:
 
-            @pl.when(((pv != v) | (core == 0)) & (me != 0))
+            @pl.when((pv != v) | (core == 0))
             def _(pv=pv):
                 landed(q2.at[pv], q2_recv.at[pv])
 
@@ -659,10 +645,6 @@
                 o1[1, pv] = o1src[pv]
 
     pairs = side // 2
-    @pl.when(me == 0)
-    def _():
-        landed(q2, q2_recv.at[0])
-
     queries_in(pair(0))
     score_pair(pair(0), 0)
 
@@ -675,31 +657,22 @@
             weigh_pair(pair(k), k % 2)
 
         results_out(pair(k))
-        if k == 0:
-
-            @pl.when(me == 1)
-            def _():
-                landed(q2x.at[pl.ds(0, side - 1)], q2x_recv)
-                remote(q2x, q2, q2x_send, q2_recv.at[0], chip(0, 0, 0)).start()
+
+    @pl.when((core == 0) | (x != 0))
+    def _():
+        landed(q2l, q2l_recv)
 
     @pl.when(always)
     def _():
+        query = jnp.concatenate([q2l[...].astype(F32), jnp.zeros((piece - GROUP, width), F32)])
+        score(query.astype(BF16), span_tok <= 0, pairs % 2)
         weigh_pair(pair(pairs - 1), (pairs - 1) % 2)
 
     results_out(pair(pairs - 1))
 
-    @pl.when((core == 0) | (x != 0))
-    def _():
-        landed(q2l, q2l_recv)
-
     @pl.when(always)
     def _():
-        query = jnp.concatenate([q2l[...].astype(F32), jnp.zeros((piece - GROUP, width), F32)])
-        score(query.astype(BF16), span_tok <= 0, 0)
-
-    @pl.when(always)
-    def _():
-        num, stat = weigh(0, piece)
+        num, stat = weigh(pairs % 2, piece)
         late_src[0] = num.T[0:GROUP].astype(BF16)
         wide = jnp.concatenate([stat, jnp.zeros((width - EXTRA, piece), F32)])
         late_src[1] = wide.T[0:GROUP].astype(BF16)
@@ -739,66 +712,40 @@
                 stat = jnp.where(lane == 6 * b + k, value, stat)
         out[2] = stat.astype(BF16)
 
-    for which, buf in enumerate((kall, vall)):
-        sent(buf.at[pl.ds(0, near_units // 2)], kv_send.at[which, 0])
-
-        @pl.when(core == 0)
-        def _(which=which, buf=buf):
-            sent(buf.at[pl.ds(0, near_units // 2 + 2)], kv_send.at[which, 1])
-
-        @pl.when(core == 1)
-        def _(which=which, buf=buf):
-            sent(buf.at[pl.ds(0, near_units // 2)], kv_send.at[which, 1])
-            for here, amount in (
-                (line0 * by_chip0 == 0, remote_units),
-                ((y == 0) & by_chip0, remote_units - 2),
-                ((x == 0) & by_chip0, remote_units - 1),
-            ):
-
-                @pl.when(here)
-                def _(which=which, buf=buf, amount=amount):
-                    sent(buf.at[pl.ds(0, amount)], on_send.at[which])
-
-
-    @pl.when(jnp.logical_not(late_stays))
-    def _():
-        sent(late_src, o1l_send)
+    def cache_gone():
+        for which, buf in enumerate((kall, vall)):
+            sent(buf.at[pl.ds(0, near_units // 2)], kv_send.at[which, 0])
+
+            @pl.when(core == 0)
+            def _(which=which, buf=buf):
+                sent(buf.at[pl.ds(0, near_units // 2 + 2)], kv_send.at[which, 1])
+
+            @pl.when(core == 1)
+            def _(which=which, buf=buf):
+                sent(buf.at[pl.ds(0, near_units // 2)], kv_send.at[which, 1])
+                for here, amount in (
+                    (line0 * by_chip0 == 0, remote_units),
+                    ((y == 0) & by_chip0, remote_units - 2),
+                    ((x == 0) & by_chip0, remote_units - 1),
+                ):
+
+                    @pl.when(here)
+                    def _(which=which, buf=buf, amount=amount):
+                        sent(buf.at[pl.ds(0, amount)], on_send.at[which])
+
+        @pl.when(jnp.logical_not(late_stays))
+        def _():
+            sent(late_src, o1l_send)
 
     @pl.when(core == 0)
     def _():
+        cache_gone()
+
         sent(qsrc.at[:, :, :, 0], q0_sem)
-
         sent(o1.at[0], o1_send)
 
     @pl.when(core == 1)
     def _():
-        @pl.when(me == 1)
-        def _():
-            sent(q1.at[:, :, pl.ds(0, toks - 2)], q1_send)
-            sent(q2.at[0, pl.ds(0, toks - 1)], q2l_send)
-
-        @pl.when((me != 1) & (y == 0))
-        def _():
-            sent(q2.at[0, pl.ds(0, side)], q2l_send)
-
-        @pl.when((me != 1) & (x == 0))
-        def _():
-            sent(q2.at[0, pl.ds(0, side - 1)], q2l_send)
-
-        @pl.when(me > 1)
-        def _():
-            sent(q1.at[:, :, pl.ds(0, toks - 2)], q1_send)
-
-        @pl.when(me == 1)
-        def _():
-            sent(q2.at[pl.ds(0, side - 1)], q2_send.at[0])
-            sent(q2x, q2x_send)
-
-        @pl.when(me != 1)
-        def _():
-            sent(q2, q2_send.at[0])
-
-        sent(q2.at[pl.ds(0, side - 1)], q2_send.at[1])
         pl.semaphore_wait(side_row, jnp.where((y == 0) & (x != 0), side - 2, side - 1))
         for step in range(2):
             net = jnp.where(jnp.minimum(y, side - y) <= jnp.minimum(x, side - x), step, 1 - step)
@@ -848,7 +795,7 @@
             o2[line] = o2src[net, 2 * nu + 1]
 
             @pl.when((across == 0) & (me != 1))
-            def _(net=net, nu=nu, line=line):
+            def _(net=net, nu=nu):
                 @pl.when(net == 0)
                 def _():
                     landed(o1l.at[0], o1l_recv.at[0])
@@ -858,8 +805,29 @@
                     landed(o1l.at[1, pl.ds(0, side - 1)], o1l_recv.at[1])
 
                 merge_late(net, nu, o2l)
-                send_o2(o2l, 0)
-
+                send_o2(o2l, owner(0, 0))
+
+        cache_gone()
+
+        @pl.when(me == 1)
+        def _():
+            sent(q1.at[:, :, pl.ds(0, toks - 2)], q1_send)
+            sent(q2.at[0, pl.ds(0, toks - 1)], q2l_send)
+
+        @pl.when((me != 1) & (y == 0))
+        def _():
+            sent(q2.at[0, pl.ds(0, side)], q2l_send)
+
+        @pl.when((me != 1) & (x == 0))
+        def _():
+            sent(q2.at[0, pl.ds(0, side - 1)], q2l_send)
+
+        @pl.when(me > 1)
+        def _():
+            sent(q1.at[:, :, pl.ds(0, toks - 2)], q1_send)
+
+        sent(q2, q2_send.at[0])
+        sent(q2.at[pl.ds(0, side - 1)], q2_send.at[1])
         sent(o1.at[0, pl.ds(0, side - 1)], o1_send)
         landed(o2.at[pl.ds(0, toks - 2)], o2_recv)
 
@@ -921,9 +889,9 @@
         vm = pltpu.VMEM
         dma = pltpu.SemaphoreType.DMA
         hbm = pl.BlockSpec(memory_space=pl.ANY)
+        smem = pl.BlockSpec(memory_space=pltpu.SMEM)
+        vmem = pl.BlockSpec(memory_space=pltpu.VMEM)
         scratch = [
-            pltpu.SMEM(span_start.shape, jnp.int32),
-            pltpu.SMEM(page_counts.shape, jnp.int32),
             pltpu.SMEM(page_table.shape, jnp.int32),
             vm(table.shape, F32),
             vm((1, H * width), BF16),
@@ -955,11 +923,10 @@
             vm((toks, 3, GROUP, width), BF16),
             vm((2, 2, GROUP, width), BF16),
             vm((GROUP, width), BF16),
-            vm((side, toks, GROUP, width), BF16),
             vm((2, GROUP, width), BF16),
             vm((2, side, 2, GROUP, width), BF16),
             vm((3, GROUP, width), BF16),
-            dma((9,)),
+            dma((7,)),
             dma((2, 2)),
             dma((2, 2)),
             dma((2,)),
@@ -976,8 +943,6 @@
             dma(()),
             dma(()),
             dma(()),
-            dma(()),
-            dma(()),
             dma((2,)),
             pltpu.SemaphoreType.REGULAR,
             pltpu.SemaphoreType.REGULAR,
@@ -991,7 +956,7 @@
         out = pl.pallas_call(
             functools.partial(kernel, side),
             out_shape=pltpu.VMEM((H, width), F32),
-            in_specs=[hbm] * 9,
+            in_specs=[smem] * 2 + [hbm] * 7,
             out_specs=pl.BlockSpec(memory_space=pltpu.VMEM),
             scratch_shapes=scratch,
             compiler_params=pltpu.CompilerParams(collective_id=0, has_side_effects=True),

time: 40.8 us -> 40.1 us (0.983)
  Pallas kernels: 38.6 us -> 37.6 us
    pallas_call x1, Pallas kernels: 38.6 us -> 37.6 us  [body(): pl.pallas_call(functools.partial(kernel, side), out_shape=pltpu.VMEM((H,...]
where the time goes in v8:
time: 40.1 us; the launch traced here: 39.5 us
  Pallas kernels  37.6 us (94%)
  between operations  1.31 us (3%)
  local copies, waits for them, and re-layouts  0.64 us (2%)
    pallas_call x1, Pallas kernels, body(): pl.pallas_call(functools.partial(kernel, side), out_shape=pltpu.VMEM((H,...  37.6 us

profile of v8, /device:TPU:513, one launch (start us, length us, event | category | flops | bytes accessed | tf_op | source)
XLA Modules:
  0.0 39.5 jit_solution(6880181568174924670)
XLA Ops:
  1.3 37.6 %paged_prefix.1 = f32[64,128]{1,0:T(8,128)S(1)} custom-call(s32[1]{0:T(128)S(6)} %copy.14.start_ref, s32[1]{0:T(128)S(6)} %copy.13.count_ref, s32[16]{0:T(128)} %pages_hbm.1, f32[40,128]{1,0:T(8,128)} %constant.2.clone.table_hbm, bf16[1,8192]{1,0:T(2,128)(2,1)} %q_hbm.1, bf16[1,1024]{1,0:T(2,128)(2,1)} %sk_hbm.1, bf16[1,1024]{1,0:T(2,128)(2,1)} %sv_hbm.1, ...), custom_call_target="tpu_custom_call" | custom-call | tf_op jit(solution)/shard_map/paged_prefix/pallas_call | solution.py:956
  38.9 0.6 %copy.12 = bf16[1,1,64,128]{3,1,2,0:T(2,128)(2,1)} copy(bf16[1,1,64,128]{3,2,1,0:T(8,128)(2,1)S(1)} %convert_bitcast_fusion) | data formatting | bytes 32768
  (1 shorter events, 0.0 us)

commit v9 on v8

--- a/solution.py
+++ b/solution.py
@@ -104,6 +104,7 @@
     q2l,
     late_src,
     o1l,
+    o1d,
     o2l,
     local_sem,
     kv_send,
@@ -123,6 +124,7 @@
     q2l_recv,
     o1l_send,
     o1l_recv,
+    o1d_recv,
     told,
     told_far,
     side_row,
@@ -620,7 +622,7 @@
 
     def pair(k):
         late, away, half = (me <= 1) | by_chip0, jnp.where(v < side // 2, -1, 1), side // 2
-        a, b = [(0, 1), (half, half - 1), (1 - half, half - 2), (2 - half, -1)][k]
+        a, b = [(0, 1), (4, 3), (-3, 2), (-2, -1)][k]
         return [
             jnp.where(late, (side - k) % side, (v + away * a + side) % side),
             jnp.where(late, k + 1, (v + away * b + side) % side),
@@ -677,15 +679,27 @@
         wide = jnp.concatenate([stat, jnp.zeros((width - EXTRA, piece), F32)])
         late_src[1] = wide.T[0:GROUP].astype(BF16)
 
+    far_lines = range(3, side - 2)
+
+    def is_far(n):
+        return (n >= far_lines[0]) & (n <= far_lines[-1])
+
     late_slot = jnp.where(core == 0, y, x)
+    late_line = jnp.where(core == 0, x, y)
+    late_far = is_far(late_line)
     late_to = jnp.where(
         core == 0,
         jnp.where(x == 0, 0, chip(x, 0, 1)),
         jnp.where(y == 0, 0, chip(0, y, 1)),
     )
-    late_stays = (me == 0) | ((core == 1) & (x == 0) & (y != 0))
-
-    @pl.when(jnp.logical_not(late_stays))
+    late_stays = (me == 0) | ((core == 1) & (x == 0) & (y != 0) & jnp.logical_not(late_far))
+
+    @pl.when(late_far)
+    def _():
+        place = o1d.at[core, jnp.clip(late_line - far_lines[0], 0, len(far_lines) - 1), late_slot]
+        remote(late_src, place, o1l_send, o1d_recv, chip(0, 0, 0)).start()
+
+    @pl.when(jnp.logical_not(late_stays | late_far))
     def _():
         remote(late_src, o1l.at[core, late_slot], o1l_send, o1l_recv.at[core], late_to).start()
 
@@ -693,20 +707,20 @@
     def _():
         o1l[core, late_slot] = late_src[...]
 
-    def merge_late(net, nu, out):
+    def merge_late(parts, nu, out):
         stat = jnp.zeros((GROUP, width), F32)
         for b in range(2):
             vs = [(nu // 2 + b) % 2 + 2 * k for k in range(side // 2)]
             tops, dens = [], []
             for pv in vs:
-                tile = o1l[net, pv, 1].astype(F32)
+                tile = parts[pv, 1].astype(F32)
                 tile = tile + pltpu.roll(tile, width - 1, 1) + pltpu.roll(tile, width - 2, 1)
                 tops.append(jnp.broadcast_to(tile[:, 0:1], (GROUP, width)))
                 dens.append(jnp.broadcast_to(tile[:, 3:4], (GROUP, width)))
             top = functools.reduce(jnp.maximum, tops)
             ws = [jnp.exp2((t - top) * exponent) for t in tops]
             den = sum(w * d for w, d in zip(ws, dens))
-            num = sum(w * o1l[net, pv, 0].astype(F32) for w, pv in zip(ws, vs))
+            num = sum(w * parts[pv, 0].astype(F32) for w, pv in zip(ws, vs))
             out[b] = num.astype(BF16)
             for k, value in enumerate(in_three(top) + in_three(den)):
                 stat = jnp.where(lane == 6 * b + k, value, stat)
@@ -756,8 +770,8 @@
             def owner(along, pc, net=net):
                 return chip(jnp.where(net == 0, along, x), jnp.where(net == 0, y, along), pc)
 
-            def send_o2(src, device, line=line):
-                remote(src, o2.at[line], o2_send, o2_recv, device).start()
+            def send_o2(src, device, net=net, line=line):
+                remote(src, o2.at[line], o2_send.at[net], o2_recv, device).start()
 
             @pl.when(net == 0)
             def _():
@@ -783,18 +797,22 @@
                 o2src[net, :, b] = total.T.reshape(toks, GROUP, width).astype(BF16)
             stat = jnp.concatenate(stats + [jnp.zeros((width - len(stats), piece), F32)]).T
             o2src[net, :, 2] = stat.reshape(toks, GROUP, width).astype(BF16)
-            for d in far_first + [0]:
-                along = (nu + d) % side
-
-                @pl.when((along != 0) | (across != 0))
+            for along in [0] + far_first[::-1]:
+
+                @pl.when(nu != along)
                 def _(along=along):
+                    send_o2(o2src.at[net, 2 * along + 1], owner(along, 1))
+
+                if along:
                     send_o2(o2src.at[net, 2 * along], owner(along, 0))
 
-                if d:
-                    send_o2(o2src.at[net, 2 * along + 1], owner(along, 1))
+            @pl.when(across != 0)
+            def _():
+                send_o2(o2src.at[net, 0], owner(0, 0))
+
             o2[line] = o2src[net, 2 * nu + 1]
 
-            @pl.when((across == 0) & (me != 1))
+            @pl.when((across == 0) & (me != 1) & jnp.logical_not(is_far(nu)))
             def _(net=net, nu=nu):
                 @pl.when(net == 0)
                 def _():
@@ -804,7 +822,7 @@
                 def _():
                     landed(o1l.at[1, pl.ds(0, side - 1)], o1l_recv.at[1])
 
-                merge_late(net, nu, o2l)
+                merge_late(o1l.at[net], nu, o2l)
                 send_o2(o2l, owner(0, 0))
 
         cache_gone()
@@ -841,9 +859,13 @@
         def _():
             landed(o1l.at[0, pl.ds(0, side - 1)], o1l_recv.at[0])
             landed(o1l.at[1], o1l_recv.at[1])
-            merge_late(0, 0, o2.at[0])
-            merge_late(1, 0, o2.at[side])
-            landed(o2.at[pl.ds(0, toks - 2)], o2_recv)
+            merge_late(o1l.at[0], 0, o2.at[0])
+            merge_late(o1l.at[1], 0, o2.at[side])
+            landed(o1d, o1d_recv)
+            for net in range(2):
+                for k, line in enumerate(far_lines):
+                    merge_late(o1d.at[net, k], line, o2.at[net * side + line])
+            landed(o2.at[pl.ds(0, toks - 2 - 2 * len(far_lines))], o2_recv)
 
     tops, dens = [[], []], [[], []]
     for src in range(toks):
@@ -863,13 +885,18 @@
                 head = CLASSES * net + e + 2 * b
                 out_ref[head * GROUP : (head + 1) * GROUP, :] = num / den
 
-    @pl.when(me == 1)
-    def _():
-        sent(o2src.at[:, pl.ds(0, toks - 2)], o2_send)
-
-    @pl.when((core == 1) & (me != 1))
-    def _():
-        sent(o2src.at[:, pl.ds(0, toks - 1)], o2_send)
+    @pl.when(core == 1)
+    def _():
+        for net, nu, across in ((0, x, y), (1, y, x)):
+            fewer = (across == 0) & ((me == 1) | is_far(nu))
+
+            @pl.when(fewer)
+            def _(net=net):
+                sent(o2src.at[net, pl.ds(0, toks - 2)], o2_send.at[net])
+
+            @pl.when(jnp.logical_not(fewer))
+            def _(net=net):
+                sent(o2src.at[net, pl.ds(0, toks - 1)], o2_send.at[net])
 
 
 def solution(mesh):
@@ -925,6 +952,7 @@
             vm((GROUP, width), BF16),
             vm((2, GROUP, width), BF16),
             vm((2, side, 2, GROUP, width), BF16),
+            vm((2, side - 5, side, 2, GROUP, width), BF16),
             vm((3, GROUP, width), BF16),
             dma((7,)),
             dma((2, 2)),
@@ -937,13 +965,14 @@
             dma((side,)),
             dma(()),
             dma((2,)),
-            dma(()),
+            dma((2,)),
             dma(()),
             dma((2,)),
             dma(()),
             dma(()),
             dma(()),
             dma((2,)),
+            dma(()),
             pltpu.SemaphoreType.REGULAR,
             pltpu.SemaphoreType.REGULAR,
             pltpu.SemaphoreType.REGULAR,

time: 40.1 us -> 39.9 us (level); the launches traced: 39.5 us -> 39.8 us
  no operation moved by 1% of the time
where the time goes in v9:
time: 39.9 us; the launch traced here: 39.8 us
  Pallas kernels  37.8 us (95%)
  between operations  1.31 us (3%)
  local copies, waits for them, and re-layouts  0.64 us (2%)
    pallas_call x1, Pallas kernels, body(): pl.pallas_call(functools.partial(kernel, side), out_shape=pltpu.VMEM((H,...  37.8 us

profile of v9, /device:TPU:513, one launch (start us, length us, event | category | flops | bytes accessed | tf_op | source)
XLA Modules:
  0.0 39.8 jit_solution(16534670290588473971)
XLA Ops:
  1.3 37.8 %paged_prefix.1 = f32[64,128]{1,0:T(8,128)S(1)} custom-call(s32[1]{0:T(128)S(6)} %copy.14.start_ref, s32[1]{0:T(128)S(6)} %copy.13.count_ref, s32[16]{0:T(128)} %pages_hbm.1, f32[40,128]{1,0:T(8,128)} %constant.2.clone.table_hbm, bf16[1,8192]{1,0:T(2,128)(2,1)} %q_hbm.1, bf16[1,1024]{1,0:T(2,128)(2,1)} %sk_hbm.1, bf16[1,1024]{1,0:T(2,128)(2,1)} %sv_hbm.1, ...), custom_call_target="tpu_custom_call" | custom-call | tf_op jit(solution)/shard_map/paged_prefix/pallas_call | solution.py:985
  39.1 0.6 %copy.12 = bf16[1,1,64,128]{3,1,2,0:T(2,128)(2,1)} copy(bf16[1,1,64,128]{3,2,1,0:T(8,128)(2,1)S(1)} %convert_bitcast_fusion) | data formatting | bytes 32768
  (1 shorter events, 0.0 us)

commit v10 on v9

--- a/solution.py
+++ b/solution.py
@@ -171,7 +171,7 @@
         remote(ref, ref, sem, sem, chip(x, y, other)).wait_recv()
 
     local = {
-        name: pltpu.make_async_copy(src, dst, local_sem.at[k])
+        name: pltpu.make_async_copy(src, dst, local_sem.at[k // 3])
         for k, (name, src, dst) in enumerate(
             (
                 ("pages", pages_hbm, pages_ref),
@@ -190,7 +190,7 @@
             pltpu.make_async_copy(
                 v_hbm.at[pl.ds(hf * half_rows, half_rows), pl.ds(h * width, width)],
                 vx.at[h, hf],
-                local_sem.at[len(local)],
+                local_sem.at[2],
             ).start()
 
     barrier = pltpu.get_barrier_semaphore()
@@ -263,7 +263,7 @@
             def send(head, half, slot, device):
                 src = buf.at[head] if half is None else buf.at[head, half]
                 dst = landing.at[pl.ds(slot, 2)] if half is None else landing.at[slot]
-                remote(src, dst, kv_send.at[which, net], kv_recv.at[which, net], device).start()
+                remote(src, dst, kv_send.at[which], kv_recv.at[which, net], device).start()
 
             nu, nv = (x, y) if net == 0 else (y, x)
 
@@ -298,7 +298,7 @@
             remote(
                 buf.at[head1],
                 own[0].at[pl.ds(0, 2)],
-                kv_send.at[which, 1],
+                kv_send.at[which],
                 kv_recv.at[which, 1],
                 chip(x, y, 1),
             ).start()
@@ -308,7 +308,7 @@
             own[0][2:4] = buf[head1]
             own[1][2:4] = buf[head0]
 
-    pltpu.make_async_copy(vx, vx, local_sem.at[len(local)]).wait()
+    pltpu.make_async_copy(vx, vx, local_sem.at[2]).wait()
 
     @pl.when(core == 0)
     def _():
@@ -426,7 +426,7 @@
             remote(
                 q1.at[net, (nu // 2 + pv) % 2],
                 q2.at[nv],
-                q2_send.at[net],
+                q2_send,
                 q2_recv.at[nv],
                 chip(x, pv, 0) if net == 0 else chip(pv, y, 1),
             ).start()
@@ -623,10 +623,9 @@
     def pair(k):
         late, away, half = (me <= 1) | by_chip0, jnp.where(v < side // 2, -1, 1), side // 2
         a, b = [(0, 1), (4, 3), (-3, 2), (-2, -1)][k]
-        return [
-            jnp.where(late, (side - k) % side, (v + away * a + side) % side),
-            jnp.where(late, k + 1, (v + away * b + side) % side),
-        ]
+        a, b = (v + away * a + side) % side, (v + away * b + side) % side
+        a, b = jnp.where(b == 0, b, a), jnp.where(b == 0, a, b)
+        return [jnp.where(late, (side - k) % side, a), jnp.where(late, k + 1, b)]
 
     def queries_in(pvs):
         for pv in pvs:
@@ -728,15 +727,13 @@
 
     def cache_gone():
         for which, buf in enumerate((kall, vall)):
-            sent(buf.at[pl.ds(0, near_units // 2)], kv_send.at[which, 0])
-
             @pl.when(core == 0)
             def _(which=which, buf=buf):
-                sent(buf.at[pl.ds(0, near_units // 2 + 2)], kv_send.at[which, 1])
+                sent(buf.at[pl.ds(0, near_units + 2)], kv_send.at[which])
 
             @pl.when(core == 1)
             def _(which=which, buf=buf):
-                sent(buf.at[pl.ds(0, near_units // 2)], kv_send.at[which, 1])
+                sent(buf.at[pl.ds(0, near_units)], kv_send.at[which])
                 for here, amount in (
                     (line0 * by_chip0 == 0, remote_units),
                     ((y == 0) & by_chip0, remote_units - 2),
@@ -844,8 +841,7 @@
         def _():
             sent(q1.at[:, :, pl.ds(0, toks - 2)], q1_send)
 
-        sent(q2, q2_send.at[0])
-        sent(q2.at[pl.ds(0, side - 1)], q2_send.at[1])
+        sent(vall.at[pl.ds(0, toks - 1)], q2_send)
         sent(o1.at[0, pl.ds(0, side - 1)], o1_send)
         landed(o2.at[pl.ds(0, toks - 2)], o2_recv)
 
@@ -954,14 +950,14 @@
             vm((2, side, 2, GROUP, width), BF16),
             vm((2, side - 5, side, 2, GROUP, width), BF16),
             vm((3, GROUP, width), BF16),
-            dma((7,)),
-            dma((2, 2)),
+            dma((3,)),
+            dma((2,)),
             dma((2, 2)),
             dma((2,)),
             dma(()),
             dma(()),
             dma((2,)),
-            dma((2,)),
+            dma(()),
             dma((side,)),
             dma(()),
             dma((2,)),

time: 39.9 us -> 39.8 us (level)
  no operation moved by 1% of the time
where the time goes in v10:
time: 39.8 us; the launch traced here: 39.7 us
  Pallas kernels  37.7 us (95%)
  between operations  1.31 us (3%)
  local copies, waits for them, and re-layouts  0.64 us (2%)
    pallas_call x1, Pallas kernels, body(): pl.pallas_call(functools.partial(kernel, side), out_shape=pltpu.VMEM((H,...  37.7 us

profile of v10, /device:TPU:513, one launch (start us, length us, event | category | flops | bytes accessed | tf_op | source)
XLA Modules:
  0.0 39.7 jit_solution(5119679637185184322)
XLA Ops:
  1.3 37.7 %paged_prefix.1 = f32[64,128]{1,0:T(8,128)S(1)} custom-call(s32[1]{0:T(128)S(6)} %copy.14.start_ref, s32[1]{0:T(128)S(6)} %copy.13.count_ref, s32[16]{0:T(128)} %pages_hbm.1, f32[40,128]{1,0:T(8,128)} %constant.2.clone.table_hbm, bf16[1,8192]{1,0:T(2,128)(2,1)} %q_hbm.1, bf16[1,1024]{1,0:T(2,128)(2,1)} %sk_hbm.1, bf16[1,1024]{1,0:T(2,128)(2,1)} %sv_hbm.1, ...), custom_call_target="tpu_custom_call" | custom-call | tf_op jit(solution)/shard_map/paged_prefix/pallas_call | solution.py:981
  39.1 0.6 %copy.12 = bf16[1,1,64,128]{3,1,2,0:T(2,128)(2,1)} copy(bf16[1,1,64,128]{3,2,1,0:T(8,128)(2,1)S(1)} %convert_bitcast_fusion) | data formatting | bytes 32768
  (1 shorter events, 0.0 us)

commit v11 on v10

--- a/solution.py
+++ b/solution.py
@@ -624,6 +624,11 @@
         late, away, half = (me <= 1) | by_chip0, jnp.where(v < side // 2, -1, 1), side // 2
         a, b = [(0, 1), (4, 3), (-3, 2), (-2, -1)][k]
         a, b = (v + away * a + side) % side, (v + away * b + side) % side
+        early, near = (u == side // 2), (v + away + side) % side
+        if k == 0:
+            b = jnp.where(early & (v != 0), 0, b)
+        else:
+            a, b = jnp.where(early & (a == 0), near, a), jnp.where(early & (b == 0), near, b)
         a, b = jnp.where(b == 0, b, a), jnp.where(b == 0, a, b)
         return [jnp.where(late, (side - k) % side, a), jnp.where(late, k + 1, b)]
 

time: 39.8 us -> 39.8 us (level)
  no operation moved by 1% of the time
where the time goes in v11:
time: 39.8 us; the launch traced here: 39.4 us
  Pallas kernels  37.4 us (94%)
  between operations  1.31 us (3%)
  local copies, waits for them, and re-layouts  0.64 us (2%)
    pallas_call x1, Pallas kernels, body(): pl.pallas_call(functools.partial(kernel, side), out_shape=pltpu.VMEM((H,...  37.4 us

profile of v11, /device:TPU:513, one launch (start us, length us, event | category | flops | bytes accessed | tf_op | source)
XLA Modules:
  0.0 39.4 jit_solution(524295951089417073)
XLA Ops:
  1.3 37.4 %paged_prefix.1 = f32[64,128]{1,0:T(8,128)S(1)} custom-call(s32[1]{0:T(128)S(6)} %copy.14.start_ref, s32[1]{0:T(128)S(6)} %copy.13.count_ref, s32[16]{0:T(128)} %pages_hbm.1, f32[40,128]{1,0:T(8,128)} %constant.2.clone.table_hbm, bf16[1,8192]{1,0:T(2,128)(2,1)} %q_hbm.1, bf16[1,1024]{1,0:T(2,128)(2,1)} %sk_hbm.1, bf16[1,1024]{1,0:T(2,128)(2,1)} %sv_hbm.1, ...), custom_call_target="tpu_custom_call" | custom-call | tf_op jit(solution)/shard_map/paged_prefix/pallas_call | solution.py:986
  38.7 0.6 %copy.12 = bf16[1,1,64,128]{3,1,2,0:T(2,128)(2,1)} copy(bf16[1,1,64,128]{3,2,1,0:T(8,128)(2,1)S(1)} %convert_bitcast_fusion) | data formatting | bytes 32768
  (1 shorter events, 0.0 us)

commit v12 on v11

--- a/solution.py
+++ b/solution.py
@@ -683,7 +683,7 @@
         wide = jnp.concatenate([stat, jnp.zeros((width - EXTRA, piece), F32)])
         late_src[1] = wide.T[0:GROUP].astype(BF16)
 
-    far_lines = range(3, side - 2)
+    far_lines = range(4, side - 3)
 
     def is_far(n):
         return (n >= far_lines[0]) & (n <= far_lines[-1])
@@ -953,7 +953,7 @@
             vm((GROUP, width), BF16),
             vm((2, GROUP, width), BF16),
             vm((2, side, 2, GROUP, width), BF16),
-            vm((2, side - 5, side, 2, GROUP, width), BF16),
+            vm((2, side - 7, side, 2, GROUP, width), BF16),
             vm((3, GROUP, width), BF16),
             dma((3,)),
             dma((2,)),

time: 39.8 us -> 39.6 us (level)
  no operation moved by 1% of the time
where the time goes in v12:
time: 39.6 us; the launch traced here: 39.4 us
  Pallas kernels  37.4 us (94%)
  between operations  1.31 us (3%)
  local copies, waits for them, and re-layouts  0.64 us (2%)
    pallas_call x1, Pallas kernels, body(): pl.pallas_call(functools.partial(kernel, side), out_shape=pltpu.VMEM((H,...  37.4 us

profile of v12, /device:TPU:513, one launch (start us, length us, event | category | flops | bytes accessed | tf_op | source)
XLA Modules:
  0.0 39.4 jit_solution(11878363334146038408)
XLA Ops:
  1.3 37.4 %paged_prefix.1 = f32[64,128]{1,0:T(8,128)S(1)} custom-call(s32[1]{0:T(128)S(6)} %copy.14.start_ref, s32[1]{0:T(128)S(6)} %copy.13.count_ref, s32[16]{0:T(128)} %pages_hbm.1, f32[40,128]{1,0:T(8,128)} %constant.2.clone.table_hbm, bf16[1,8192]{1,0:T(2,128)(2,1)} %q_hbm.1, bf16[1,1024]{1,0:T(2,128)(2,1)} %sk_hbm.1, bf16[1,1024]{1,0:T(2,128)(2,1)} %sv_hbm.1, ...), custom_call_target="tpu_custom_call" | custom-call | tf_op jit(solution)/shard_map/paged_prefix/pallas_call | solution.py:986
  38.7 0.6 %copy.12 = bf16[1,1,64,128]{3,1,2,0:T(2,128)(2,1)} copy(bf16[1,1,64,128]{3,2,1,0:T(8,128)(2,1)S(1)} %convert_bitcast_fusion) | data formatting | bytes 32768
  (1 shorter events, 0.0 us)

commit v13 on v12

--- a/solution.py
+++ b/solution.py
@@ -624,7 +624,7 @@
         late, away, half = (me <= 1) | by_chip0, jnp.where(v < side // 2, -1, 1), side // 2
         a, b = [(0, 1), (4, 3), (-3, 2), (-2, -1)][k]
         a, b = (v + away * a + side) % side, (v + away * b + side) % side
-        early, near = (u == side // 2), (v + away + side) % side
+        early, near = ((u >= 3) & (u <= side - 3)), (v + away + side) % side
         if k == 0:
             b = jnp.where(early & (v != 0), 0, b)
         else:

time: 39.6 us -> 39.6 us (level)
  no operation moved by 1% of the time
where the time goes in v13:
time: 39.6 us; the launch traced here: 39.1 us
  Pallas kernels  37.1 us (94%)
  between operations  1.31 us (3%)
  local copies, waits for them, and re-layouts  0.64 us (2%)
    pallas_call x1, Pallas kernels, body(): pl.pallas_call(functools.partial(kernel, side), out_shape=pltpu.VMEM((H,...  37.1 us

profile of v13, /device:TPU:513, one launch (start us, length us, event | category | flops | bytes accessed | tf_op | source)
XLA Modules:
  0.0 39.1 jit_solution(9358079509205503007)
XLA Ops:
  1.3 37.1 %paged_prefix.1 = f32[64,128]{1,0:T(8,128)S(1)} custom-call(s32[1]{0:T(128)S(6)} %copy.14.start_ref, s32[1]{0:T(128)S(6)} %copy.13.count_ref, s32[16]{0:T(128)} %pages_hbm.1, f32[40,128]{1,0:T(8,128)} %constant.2.clone.table_hbm, bf16[1,8192]{1,0:T(2,128)(2,1)} %q_hbm.1, bf16[1,1024]{1,0:T(2,128)(2,1)} %sk_hbm.1, bf16[1,1024]{1,0:T(2,128)(2,1)} %sv_hbm.1, ...), custom_call_target="tpu_custom_call" | custom-call | tf_op jit(solution)/shard_map/paged_prefix/pallas_call | solution.py:986
  38.4 0.6 %copy.12 = bf16[1,1,64,128]{3,1,2,0:T(2,128)(2,1)} copy(bf16[1,1,64,128]{3,2,1,0:T(8,128)(2,1)S(1)} %convert_bitcast_fusion) | data formatting | bytes 32768
  (1 shorter events, 0.0 us)
